TPU v7x, 128 devices: a whole 4x4x4 slice. The times are simulated.
128 devices in a mesh: dom: 128 (over z, y, x, core).
Axes of the slice: x: 4, y: 4, z: 4, core: 2. Of those that a mesh axis runs over, the one named last changes fastest.
Arguments:
- right_side: float32 [18, 131072], P(None, 'dom'), may hold values from -20 to 20
- element_matrix: bfloat16 [72, 72, 65536], P(None, None, 'dom'), may hold values from -8 to 8, as said below
- face_map: int32 [4, 65536], P(None, 'dom'), may hold values from 0 to 1535
- share_index: int32 [128, 4, 128], P('dom'), may hold values from 0 to 1023
- share_count: int32 [128, 4], P('dom'), may hold values from 0 to 128, as said below
- face_mass: float32 [131072], P('dom'), may hold values from 0.5 to 2
- absorbing: int32 [131072], P('dom'), may hold values 0 or 1
- impedance: float32 [131072], P('dom'), may hold values from 0.5 to 4
Outputs:
- solution: float32 [18, 131072], P(None, 'dom')
- residual: float32 [18, 131072], P(None, 'dom')
Inputs may be any that keep to these rules, and one draw needn't show every extreme that they name: `element_matrix`: each element's 72 x 72 matrix is symmetric positive definite. share_count[d, k] is 0 where device d + o_k lies outside the axis; it equals 128 for some device and offset in every draw.
All inputs are finite; a program needn't handle non-finite values. No bound on the sum of `absorbing` on one device may be relied on, other than what follows from the above.
Results may differ from a plain program's by a relative error of at most 0.0003.
Values sent between devices are 32-bit elements; how exact they have to be, the bound alone decides.
No kernel may reach another device: no remote copies, remote signals or barrier semaphores. Data moves between devices by JAX's collectives and lax.ppermute only.
A program may use at most 64 MiB of HBM per device.

v0:
```python
import functools

import jax
import jax.numpy as jnp
from jax import lax
from jax.sharding import Mesh
from jax.sharding import PartitionSpec as P

ITERS = 2
DOM = ("dom_0", "dom_1", "dom_2", "dom_3")


def passed_along(value, axis, steps):
    count = lax.axis_size(axis)
    first, last = (max(0, -steps), min(count, count - steps))
    return lax.ppermute(value, axis, [(source, source + steps) for source in range(first, last)])


def by_axis(value, axes):
    return functools.reduce(lax.psum, axes, value)


def offset_list(block_count):
    half_count = block_count // 2
    return [
        block_index - half_count if block_index < half_count else block_index - half_count + 1
        for block_index in range(block_count)
    ]


def shards(
    right_side, element_matrix, face_map, share_index, share_count, face_mass, absorbing, impedance
):
    trace_width = right_side.shape[0]
    own_faces = right_side.shape[1]
    side_count = face_map.shape[0]
    element_count = face_map.shape[1]
    block_count = share_index.shape[1]
    block_width = share_index.shape[2]
    dof_count = side_count * trace_width
    slot_total = own_faces + block_count * block_width
    offsets = offset_list(block_count)
    send_rows = share_index[0]
    slot_iota = lax.broadcasted_iota(jnp.int32, (block_count, block_width), 1)
    alive_mask = (slot_iota < share_count[0][:, None]).astype(jnp.float32)
    diagonal = face_mass + absorbing.astype(jnp.float32) * impedance
    flat_map = face_map.reshape(side_count * element_count)
    selector = (
        lax.broadcasted_iota(jnp.int32, (slot_total, side_count * element_count), 0)
        == flat_map[None, :]
    ).astype(jnp.float32)

    def fetch_ghosts(outgoing):
        received = []
        for block_index in range(block_count):
            received.append(passed_along(outgoing[block_index], DOM, offsets[block_index]))
        return jnp.stack(received)

    def return_sums(partial_value):
        received = []
        for block_index in range(block_count):
            received.append(passed_along(partial_value[block_index], DOM, -offsets[block_index]))
        return jnp.stack(received)

    def operate(field_now):
        outgoing = (
            jnp.take(field_now, send_rows, axis=1).transpose(1, 0, 2) * alive_mask[:, None, :]
        )
        ghosts = fetch_ghosts(outgoing)
        extended = jnp.concatenate(
            [field_now, ghosts.transpose(1, 0, 2).reshape(trace_width, block_count * block_width)],
            axis=1,
        )
        gathered = jnp.dot(
            extended, selector, precision=lax.Precision.HIGHEST, preferred_element_type=jnp.float32
        )
        picked = (
            gathered.reshape(trace_width, side_count, element_count)
            .transpose(1, 0, 2)
            .reshape(dof_count, element_count)
        )
        product = jnp.sum(element_matrix.astype(jnp.float32) * picked[None, :, :], axis=1)
        spread = (
            product.reshape(side_count, trace_width, element_count)
            .transpose(1, 0, 2)
            .reshape(trace_width, side_count * element_count)
        )
        summed = lax.dot_general(
            spread,
            selector,
            (((1,), (1,)), ((), ())),
            precision=lax.Precision.HIGHEST,
            preferred_element_type=jnp.float32,
        )
        partial_value = (
            summed[:, own_faces:].reshape(trace_width, block_count, block_width).transpose(1, 0, 2)
        )
        returned = return_sums(partial_value) * alive_mask[:, None, :]
        result = summed[:, :own_faces].at[:, send_rows].add(returned.transpose(1, 0, 2))
        return result + diagonal[None, :] * field_now

    def paired(values, image_vec):
        return (by_axis(jnp.sum(values * values), DOM), by_axis(jnp.sum(values * image_vec), DOM))

    solution = jnp.zeros_like(right_side)
    residual = right_side
    image_vec = operate(residual)
    norm_now, curvature = paired(residual, image_vec)
    step_size = norm_now / curvature
    direction = residual
    image_dir = image_vec
    for rounds in range(ITERS):
        solution = solution + step_size * direction
        residual = residual - step_size * image_dir
        if rounds + 1 < ITERS:
            image_vec = operate(residual)
            norm_next, curvature = paired(residual, image_vec)
            beta_ratio = norm_next / norm_now
            step_size = norm_next / (curvature - beta_ratio * norm_next / step_size)
            direction = residual + beta_ratio * direction
            image_dir = image_vec + beta_ratio * image_dir
            norm_now = norm_next
    return (solution, residual)


def solution(mesh):
    torus = Mesh(mesh.devices.reshape(4, 4, 4, 2), ("dom_0", "dom_1", "dom_2", "dom_3"))
    in_specs = (
        P(None, DOM),
        P(None, None, DOM),
        P(None, DOM),
        P(DOM, None, None),
        P(DOM, None),
        P(DOM),
        P(DOM),
        P(DOM),
    )
    out_specs = (P(None, DOM), P(None, DOM))
    return jax.shard_map(
        shards, mesh=torus, in_specs=in_specs, out_specs=out_specs, check_vma=False
    )
```

profile of v0, /device:TPU:1, one launch (start us, length us, event | category | flops | bytes accessed | tf_op | source)
XLA Modules:
  0.0 202.6 jit_solution(18133817289970364441)
XLA Ops:
  5.7 4.6 %collective-permute-start.3 = (f32[18,128]{1,0:T(8,128)S(1)}, f32[18,128]{1,0:T(8,128)S(1)}, u32[]{:S(2)}, u32[]{:S(2)}) collective-permute-start(f32[18,128]{1,0:T(8,128)S(1)} %get-tuple-element.34), channel_id=1, source_target_pairs={{0,2},{1,3},{2,4},{3,5},{4,6},{5,7},{6,8},{7,9},{8,10},{9,11},{10,... | collective-permute-start | bytes 27656 | tf_op jit(solution)/shard_map/ppermute | solution.py:16
  10.3 4.5 %collective-permute-start.2 = (f32[18,128]{1,0:T(8,128)S(1)}, f32[18,128]{1,0:T(8,128)S(1)}, u32[]{:S(2)}, u32[]{:S(2)}) collective-permute-start(f32[18,128]{1,0:T(8,128)S(1)} %get-tuple-element.35), channel_id=1, source_target_pairs={{0,1},{1,2},{2,3},{3,4},{4,5},{5,6},{6,7},{7,8},{8,9},{9,10},{10,1... | collective-permute-start | bytes 27656 | tf_op jit(solution)/shard_map/ppermute | solution.py:16
  19.8 4.9 %fusion.3 = f32[18,2048]{1,0:T(8,128)S(1)} fusion(s32[2048]{0:T(1024)S(1)} %bitcast.155, f32[18,512]{1,0:T(8,128)S(1)} %bitcast.133, f32[18,1024]{1,0:T(8,128)} %param.10), kind=kOutput, calls=%fused_computation.10 | convolution fusion | flops 682650624 | bytes 266240 | tf_op jit(solution)/shard_map/dot_general | solution.py:74
  25.0 4.1 %fusion.4 = f32[72,512]{1,0:T(8,128)S(1)} fusion(bf16[72,72,512]{2,1,0:T(8,128)(2,1)} %param.11, f32[72,512]{1,0:T(8,128)S(1)} %mul.120), kind=kLoop, calls=%fused_computation.11 | loop fusion | flops 7925760 | bytes 5603328 | tf_op jit(solution)/shard_map/reduce_sum | solution.py:82
  29.3 5.6 %fusion.2 = f32[18,1536]{1,0:T(8,128)S(1)} fusion(f32[18,2048]{1,0:T(8,128)S(1)} %bitcast.128, s32[2048]{0:T(1024)S(1)} %bitcast.156), kind=kOutput, calls=%fused_computation.9 | convolution fusion | flops 682622976 | bytes 266240 | tf_op jit(solution)/shard_map/dot_general | solution.py:88
  38.2 4.3 %collective-permute-start.5 = (f32[18,128]{1,0:T(8,128)S(1)}, f32[18,128]{1,0:T(8,128)S(1)}, u32[]{:S(2)}, u32[]{:S(2)}) collective-permute-start(f32[18,128]{1,0:T(8,128)S(1)} %bitcast.148), channel_id=1, source_target_pairs={{0,1},{1,2},{2,3},{3,4},{4,5},{5,6},{6,7},{7,8},{8,9},{9,10},{10,1... | collective-permute-start | bytes 27656 | tf_op jit(solution)/shard_map/ppermute | solution.py:16
  42.5 3.6 %collective-permute-start.4 = (f32[18,128]{1,0:T(8,128)S(1)}, f32[18,128]{1,0:T(8,128)S(1)}, u32[]{:S(2)}, u32[]{:S(2)}) collective-permute-start(f32[18,128]{1,0:T(8,128)S(1)} %bitcast.147), channel_id=1, source_target_pairs={{0,2},{1,3},{2,4},{3,5},{4,6},{5,7},{6,8},{7,9},{8,10},{9,11},{10,... | collective-permute-start | bytes 27656 | tf_op jit(solution)/shard_map/ppermute | solution.py:16
  47.2 3.7 %scatter_fusion = f32[18,1024]{0,1:T(8,128)S(1)} fusion(f32[18,1024]{0,1:T(8,128)S(1)} %copy.40, s32[512]{0:T(512)S(1)} %fusion.20, f32[512,18]{1,0:T(8,128)S(1)} %bitcast.124), kind=kCustom, calls=%fused_computation.2 | custom fusion | flops 9216 | bytes 112640 | tf_op jit(solution)/shard_map/scatter-add | solution.py:99
  51.8 26.5 %all-reduce.5 = (f32[]{:T(128)}, f32[]{:T(128)}) all-reduce(f32[]{:T(128)} %get-tuple-element.23, f32[]{:T(128)} %multiply_reduce_fusion), channel_id=1, replica_groups=mesh['dom_0'=4,'dom_1'=4,'dom_2'=4,'dom_3'=2] {'dom_0'}, use_global_device_ids=true, to_apply=%region_1.2 | all-reduce | flops 2 | bytes 16 | tf_op jit(solution)/shard_map/psum | solution.py:20
  78.3 6.6 %all-reduce.3 = (f32[]{:T(128)}, f32[]{:T(128)}) all-reduce(f32[]{:T(128)} %get-tuple-element.15, f32[]{:T(128)} %get-tuple-element.16), channel_id=1, replica_groups=mesh['dom_0'=4,'dom_1'=4,'dom_2'=4,'dom_3'=2] {'dom_1'}, use_global_device_ids=true, to_apply=%region_2.3 | all-reduce | flops 2 | bytes 16 | tf_op jit(solution)/shard_map/psum | solution.py:20
  84.9 6.6 %all-reduce.1 = (f32[]{:T(128)}, f32[]{:T(128)}) all-reduce(f32[]{:T(128)} %get-tuple-element.11, f32[]{:T(128)} %get-tuple-element.12), channel_id=1, replica_groups=mesh['dom_0'=4,'dom_1'=4,'dom_2'=4,'dom_3'=2] {'dom_2'}, use_global_device_ids=true, to_apply=%region_3.4 | all-reduce | flops 2 | bytes 16 | tf_op jit(solution)/shard_map/psum | solution.py:20
  91.6 7.9 %all-reduce.7 = (f32[]{:T(128)}, f32[]{:T(128)}) all-reduce(f32[]{:T(128)} %get-tuple-element.7, f32[]{:T(128)} %get-tuple-element.8), channel_id=1, replica_groups=mesh['dom_0'=4,'dom_1'=4,'dom_2'=4,'dom_3'=2] {'dom_3'}, use_global_device_ids=true, to_apply=%region_4.5 | all-reduce | flops 2 | bytes 16 | tf_op jit(solution)/shard_map/psum | solution.py:20
  103.5 4.5 %collective-permute-start.10 = (f32[18,128]{1,0:T(8,128)S(1)}, f32[18,128]{1,0:T(8,128)S(1)}, u32[]{:S(2)}, u32[]{:S(2)}) collective-permute-start(f32[18,128]{1,0:T(8,128)S(1)} %get-tuple-element.31), channel_id=1, source_target_pairs={{0,1},{1,2},{2,3},{3,4},{4,5},{5,6},{6,7},{7,8},{8,9},{9,10},{10,1... | collective-permute-start | bytes 27656 | tf_op jit(solution)/shard_map/ppermute | solution.py:16
  109.9 3.6 %collective-permute-start.11 = (f32[18,128]{1,0:T(8,128)S(1)}, f32[18,128]{1,0:T(8,128)S(1)}, u32[]{:S(2)}, u32[]{:S(2)}) collective-permute-start(f32[18,128]{1,0:T(8,128)S(1)} %get-tuple-element.30), channel_id=1, source_target_pairs={{0,2},{1,3},{2,4},{3,5},{4,6},{5,7},{6,8},{7,9},{8,10},{9,11},{10,... | collective-permute-start | bytes 27656 | tf_op jit(solution)/shard_map/ppermute | solution.py:16
  114.5 4.0 %fusion.1 = f32[18,2048]{1,0:T(8,128)S(1)} fusion(s32[2048]{0:T(1024)S(1)} %bitcast.157, f32[18,512]{1,0:T(8,128)S(1)} %bitcast.134, f32[18,1024]{1,0:T(8,128)S(1)} %multiply_subtract_fusion.1), kind=kOutput, calls=%fused_computation.8 | convolution fusion | flops 682650624 | bytes 266240 | tf_op jit(solution)/shard_map/dot_general | solution.py:74
  118.7 4.0 %fusion.5 = f32[72,512]{1,0:T(8,128)S(1)} fusion(bf16[72,72,512]{2,1,0:T(8,128)(2,1)} %param.11, f32[72,512]{1,0:T(8,128)S(1)} %mul.135), kind=kLoop, calls=%fused_computation.12 | loop fusion | flops 7925760 | bytes 5603328 | tf_op jit(solution)/shard_map/reduce_sum | solution.py:82
  123.0 5.6 %fusion = f32[18,1536]{1,0:T(8,128)S(1)} fusion(f32[18,2048]{1,0:T(8,128)S(1)} %bitcast.127, s32[2048]{0:T(1024)S(1)} %bitcast.158), kind=kOutput, calls=%fused_computation.7 | convolution fusion | flops 682622976 | bytes 266240 | tf_op jit(solution)/shard_map/dot_general | solution.py:88
  128.7 3.6 %collective-permute-start.12 = (f32[18,128]{1,0:T(8,128)S(1)}, f32[18,128]{1,0:T(8,128)S(1)}, u32[]{:S(2)}, u32[]{:S(2)}) collective-permute-start(f32[18,128]{1,0:T(8,128)S(1)} %get-tuple-element.25), channel_id=1, source_target_pairs={{0,2},{1,3},{2,4},{3,5},{4,6},{5,7},{6,8},{7,9},{8,10},{9,11},{10,... | collective-permute-start | bytes 27656 | tf_op jit(solution)/shard_map/ppermute | solution.py:16
  137.1 4.2 %collective-permute-start.13 = (f32[18,128]{1,0:T(8,128)S(1)}, f32[18,128]{1,0:T(8,128)S(1)}, u32[]{:S(2)}, u32[]{:S(2)}) collective-permute-start(f32[18,128]{1,0:T(8,128)S(1)} %get-tuple-element.28), channel_id=1, source_target_pairs={{0,1},{1,2},{2,3},{3,4},{4,5},{5,6},{6,7},{7,8},{8,9},{9,10},{10,1... | collective-permute-start | bytes 27656 | tf_op jit(solution)/shard_map/ppermute | solution.py:16
  142.2 3.7 %scatter_fusion.1 = f32[18,1024]{0,1:T(8,128)S(1)} fusion(f32[18,1024]{0,1:T(8,128)S(1)} %copy.52, s32[512]{0:T(512)S(1)} %fusion.20, f32[512,18]{1,0:T(8,128)S(1)} %bitcast.123), kind=kCustom, calls=%fused_computation.3 | custom fusion | flops 9216 | bytes 112640 | tf_op jit(solution)/shard_map/scatter-add | solution.py:99
  146.9 22.7 %all-reduce.4 = (f32[]{:T(128)}, f32[]{:T(128)}) all-reduce(f32[]{:T(128)} %get-tuple-element.4, f32[]{:T(128)} %get-tuple-element.3), channel_id=1, replica_groups=mesh['dom_0'=4,'dom_1'=4,'dom_2'=4,'dom_3'=2] {'dom_0'}, use_global_device_ids=true, to_apply=%region_13.15 | all-reduce | flops 2 | bytes 16 | tf_op jit(solution)/shard_map/psum | solution.py:20
  169.5 6.7 %all-reduce.2 = (f32[]{:T(128)}, f32[]{:T(128)}) all-reduce(f32[]{:T(128)} %get-tuple-element.13, f32[]{:T(128)} %get-tuple-element.14), channel_id=1, replica_groups=mesh['dom_0'=4,'dom_1'=4,'dom_2'=4,'dom_3'=2] {'dom_1'}, use_global_device_ids=true, to_apply=%region_14.16 | all-reduce | flops 2 | bytes 16 | tf_op jit(solution)/shard_map/psum | solution.py:20
  176.2 11.0 %all-reduce = (f32[]{:T(128)}, f32[]{:T(128)}) all-reduce(f32[]{:T(128)} %get-tuple-element.9, f32[]{:T(128)} %get-tuple-element.10), channel_id=1, replica_groups=mesh['dom_0'=4,'dom_1'=4,'dom_2'=4,'dom_3'=2] {'dom_2'}, use_global_device_ids=true, to_apply=%region_15.17 | all-reduce | flops 2 | bytes 16 | tf_op jit(solution)/shard_map/psum | solution.py:20
  187.2 10.2 %all-reduce.6 = (f32[]{:T(128)}, f32[]{:T(128)}) all-reduce(f32[]{:T(128)} %get-tuple-element.5, f32[]{:T(128)} %get-tuple-element.6), channel_id=1, replica_groups=mesh['dom_0'=4,'dom_1'=4,'dom_2'=4,'dom_3'=2] {'dom_3'}, use_global_device_ids=true, to_apply=%region_16.18 | all-reduce | flops 2 | bytes 16 | tf_op jit(solution)/shard_map/psum | solution.py:20
  (92 shorter events, 28.8 us)
Async XLA Ops:
  4.4 14.4 %collective-permute-start = (f32[18,128]{1,0:T(8,128)S(1)}, f32[18,128]{1,0:T(8,128)S(1)}, u32[]{:S(2)}, u32[]{:S(2)}) collective-permute-start(f32[18,128]{1,0:T(8,128)S(1)} %get-tuple-element.33), channel_id=1, source_target_pairs={{2,0},{3,1},{4,2},{5,3},{6,4},{7,5},{8,6},{9,7},{10,8},{11,9},{12,... | collective-permute-start | bytes 27656 | tf_op jit(solution)/shard_map/ppermute | solution.py:16
  5.7 13.1 %collective-permute-start.3 = (f32[18,128]{1,0:T(8,128)S(1)}, f32[18,128]{1,0:T(8,128)S(1)}, u32[]{:S(2)}, u32[]{:S(2)}) collective-permute-start(f32[18,128]{1,0:T(8,128)S(1)} %get-tuple-element.34), channel_id=1, source_target_pairs={{0,2},{1,3},{2,4},{3,5},{4,6},{5,7},{6,8},{7,9},{8,10},{9,11},{10,... | collective-permute-start | bytes 27656 | tf_op jit(solution)/shard_map/ppermute | solution.py:16
  10.3 8.5 %collective-permute-start.2 = (f32[18,128]{1,0:T(8,128)S(1)}, f32[18,128]{1,0:T(8,128)S(1)}, u32[]{:S(2)}, u32[]{:S(2)}) collective-permute-start(f32[18,128]{1,0:T(8,128)S(1)} %get-tuple-element.35), channel_id=1, source_target_pairs={{0,1},{1,2},{2,3},{3,4},{4,5},{5,6},{6,7},{7,8},{8,9},{9,10},{10,1... | collective-permute-start | bytes 27656 | tf_op jit(solution)/shard_map/ppermute | solution.py:16
  14.8 5.0 %collective-permute-start.1 = (f32[18,128]{1,0:T(8,128)S(1)}, f32[18,128]{1,0:T(8,128)S(1)}, u32[]{:S(2)}, u32[]{:S(2)}) collective-permute-start(f32[18,128]{1,0:T(8,128)S(1)} %get-tuple-element.36), channel_id=1, source_target_pairs={{1,0},{2,1},{3,2},{4,3},{5,4},{6,5},{7,6},{8,7},{9,8},{10,9},{11,1... | collective-permute-start | bytes 27656 | tf_op jit(solution)/shard_map/ppermute | solution.py:16
  25.0 21.2 %copy-start = (f32[18,1024]{1,0:T(8,128)S(1)}, f32[18,1024]{1,0:T(8,128)}, u32[]{:S(2)}) copy-start(f32[18,1024]{1,0:T(8,128)} %param.10) | copy-start | bytes 221188
  35.0 12.0 %collective-permute-start.6 = (f32[18,128]{1,0:T(8,128)S(1)}, f32[18,128]{1,0:T(8,128)S(1)}, u32[]{:S(2)}, u32[]{:S(2)}) collective-permute-start(f32[18,128]{1,0:T(8,128)S(1)} %bitcast.150), channel_id=1, source_target_pairs={{1,0},{2,1},{3,2},{4,3},{5,4},{6,5},{7,6},{8,7},{9,8},{10,9},{11,1... | collective-permute-start | bytes 27656 | tf_op jit(solution)/shard_map/ppermute | solution.py:16
  36.9 10.1 %collective-permute-start.7 = (f32[18,128]{1,0:T(8,128)S(1)}, f32[18,128]{1,0:T(8,128)S(1)}, u32[]{:S(2)}, u32[]{:S(2)}) collective-permute-start(f32[18,128]{1,0:T(8,128)S(1)} %bitcast.149), channel_id=1, source_target_pairs={{2,0},{3,1},{4,2},{5,3},{6,4},{7,5},{8,6},{9,7},{10,8},{11,9},{12,... | collective-permute-start | bytes 27656 | tf_op jit(solution)/shard_map/ppermute | solution.py:16
  38.2 8.8 %collective-permute-start.5 = (f32[18,128]{1,0:T(8,128)S(1)}, f32[18,128]{1,0:T(8,128)S(1)}, u32[]{:S(2)}, u32[]{:S(2)}) collective-permute-start(f32[18,128]{1,0:T(8,128)S(1)} %bitcast.148), channel_id=1, source_target_pairs={{0,1},{1,2},{2,3},{3,4},{4,5},{5,6},{6,7},{7,8},{8,9},{9,10},{10,1... | collective-permute-start | bytes 27656 | tf_op jit(solution)/shard_map/ppermute | solution.py:16
  42.5 4.5 %collective-permute-start.4 = (f32[18,128]{1,0:T(8,128)S(1)}, f32[18,128]{1,0:T(8,128)S(1)}, u32[]{:S(2)}, u32[]{:S(2)}) collective-permute-start(f32[18,128]{1,0:T(8,128)S(1)} %bitcast.147), channel_id=1, source_target_pairs={{0,2},{1,3},{2,4},{3,5},{4,6},{5,7},{6,8},{7,9},{8,10},{9,11},{10,... | collective-permute-start | bytes 27656 | tf_op jit(solution)/shard_map/ppermute | solution.py:16
  102.2 11.4 %collective-permute-start.8 = (f32[18,128]{1,0:T(8,128)S(1)}, f32[18,128]{1,0:T(8,128)S(1)}, u32[]{:S(2)}, u32[]{:S(2)}) collective-permute-start(f32[18,128]{1,0:T(8,128)S(1)} %get-tuple-element.29), channel_id=1, source_target_pairs={{2,0},{3,1},{4,2},{5,3},{6,4},{7,5},{8,6},{9,7},{10,8},{11,9},{12,... | collective-permute-start | bytes 27656 | tf_op jit(solution)/shard_map/ppermute | solution.py:16
  103.5 10.1 %collective-permute-start.10 = (f32[18,128]{1,0:T(8,128)S(1)}, f32[18,128]{1,0:T(8,128)S(1)}, u32[]{:S(2)}, u32[]{:S(2)}) collective-permute-start(f32[18,128]{1,0:T(8,128)S(1)} %get-tuple-element.31), channel_id=1, source_target_pairs={{0,1},{1,2},{2,3},{3,4},{4,5},{5,6},{6,7},{7,8},{8,9},{9,10},{10,1... | collective-permute-start | bytes 27656 | tf_op jit(solution)/shard_map/ppermute | solution.py:16
  108.0 5.6 %collective-permute-start.9 = (f32[18,128]{1,0:T(8,128)S(1)}, f32[18,128]{1,0:T(8,128)S(1)}, u32[]{:S(2)}, u32[]{:S(2)}) collective-permute-start(f32[18,128]{1,0:T(8,128)S(1)} %get-tuple-element.32), channel_id=1, source_target_pairs={{1,0},{2,1},{3,2},{4,3},{5,4},{6,5},{7,6},{8,7},{9,8},{10,9},{11,1... | collective-permute-start | bytes 27656 | tf_op jit(solution)/shard_map/ppermute | solution.py:16
  109.9 4.5 %collective-permute-start.11 = (f32[18,128]{1,0:T(8,128)S(1)}, f32[18,128]{1,0:T(8,128)S(1)}, u32[]{:S(2)}, u32[]{:S(2)}) collective-permute-start(f32[18,128]{1,0:T(8,128)S(1)} %get-tuple-element.30), channel_id=1, source_target_pairs={{0,2},{1,3},{2,4},{3,5},{4,6},{5,7},{6,8},{7,9},{8,10},{9,11},{10,... | collective-permute-start | bytes 27656 | tf_op jit(solution)/shard_map/ppermute | solution.py:16
  128.7 12.8 %collective-permute-start.12 = (f32[18,128]{1,0:T(8,128)S(1)}, f32[18,128]{1,0:T(8,128)S(1)}, u32[]{:S(2)}, u32[]{:S(2)}) collective-permute-start(f32[18,128]{1,0:T(8,128)S(1)} %get-tuple-element.25), channel_id=1, source_target_pairs={{0,2},{1,3},{2,4},{3,5},{4,6},{5,7},{6,8},{7,9},{8,10},{9,11},{10,... | collective-permute-start | bytes 27656 | tf_op jit(solution)/shard_map/ppermute | solution.py:16
  132.3 9.2 %collective-permute-start.15 = (f32[18,128]{1,0:T(8,128)S(1)}, f32[18,128]{1,0:T(8,128)S(1)}, u32[]{:S(2)}, u32[]{:S(2)}) collective-permute-start(f32[18,128]{1,0:T(8,128)S(1)} %get-tuple-element.26), channel_id=1, source_target_pairs={{2,0},{3,1},{4,2},{5,3},{6,4},{7,5},{8,6},{9,7},{10,8},{11,9},{12,... | collective-permute-start | bytes 27656 | tf_op jit(solution)/shard_map/ppermute | solution.py:16
  133.6 7.9 %collective-permute-start.14 = (f32[18,128]{1,0:T(8,128)S(1)}, f32[18,128]{1,0:T(8,128)S(1)}, u32[]{:S(2)}, u32[]{:S(2)}) collective-permute-start(f32[18,128]{1,0:T(8,128)S(1)} %get-tuple-element.27), channel_id=1, source_target_pairs={{1,0},{2,1},{3,2},{4,3},{5,4},{6,5},{7,6},{8,7},{9,8},{10,9},{11,1... | collective-permute-start | bytes 27656 | tf_op jit(solution)/shard_map/ppermute | solution.py:16
  137.1 5.0 %collective-permute-start.13 = (f32[18,128]{1,0:T(8,128)S(1)}, f32[18,128]{1,0:T(8,128)S(1)}, u32[]{:S(2)}, u32[]{:S(2)}) collective-permute-start(f32[18,128]{1,0:T(8,128)S(1)} %get-tuple-element.28), channel_id=1, source_target_pairs={{0,1},{1,2},{2,3},{3,4},{4,5},{5,6},{6,7},{7,8},{8,9},{9,10},{10,1... | collective-permute-start | bytes 27656 | tf_op jit(solution)/shard_map/ppermute | solution.py:16
where the time goes:
time: 204 us; the launch traced here: 203 us
  blocking collectives  98.1 us (48%)
  starting transfers between devices  47.3 us (23%)
  other arithmetic  21.3 us (10%)
  matrix products  20.2 us (10%)
  between operations  7.17 us (4%)
  local copies, waits for them, and re-layouts  6.39 us (3%)
  waiting for transfers between devices  2.25 us (1%)
    psum x8, blocking collectives, by_axis(): return functools.reduce(lax.psum, axes, value)  98.1 us
    ppermute x16, starting transfers between devices, passed_along(): lax.ppermute(value, axis, [(source, source + steps) for source in range(f...  47.3 us
    dot_general x2, matrix products, operate(): lax.dot_general(spread, selector, (((1,), (1,)), ((), ())), precision=lax...  11.2 us
    dot_general x2, matrix products, operate(): jnp.dot(extended, selector, precision=lax.Precision.HIGHEST, preferred_el...  8.99 us
    reduce_sum x2, other arithmetic, operate(): jnp.sum(element_matrix.astype(jnp.float32) * picked[None, :, :], axis=1)  8.08 us
    scatter-add x2, other arithmetic, operate(): summed[:, :own_faces].at[:, send_rows].add(returned.transpose(1, 0, 2))  7.41 us
  transfers between devices with their start and end apart: 16, of which 3 were waited for; matrix products, arithmetic and copies ran while one was open for 2% of the time, Pallas kernels for 0%

commit v1 on v0

v1 whole, which is shorter than its diff:
```python
import functools

import jax
import jax.numpy as jnp
from jax import lax
from jax.experimental import pallas as pl
from jax.experimental.pallas import tpu as pltpu
from jax.sharding import Mesh
from jax.sharding import PartitionSpec as P

DOM = "dom"
TR = 18
TP = 24
SIDES = 4
E = 512
F = 1024
GH = 128
NB = 4
SLOTS = F + NB * GH
PICKS = SIDES * E
DOFS = SIDES * TR
F32 = jnp.float32
BF16 = jnp.bfloat16
VMEM = pltpu.VMEM
SMEM = pltpu.SMEM
PARAMS = pltpu.CompilerParams(vmem_limit_bytes=60 * 1024 * 1024)


def vspec():
    return pl.BlockSpec(memory_space=VMEM)


def sspec():
    return pl.BlockSpec(memory_space=SMEM)


def pieces(x):
    hi = x.astype(BF16).astype(F32)
    rest = x - hi
    mid = rest.astype(BF16).astype(F32)
    return jnp.concatenate([hi, mid, rest - mid], axis=0).astype(BF16)


def joined(y):
    rows = y.shape[0] // 3
    return y[:rows] + y[rows : 2 * rows] + y[2 * rows :]


def pick(x, selector):
    return joined(jnp.dot(pieces(x), selector, preferred_element_type=F32))


def spread_out(x, selector):
    return joined(
        lax.dot_general(pieces(x), selector, (((1,), (1,)), ((), ())), preferred_element_type=F32)
    )


def share_selector(index_ref, count_ref):
    cols = []
    for k in range(NB):
        rows = lax.broadcasted_iota(jnp.int32, (F, GH), 0)
        lanes = lax.broadcasted_iota(jnp.int32, (1, GH), 1)
        face = jnp.where(lanes < count_ref[0, k], index_ref[k : k + 1, :], -1)
        cols.append(jnp.where(rows == face, 1.0, 0.0).astype(BF16))
    return jnp.concatenate(cols, axis=1)


def write_blocks(blocks, core, up_ref, down_ref, mid_ref):
    up_ref[0] = blocks[3][:TR]
    up_ref[1] = blocks[2][:TR]
    down_ref[0] = blocks[0][:TR]
    down_ref[1] = blocks[1][:TR]
    mid_ref[...] = jnp.where(core == 1, blocks[1][:TR], blocks[2][:TR])


def read_blocks(core, up_ref, down_ref, mid_ref):
    first, second = mid_ref[0], mid_ref[1]
    return [
        down_ref[0],
        jnp.where(core == 1, second, first),
        jnp.where(core == 1, first, second),
        up_ref[0],
    ]


def lanes_of(values):
    lane = lax.broadcasted_iota(jnp.int32, (1, GH), 1)
    row = jnp.zeros((1, GH), F32)
    for at, value in enumerate(values):
        row = row + jnp.where(lane == at, value, 0.0)
    return row


def total(x):
    return jnp.sum(jnp.sum(x, axis=0, keepdims=True), axis=1, keepdims=True)


def send_kernel(core_ref, count_ref, field_ref, index_ref, up_ref, down_ref, mid_ref, pad_ref):
    pad_ref[...] = jnp.zeros_like(pad_ref)
    pad_ref[:TR, :] = field_ref[...]
    out = pick(pad_ref[...], share_selector(index_ref, count_ref))
    blocks = [out[:, k * GH : (k + 1) * GH] for k in range(NB)]
    write_blocks(blocks, core_ref[0], up_ref, down_ref, mid_ref)


def selector_kernel(map_ref, sel_ref):
    for s in range(SIDES):
        rows = lax.broadcasted_iota(jnp.int32, (SLOTS, E), 0)
        sel_ref[:, s * E : (s + 1) * E] = jnp.where(rows == map_ref[s : s + 1, :], 1.0, 0.0).astype(BF16)


def apply_kernel(
    core_ref,
    field_ref,
    up_ref,
    down_ref,
    mid_ref,
    sel_ref,
    matrix_ref,
    own_ref,
    up_out,
    down_out,
    mid_out,
    energy_ref,
    ext_ref,
    pick_ref,
    prod_ref,
    spread_ref,
):
    core = core_ref[0]
    ext_ref[TR:, :] = jnp.zeros((TP - TR, SLOTS), F32)
    ext_ref[:TR, :F] = field_ref[...]
    for k, block in enumerate(read_blocks(core, up_ref, down_ref, mid_ref)):
        ext_ref[:TR, F + k * GH : F + (k + 1) * GH] = block
    pick_ref[...] = pick(ext_ref[...], sel_ref[...])
    for t in range(E // 128):
        acc = jnp.zeros((DOFS, 128), F32)
        for j in range(DOFS):
            s, c = divmod(j, TR)
            row = pick_ref[c : c + 1, s * E + t * 128 : s * E + (t + 1) * 128]
            acc = acc + matrix_ref[j, :, t * 128 : (t + 1) * 128].astype(F32) * row
        prod_ref[:, t * 128 : (t + 1) * 128] = acc
    spread_ref[TR:, :] = jnp.zeros((TP - TR, PICKS), F32)
    for s in range(SIDES):
        spread_ref[:TR, s * E : (s + 1) * E] = prod_ref[s * TR : (s + 1) * TR, :]
    spread = spread_ref[...]
    energy_ref[...] = lanes_of([total(spread * pick_ref[...])])
    summed = spread_out(spread, sel_ref[...])
    own_ref[...] = summed[:TR, :F]
    parts = [summed[:, F + k * GH : F + (k + 1) * GH] for k in range(NB)]
    write_blocks(parts[::-1], core, up_out, down_out, mid_out)


def finished(core, own_ref, up_ref, down_ref, mid_ref, selector, diagonal, field, back_ref):
    back_ref[...] = jnp.zeros_like(back_ref)
    for k, block in enumerate(read_blocks(core, up_ref, down_ref, mid_ref)[::-1]):
        back_ref[:TR, k * GH : (k + 1) * GH] = block
    return own_ref[...] + spread_out(back_ref[...], selector)[:TR] + diagonal * field


def diagonal_of(mass_ref, absorbing_ref, impedance_ref):
    return mass_ref[...] + absorbing_ref[...].astype(F32) * impedance_ref[...]


def combine_kernel(
    core_ref,
    count_ref,
    field_ref,
    own_ref,
    up_ref,
    down_ref,
    mid_ref,
    index_ref,
    mass_ref,
    absorbing_ref,
    impedance_ref,
    energy_ref,
    image_ref,
    up_out,
    down_out,
    mid_out,
    sums_ref,
    back_ref,
    pad_ref,
):
    core = core_ref[0]
    selector = share_selector(index_ref, count_ref)
    diagonal = diagonal_of(mass_ref, absorbing_ref, impedance_ref)
    field = field_ref[...]
    image = finished(core, own_ref, up_ref, down_ref, mid_ref, selector, diagonal, field, back_ref)
    image_ref[...] = image
    pad_ref[...] = jnp.zeros_like(pad_ref)
    pad_ref[:TR, :] = image
    out = pick(pad_ref[...], selector)
    blocks = [out[:, k * GH : (k + 1) * GH] for k in range(NB)]
    write_blocks(blocks, core, up_out, down_out, mid_out)
    sums_ref[...] = lanes_of(
        [
            total(field * field),
            total(diagonal * field * field) + energy_ref[:, :1],
            total(image * image),
            total(diagonal * image * image),
        ]
    )


def sums_kernel(sums_ref, energy_ref, out_ref):
    lane = lax.broadcasted_iota(jnp.int32, (1, GH), 1)
    row = sums_ref[...] + jnp.where(lane == 3, energy_ref[:, :1], 0.0)
    out_ref[...] = jnp.broadcast_to(row[None], out_ref.shape)


def final_kernel(
    core_ref,
    count_ref,
    field_ref,
    image_ref,
    own_ref,
    up_ref,
    down_ref,
    mid_ref,
    index_ref,
    mass_ref,
    absorbing_ref,
    impedance_ref,
    sums_ref,
    solution_ref,
    residual_ref,
    back_ref,
):
    selector = share_selector(index_ref, count_ref)
    diagonal = diagonal_of(mass_ref, absorbing_ref, impedance_ref)
    field = field_ref[...]
    image = image_ref[...]
    second = finished(
        core_ref[0], own_ref, up_ref, down_ref, mid_ref, selector, diagonal, image, back_ref
    )
    row = jnp.sum(sums_ref[...], axis=0)
    s0, s1, s2, s3 = (row[:, k : k + 1] for k in range(4))
    step0 = s0 / s1
    ratio = (step0 * step0 * s2 - s0) / s0
    grow = 1.0 + ratio
    curvature = grow * grow * s1 - 2.0 * step0 * grow * s2 + step0 * step0 * s3
    step1 = ratio * s0 / curvature
    along = step0 + step1 * grow
    solution_ref[...] = along * field - (step0 * step1) * image
    residual_ref[...] = field - along * image + (step0 * step1) * second


def shape(*dims, dtype=F32):
    return jax.ShapeDtypeStruct(dims, dtype)


BLOCKS = (shape(2, TR, GH), shape(2, TR, GH), shape(TR, GH))
PAD = VMEM((TP, F), F32)
BACK = VMEM((TP, NB * GH), F32)


def call(kernel, name, in_specs, out_shape, scratch=()):
    return pl.pallas_call(
        kernel,
        name=name,
        in_specs=in_specs,
        out_specs=jax.tree.map(lambda _: vspec(), out_shape),
        out_shape=out_shape,
        scratch_shapes=scratch,
        compiler_params=PARAMS,
    )


def shards(
    right_side, element_matrix, face_map, share_index, share_count, face_mass, absorbing, impedance
):
    count = lax.axis_size(DOM)
    core = lax.rem(lax.axis_index(DOM), 2).astype(jnp.int32)
    core_of = core.reshape(1)
    index = share_index[0]
    mass, absorb, imped = (x.reshape(1, F) for x in (face_mass, absorbing, impedance))

    def shift(value, steps):
        return lax.ppermute(value, DOM, [(i, (i + steps) % count) for i in range(count)])

    def exchange(up, down, mid):
        got_up = shift(up, 2)
        got_down = shift(down, -2)
        onward = jnp.where(core == 1, got_up[1], got_down[1])
        got_mid = lax.ppermute(jnp.stack([mid, onward]), DOM, [(i, i ^ 1) for i in range(count)])
        return got_up, got_down, got_mid

    sent = call(send_kernel, "send", [sspec(), sspec(), vspec(), vspec()], BLOCKS, [PAD])(
        core_of, share_count, right_side, index
    )
    got = exchange(*sent)
    selector = call(selector_kernel, "selector", [vspec()], shape(SLOTS, PICKS, dtype=BF16))(face_map)

    def apply_of(name, field, got):
        return call(
            apply_kernel,
            name,
            [sspec()] + [vspec()] * 6,
            (shape(TR, F),) + BLOCKS + (shape(1, GH),),
            [
                VMEM((TP, SLOTS), F32),
                VMEM((TP, PICKS), F32),
                VMEM((DOFS, E), F32),
                VMEM((TP, PICKS), F32),
            ],
        )(core_of, field, *got, selector, element_matrix)

    own, up, down, mid, energy = apply_of("apply0", right_side, got)
    back = exchange(up, down, mid)
    image, up, down, mid, sums = call(
        combine_kernel,
        "combine",
        [sspec(), sspec()] + [vspec()] * 10,
        (shape(TR, F),) + BLOCKS + (shape(1, GH),),
        [BACK, PAD],
    )(core_of, share_count, right_side, own, *back, index, mass, absorb, imped, energy)
    got = exchange(up, down, mid)
    own, up, down, mid, energy = apply_of("apply1", image, got)
    row = call(sums_kernel, "sums", [vspec(), vspec()], shape(count, 1, GH))(sums, energy)
    row = lax.all_to_all(row, DOM, 0, 0)
    back = exchange(up, down, mid)
    return call(
        final_kernel,
        "final",
        [sspec(), sspec()] + [vspec()] * 11,
        (shape(TR, F), shape(TR, F)),
        [BACK],
    )(core_of, share_count, right_side, image, own, *back, index, mass, absorb, imped, row)


def solution(mesh):
    line = P(DOM)
    in_specs = (
        P(None, DOM),
        P(None, None, DOM),
        P(None, DOM),
        P(DOM, None, None),
        P(DOM, None),
        line,
        line,
        line,
    )
    out_specs = (P(None, DOM), P(None, DOM))
    return jax.shard_map(
        shards, mesh=mesh, in_specs=in_specs, out_specs=out_specs, check_vma=False
    )
```

time: 204 us -> 90.8 us (0.45)
  blocking collectives: 98.1 us -> 0 us
  Pallas kernels: 0 us -> 30.8 us
  matrix products: 20.2 us -> 0 us
  other arithmetic: 21.3 us -> 2.92 us
  waiting for transfers between devices: 2.25 us -> 14 us
  starting transfers between devices: 47.3 us -> 39.4 us
  between operations: 7.17 us -> 0.74 us
  local copies, waits for them, and re-layouts: 6.39 us -> 2.44 us
    psum x8 -> x0, blocking collectives: 98.1 us -> none  [by_axis(): return functools.reduce(lax.psum, axes, value)]
    pallas_call x0 -> x7, Pallas kernels: none -> 30.8 us  [the longest x2 18.3 us: apply_of(): call(apply_kernel, name, [sspec()] + [vspec()] * 6, (shape(TR, F),) + BLO...]
    dot_general x4 -> x0, matrix products: 20.2 us -> none  [the longest x2 11.2 us: operate(): lax.dot_general(spread, selector, (((1,), (1,)), ((), ())), precision=lax...]
    ppermute x16 -> x12, starting transfers between devices: 47.3 us -> 35.3 us  [the longest x8 30.7 us: shift(): lax.ppermute(value, DOM, [(i, (i + steps) % count) for i in range(count)])]
    reduce_sum x5 -> x0, other arithmetic: 10.1 us -> none  [the longest x2 8.08 us: operate(): jnp.sum(element_matrix.astype(jnp.float32) * picked[None, :, :], axis=1)]
    scatter-add x2 -> x0, other arithmetic: 7.41 us -> none  [operate(): summed[:, :own_faces].at[:, send_rows].add(returned.transpose(1, 0, 2))]
    all_to_all x0 -> x1, waiting for transfers between devices: none -> 6.87 us  [shards(): row = lax.all_to_all(row, DOM, 0, 0)]
    ppermute x16 -> x12, waiting for transfers between devices: 2.25 us -> 7.13 us  [the longest x8 4.58 us: shift(): lax.ppermute(value, DOM, [(i, (i + steps) % count) for i in range(count)])]
  transfers between devices with their start and end apart: 16 -> 13, of which waited for: 3 -> 7; matrix products, arithmetic and copies ran while one was open for 2% -> 1% of each run, Pallas kernels for 0% -> 7%
where the time goes in v1:
time: 90.8 us; the launch traced here: 90.2 us
  starting transfers between devices  39.4 us (43%)
  Pallas kernels  30.8 us (34%)
  waiting for transfers between devices  14 us (15%)
  other arithmetic  2.92 us (3%)
  local copies, waits for them, and re-layouts  2.44 us (3%)
    ppermute x8, starting transfers between devices, shift(): lax.ppermute(value, DOM, [(i, (i + steps) % count) for i in range(count)])  30.7 us
    pallas_call x2, Pallas kernels, apply_of(): call(apply_kernel, name, [sspec()] + [vspec()] * 6, (shape(TR, F),) + BLO...  18.3 us
    all_to_all x1, waiting for transfers between devices, shards(): row = lax.all_to_all(row, DOM, 0, 0)  6.87 us
    ppermute x4, starting transfers between devices, exchange(): lax.ppermute(jnp.stack([mid, onward]), DOM, [(i, i ^ 1) for i in range(co...  4.64 us
    pallas_call x1, Pallas kernels, shards(): call(selector_kernel, 'selector', [vspec()], shape(SLOTS, PICKS, dtype=BF...  4.63 us
    ppermute x8, waiting for transfers between devices, shift(): lax.ppermute(value, DOM, [(i, (i + steps) % count) for i in range(count)])  4.58 us
    all_to_all x1, starting transfers between devices, shards(): row = lax.all_to_all(row, DOM, 0, 0)  4 us
    another operation x4, other arithmetic, exchange(): jnp.stack([mid, onward])  2.9 us
  transfers between devices with their start and end apart: 13, of which 7 were waited for; matrix products, arithmetic and copies ran while one was open for 1% of the time, Pallas kernels for 7%

profile of v1, /device:TPU:1, one launch (start us, length us, event | category | flops | bytes accessed | tf_op | source)
XLA Modules:
  0.0 90.2 jit_solution(15972760059499864041)
XLA Ops:
  0.6 1.8 %send.1 = (f32[2,18,128]{2,1,0:T(8,128)}, f32[2,18,128]{2,1,0:T(8,128)}, f32[18,128]{1,0:T(8,128)}) custom-call(s32[1]{0:T(128)} %bitcast.core_ref, s32[1,4]{1,0:T(1,128)} %count_ref.5, f32[18,1024]{1,0:T(8,128)} %field_ref.7, s32[4,128]{1,0:T(4,128)} %bitcast.9), custom_call_target="tpu_custom_call" | custom-call | tf_op jit(solution)/shard_map/send/pallas_call | solution.py:291
  2.5 2.0 %collective-permute-start = (f32[2,18,128]{2,1,0:T(8,128)}, f32[2,18,128]{2,1,0:T(8,128)S(1)}, u32[]{:S(2)}, u32[]{:S(2)}) collective-permute-start(f32[2,18,128]{2,1,0:T(8,128)} %get-tuple-element.20), channel_id=1, source_target_pairs={{0,2},{1,3},{2,4},{3,5},{4,6},{5,7},{6,8},{7,9},{8,10},{9,11},{10,... | collective-permute-start | bytes 55304 | tf_op jit(solution)/shard_map/ppermute | solution.py:282
  4.5 7.2 %collective-permute-start.1 = (f32[2,18,128]{2,1,0:T(8,128)}, f32[2,18,128]{2,1,0:T(8,128)S(1)}, u32[]{:S(2)}, u32[]{:S(2)}) collective-permute-start(f32[2,18,128]{2,1,0:T(8,128)} %get-tuple-element.21), channel_id=1, source_target_pairs={{0,126},{1,127},{2,0},{3,1},{4,2},{5,3},{6,4},{7,5},{8,6},{9,7},{1... | collective-permute-start | bytes 55304 | tf_op jit(solution)/shard_map/ppermute | solution.py:282
  11.7 1.4 %collective-permute-done.up_ref = f32[2,18,128]{2,1,0:T(8,128)S(1)} collective-permute-done((f32[2,18,128]{2,1,0:T(8,128)}, f32[2,18,128]{2,1,0:T(8,128)S(1)}, u32[]{:S(2)}, u32[]{:S(2)}) %collective-permute-start) | collective-permute-done | bytes 18464 | tf_op jit(solution)/shard_map/ppermute | solution.py:282
  13.1 0.7 pad_maximum_fusion
  13.9 1.5 %collective-permute-start.2 = (f32[2,18,128]{2,1,0:T(8,128)S(1)}, f32[2,18,128]{2,1,0:T(8,128)S(1)}, u32[]{:S(2)}, u32[]{:S(2)}) collective-permute-start(f32[2,18,128]{2,1,0:T(8,128)S(1)} %pad_maximum_fusion), channel_id=1, source_target_pairs={{0,1},{1,0},{2,3},{3,2},{4,5},{5,4},{6,7},{7,6},{8,9},{9,8},{10,11... | collective-permute-start | bytes 55304 | tf_op jit(solution)/shard_map/ppermute | solution.py:288
  15.4 4.6 %selector.1.sel_ref = bf16[1536,2048]{1,0:T(8,128)(2,1)} custom-call(s32[4,512]{1,0:T(4,128)} %map_ref.1), custom_call_target="tpu_custom_call" | custom-call | tf_op jit(solution)/shard_map/selector/pallas_call | solution.py:295
  20.7 9.1 %apply0.1 = (f32[18,1024]{1,0:T(8,128)}, f32[2,18,128]{2,1,0:T(8,128)}, f32[2,18,128]{2,1,0:T(8,128)}, f32[18,128]{1,0:T(8,128)}, f32[1,128]{1,0:T(1,128)}) custom-call(s32[1]{0:T(128)} %bitcast.core_ref, f32[18,1024]{1,0:T(8,128)} %field_ref.7, f32[2,18,128]{2,1,0:T(8,128)} %copy-done.1, f32[2,18,128]{2,1,0:T(8,128)} %copy-done.2, f32[2,18,128]{2,1,0:T(8,128)} %copy-done.9, ...), custom_call_target="tpu_custom_call" | custom-call | tf_op jit(solution)/shard_map/apply0/pallas_call | solution.py:298
  29.8 7.2 %collective-permute-start.4 = (f32[2,18,128]{2,1,0:T(8,128)}, f32[2,18,128]{2,1,0:T(8,128)S(1)}, u32[]{:S(2)}, u32[]{:S(2)}) collective-permute-start(f32[2,18,128]{2,1,0:T(8,128)} %get-tuple-element.25), channel_id=1, source_target_pairs={{0,126},{1,127},{2,0},{3,1},{4,2},{5,3},{6,4},{7,5},{8,6},{9,7},{1... | collective-permute-start | bytes 55304 | tf_op jit(solution)/shard_map/ppermute | solution.py:282
  36.9 1.8 %collective-permute-done.3.up_ref = f32[2,18,128]{2,1,0:T(8,128)S(1)} collective-permute-done((f32[2,18,128]{2,1,0:T(8,128)}, f32[2,18,128]{2,1,0:T(8,128)S(1)}, u32[]{:S(2)}, u32[]{:S(2)}) %collective-permute-start.3) | collective-permute-done | bytes 18464 | tf_op jit(solution)/shard_map/ppermute | solution.py:282
  40.1 0.8 collective-permute-done.5.mid_ref
  41.5 2.4 %combine.1 = (f32[18,1024]{1,0:T(8,128)}, f32[2,18,128]{2,1,0:T(8,128)}, f32[2,18,128]{2,1,0:T(8,128)}, f32[18,128]{1,0:T(8,128)}, f32[1,128]{1,0:T(1,128)}) custom-call(s32[1]{0:T(128)} %bitcast.core_ref, s32[1,4]{1,0:T(1,128)} %count_ref.5, f32[18,1024]{1,0:T(8,128)} %field_ref.7, f32[18,1024]{1,0:T(8,128)} %get-tuple-element.23.own_ref, ...), custom_call_target="tpu_custom_call" | custom-call | tf_op jit(solution)/shard_map/combine/pallas_call | solution.py:313
  43.9 7.2 %collective-permute-start.7 = (f32[2,18,128]{2,1,0:T(8,128)}, f32[2,18,128]{2,1,0:T(8,128)S(1)}, u32[]{:S(2)}, u32[]{:S(2)}) collective-permute-start(f32[2,18,128]{2,1,0:T(8,128)} %get-tuple-element.30), channel_id=1, source_target_pairs={{0,126},{1,127},{2,0},{3,1},{4,2},{5,3},{6,4},{7,5},{8,6},{9,7},{1... | collective-permute-start | bytes 55304 | tf_op jit(solution)/shard_map/ppermute | solution.py:282
  51.1 1.4 %collective-permute-done.6.up_ref = f32[2,18,128]{2,1,0:T(8,128)S(1)} collective-permute-done((f32[2,18,128]{2,1,0:T(8,128)}, f32[2,18,128]{2,1,0:T(8,128)S(1)}, u32[]{:S(2)}, u32[]{:S(2)}) %collective-permute-start.6) | collective-permute-done | bytes 18464 | tf_op jit(solution)/shard_map/ppermute | solution.py:282
  53.2 1.3 %collective-permute-start.8 = (f32[2,18,128]{2,1,0:T(8,128)S(1)}, f32[2,18,128]{2,1,0:T(8,128)S(1)}, u32[]{:S(2)}, u32[]{:S(2)}) collective-permute-start(f32[2,18,128]{2,1,0:T(8,128)S(1)} %pad_maximum_fusion.2), channel_id=1, source_target_pairs={{0,1},{1,0},{2,3},{3,2},{4,5},{5,4},{6,7},{7,6},{8,9},{9,8},{10,11... | collective-permute-start | bytes 55304 | tf_op jit(solution)/shard_map/ppermute | solution.py:288
  54.5 0.8 collective-permute-done.8.mid_ref
  55.9 9.1 %apply1.1 = (f32[18,1024]{1,0:T(8,128)}, f32[2,18,128]{2,1,0:T(8,128)}, f32[2,18,128]{2,1,0:T(8,128)}, f32[18,128]{1,0:T(8,128)}, f32[1,128]{1,0:T(1,128)}) custom-call(s32[1]{0:T(128)} %bitcast.core_ref, f32[18,1024]{1,0:T(8,128)} %get-tuple-element.28.field_ref.image_ref, f32[2,18,128]{2,1,0:T(8,128)} %copy-done.3, f32[2,18,128]{2,1,0:T(8,128)} %copy-done.4, ...), custom_call_target="tpu_custom_call" | custom-call | tf_op jit(solution)/shard_map/apply1/pallas_call | solution.py:298
  65.1 7.2 %collective-permute-start.10 = (f32[2,18,128]{2,1,0:T(8,128)}, f32[2,18,128]{2,1,0:T(8,128)S(1)}, u32[]{:S(2)}, u32[]{:S(2)}) collective-permute-start(f32[2,18,128]{2,1,0:T(8,128)} %get-tuple-element.34), channel_id=1, source_target_pairs={{0,126},{1,127},{2,0},{3,1},{4,2},{5,3},{6,4},{7,5},{8,6},{9,7},{1... | collective-permute-start | bytes 55304 | tf_op jit(solution)/shard_map/ppermute | solution.py:282
  72.2 1.4 %sums.1 = f32[128,1,128]{2,1,0:T(1,128)} custom-call(f32[1,128]{1,0:T(1,128)} %get-tuple-element.36.sums_ref, f32[1,128]{1,0:T(1,128)} %get-tuple-element.37.energy_ref), custom_call_target="tpu_custom_call" | custom-call | tf_op jit(solution)/shard_map/sums/pallas_call | solution.py:322
  73.7 4.0 %all-to-all-start = ((f32[128,1,128]{2,1,0:T(1,128)}), f32[128,1,128]{2,1,0:T(1,128)S(1)}, u32[]{:S(2)}, u32[]{:S(2)}) async-start(f32[128,1,128]{2,1,0:T(1,128)} %sums.1), calls=%async_computation | async-start | bytes 131072 | tf_op jit(solution)/shard_map/all_to_all | solution.py:323
  78.4 1.2 %collective-permute-start.11 = (f32[2,18,128]{2,1,0:T(8,128)S(1)}, f32[2,18,128]{2,1,0:T(8,128)S(1)}, u32[]{:S(2)}, u32[]{:S(2)}) collective-permute-start(f32[2,18,128]{2,1,0:T(8,128)S(1)} %pad_maximum_fusion.3), channel_id=1, source_target_pairs={{0,1},{1,0},{2,3},{3,2},{4,5},{5,4},{6,7},{7,6},{8,9},{9,8},{10,11... | collective-permute-start | bytes 55304 | tf_op jit(solution)/shard_map/ppermute | solution.py:288
  79.6 0.8 collective-permute-done.11.mid_ref
  80.5 6.9 %all-to-all-done.sums_ref = f32[128,1,128]{2,1,0:T(1,128)S(1)} async-done(((f32[128,1,128]{2,1,0:T(1,128)}), f32[128,1,128]{2,1,0:T(1,128)S(1)}, u32[]{:S(2)}, u32[]{:S(2)}) %all-to-all-start) | async-done | bytes 65568 | tf_op jit(solution)/shard_map/all_to_all | solution.py:323
  88.0 2.2 %final.1 = (f32[18,1024]{1,0:T(8,128)}, f32[18,1024]{1,0:T(8,128)}) custom-call(s32[1]{0:T(128)} %bitcast.core_ref, s32[1,4]{1,0:T(1,128)} %count_ref.5, f32[18,1024]{1,0:T(8,128)} %field_ref.7, f32[18,1024]{1,0:T(8,128)} %get-tuple-element.28.field_ref.image_ref, f32[18,1024]{1,0:T(8,128)} %get-tuple-element.32.own_ref, f32[2,18,128]{2,1,0:T(8,128)} %copy-done.5, ...), custom_call_target="tpu_custom_call" | custom-call | tf_op jit(solution)/shard_map/final/pallas_call | solution.py:325
  (43 shorter events, 5.2 us)
Async XLA Ops:
  2.5 10.6 %collective-permute-start = (f32[2,18,128]{2,1,0:T(8,128)}, f32[2,18,128]{2,1,0:T(8,128)S(1)}, u32[]{:S(2)}, u32[]{:S(2)}) collective-permute-start(f32[2,18,128]{2,1,0:T(8,128)} %get-tuple-element.20), channel_id=1, source_target_pairs={{0,2},{1,3},{2,4},{3,5},{4,6},{5,7},{6,8},{7,9},{8,10},{9,11},{10,... | collective-permute-start | bytes 55304 | tf_op jit(solution)/shard_map/ppermute | solution.py:282
  4.5 8.6 %collective-permute-start.1 = (f32[2,18,128]{2,1,0:T(8,128)}, f32[2,18,128]{2,1,0:T(8,128)S(1)}, u32[]{:S(2)}, u32[]{:S(2)}) collective-permute-start(f32[2,18,128]{2,1,0:T(8,128)} %get-tuple-element.21), channel_id=1, source_target_pairs={{0,126},{1,127},{2,0},{3,1},{4,2},{5,3},{6,4},{7,5},{8,6},{9,7},{1... | collective-permute-start | bytes 55304 | tf_op jit(solution)/shard_map/ppermute | solution.py:282
  13.1 6.9 %copy-start.1 = (f32[2,18,128]{2,1,0:T(8,128)}, f32[2,18,128]{2,1,0:T(8,128)S(1)}, u32[]{:S(2)}) copy-start(f32[2,18,128]{2,1,0:T(8,128)S(1)} %collective-permute-done.up_ref) | copy-start | bytes 55300
  13.1 6.9 %copy-start.2 = (f32[2,18,128]{2,1,0:T(8,128)}, f32[2,18,128]{2,1,0:T(8,128)S(1)}, u32[]{:S(2)}) copy-start(f32[2,18,128]{2,1,0:T(8,128)S(1)} %collective-permute-done.1.down_ref) | copy-start | bytes 55300
  13.9 6.2 %collective-permute-start.2 = (f32[2,18,128]{2,1,0:T(8,128)S(1)}, f32[2,18,128]{2,1,0:T(8,128)S(1)}, u32[]{:S(2)}, u32[]{:S(2)}) collective-permute-start(f32[2,18,128]{2,1,0:T(8,128)S(1)} %pad_maximum_fusion), channel_id=1, source_target_pairs={{0,1},{1,0},{2,3},{3,2},{4,5},{5,4},{6,7},{7,6},{8,9},{9,8},{10,11... | collective-permute-start | bytes 55304 | tf_op jit(solution)/shard_map/ppermute | solution.py:288
  29.8 8.9 %collective-permute-start.3 = (f32[2,18,128]{2,1,0:T(8,128)}, f32[2,18,128]{2,1,0:T(8,128)S(1)}, u32[]{:S(2)}, u32[]{:S(2)}) collective-permute-start(f32[2,18,128]{2,1,0:T(8,128)} %get-tuple-element.24), channel_id=1, source_target_pairs={{0,2},{1,3},{2,4},{3,5},{4,6},{5,7},{6,8},{7,9},{8,10},{9,11},{10,... | collective-permute-start | bytes 55304 | tf_op jit(solution)/shard_map/ppermute | solution.py:282
  29.8 9.0 %collective-permute-start.4 = (f32[2,18,128]{2,1,0:T(8,128)}, f32[2,18,128]{2,1,0:T(8,128)S(1)}, u32[]{:S(2)}, u32[]{:S(2)}) collective-permute-start(f32[2,18,128]{2,1,0:T(8,128)} %get-tuple-element.25), channel_id=1, source_target_pairs={{0,126},{1,127},{2,0},{3,1},{4,2},{5,3},{6,4},{7,5},{8,6},{9,7},{1... | collective-permute-start | bytes 55304 | tf_op jit(solution)/shard_map/ppermute | solution.py:282
  38.7 2.2 %copy-start.7 = (f32[2,18,128]{2,1,0:T(8,128)}, f32[2,18,128]{2,1,0:T(8,128)S(1)}, u32[]{:S(2)}) copy-start(f32[2,18,128]{2,1,0:T(8,128)S(1)} %collective-permute-done.3.up_ref) | copy-start | bytes 55300
  38.7 2.2 %copy-start.8 = (f32[2,18,128]{2,1,0:T(8,128)}, f32[2,18,128]{2,1,0:T(8,128)S(1)}, u32[]{:S(2)}) copy-start(f32[2,18,128]{2,1,0:T(8,128)S(1)} %collective-permute-done.4.down_ref) | copy-start | bytes 55300
  39.5 1.4 %collective-permute-start.5 = (f32[2,18,128]{2,1,0:T(8,128)S(1)}, f32[2,18,128]{2,1,0:T(8,128)S(1)}, u32[]{:S(2)}, u32[]{:S(2)}) collective-permute-start(f32[2,18,128]{2,1,0:T(8,128)S(1)} %pad_maximum_fusion.1), channel_id=1, source_target_pairs={{0,1},{1,0},{2,3},{3,2},{4,5},{5,4},{6,7},{7,6},{8,9},{9,8},{10,11... | collective-permute-start | bytes 55304 | tf_op jit(solution)/shard_map/ppermute | solution.py:288
  40.9 0.6 copy-start.12
  43.9 8.5 %collective-permute-start.6 = (f32[2,18,128]{2,1,0:T(8,128)}, f32[2,18,128]{2,1,0:T(8,128)S(1)}, u32[]{:S(2)}, u32[]{:S(2)}) collective-permute-start(f32[2,18,128]{2,1,0:T(8,128)} %get-tuple-element.29), channel_id=1, source_target_pairs={{0,2},{1,3},{2,4},{3,5},{4,6},{5,7},{6,8},{7,9},{8,10},{9,11},{10,... | collective-permute-start | bytes 55304 | tf_op jit(solution)/shard_map/ppermute | solution.py:282
  43.9 8.5 %collective-permute-start.7 = (f32[2,18,128]{2,1,0:T(8,128)}, f32[2,18,128]{2,1,0:T(8,128)S(1)}, u32[]{:S(2)}, u32[]{:S(2)}) collective-permute-start(f32[2,18,128]{2,1,0:T(8,128)} %get-tuple-element.30), channel_id=1, source_target_pairs={{0,126},{1,127},{2,0},{3,1},{4,2},{5,3},{6,4},{7,5},{8,6},{9,7},{1... | collective-permute-start | bytes 55304 | tf_op jit(solution)/shard_map/ppermute | solution.py:282
  52.4 2.9 %copy-start.3 = (f32[2,18,128]{2,1,0:T(8,128)}, f32[2,18,128]{2,1,0:T(8,128)S(1)}, u32[]{:S(2)}) copy-start(f32[2,18,128]{2,1,0:T(8,128)S(1)} %collective-permute-done.6.up_ref) | copy-start | bytes 55300
  52.4 2.9 %copy-start.4 = (f32[2,18,128]{2,1,0:T(8,128)}, f32[2,18,128]{2,1,0:T(8,128)S(1)}, u32[]{:S(2)}) copy-start(f32[2,18,128]{2,1,0:T(8,128)S(1)} %collective-permute-done.7.down_ref) | copy-start | bytes 55300
  53.2 2.2 %collective-permute-start.8 = (f32[2,18,128]{2,1,0:T(8,128)S(1)}, f32[2,18,128]{2,1,0:T(8,128)S(1)}, u32[]{:S(2)}, u32[]{:S(2)}) collective-permute-start(f32[2,18,128]{2,1,0:T(8,128)S(1)} %pad_maximum_fusion.2), channel_id=1, source_target_pairs={{0,1},{1,0},{2,3},{3,2},{4,5},{5,4},{6,7},{7,6},{8,9},{9,8},{10,11... | collective-permute-start | bytes 55304 | tf_op jit(solution)/shard_map/ppermute | solution.py:288
  65.1 12.6 %collective-permute-start.9 = (f32[2,18,128]{2,1,0:T(8,128)}, f32[2,18,128]{2,1,0:T(8,128)S(1)}, u32[]{:S(2)}, u32[]{:S(2)}) collective-permute-start(f32[2,18,128]{2,1,0:T(8,128)} %get-tuple-element.33), channel_id=1, source_target_pairs={{0,2},{1,3},{2,4},{3,5},{4,6},{5,7},{6,8},{7,9},{8,10},{9,11},{10,... | collective-permute-start | bytes 55304 | tf_op jit(solution)/shard_map/ppermute | solution.py:282
  65.1 12.6 %collective-permute-start.10 = (f32[2,18,128]{2,1,0:T(8,128)}, f32[2,18,128]{2,1,0:T(8,128)S(1)}, u32[]{:S(2)}, u32[]{:S(2)}) collective-permute-start(f32[2,18,128]{2,1,0:T(8,128)} %get-tuple-element.34), channel_id=1, source_target_pairs={{0,126},{1,127},{2,0},{3,1},{4,2},{5,3},{6,4},{7,5},{8,6},{9,7},{1... | collective-permute-start | bytes 55304 | tf_op jit(solution)/shard_map/ppermute | solution.py:282
  73.7 13.7 %all-to-all-start = ((f32[128,1,128]{2,1,0:T(1,128)}), f32[128,1,128]{2,1,0:T(1,128)S(1)}, u32[]{:S(2)}, u32[]{:S(2)}) async-start(f32[128,1,128]{2,1,0:T(1,128)} %sums.1), calls=%async_computation | async-start | bytes 131072 | tf_op jit(solution)/shard_map/all_to_all | solution.py:323
  77.7 9.7 %copy-start.5 = (f32[2,18,128]{2,1,0:T(8,128)}, f32[2,18,128]{2,1,0:T(8,128)S(1)}, u32[]{:S(2)}) copy-start(f32[2,18,128]{2,1,0:T(8,128)S(1)} %collective-permute-done.9.up_ref) | copy-start | bytes 55300
  77.7 9.7 %copy-start.6 = (f32[2,18,128]{2,1,0:T(8,128)}, f32[2,18,128]{2,1,0:T(8,128)S(1)}, u32[]{:S(2)}) copy-start(f32[2,18,128]{2,1,0:T(8,128)S(1)} %collective-permute-done.10.down_ref) | copy-start | bytes 55300
  78.4 2.1 %collective-permute-start.11 = (f32[2,18,128]{2,1,0:T(8,128)S(1)}, f32[2,18,128]{2,1,0:T(8,128)S(1)}, u32[]{:S(2)}, u32[]{:S(2)}) collective-permute-start(f32[2,18,128]{2,1,0:T(8,128)S(1)} %pad_maximum_fusion.3), channel_id=1, source_target_pairs={{0,1},{1,0},{2,3},{3,2},{4,5},{5,4},{6,7},{7,6},{8,9},{9,8},{10,11... | collective-permute-start | bytes 55304 | tf_op jit(solution)/shard_map/ppermute | solution.py:288
  80.5 6.9 %copy-start.11 = (f32[2,18,128]{2,1,0:T(8,128)}, f32[2,18,128]{2,1,0:T(8,128)S(1)}, u32[]{:S(2)}) copy-start(f32[2,18,128]{2,1,0:T(8,128)S(1)} %collective-permute-done.11.mid_ref) | copy-start | bytes 55300
  87.4 0.6 copy-start
  (2 other events, 1.2 us)

commit v2 on v0

v2 whole, which is shorter than its diff:
```python
import jax
import jax.numpy as jnp
from jax import lax
from jax.experimental import pallas as pl
from jax.experimental.pallas import tpu as pltpu
from jax.sharding import PartitionSpec as P


DOM = "dom"
TR = 18
TP = 24
SIDES = 4
E = 512
F = 1024
GH = 128
NB = 4
SHARED = NB * GH
PICKS = SIDES * E
DOFS = SIDES * TR
F32 = jnp.float32
BF16 = jnp.bfloat16
VMEM = pltpu.VMEM
SMEM = pltpu.SMEM


def pieces(x):
    hi = x.astype(BF16).astype(F32)
    rest = x - hi
    mid = rest.astype(BF16).astype(F32)
    return jnp.concatenate([hi, mid, rest - mid], axis=0).astype(BF16)


def joined(y):
    rows = y.shape[0] // 3
    return y[:rows] + y[rows : 2 * rows] + y[2 * rows :]


def pick(x, selector):
    return joined(jnp.dot(pieces(x), selector, preferred_element_type=F32))


def spread_out(x, selector):
    return joined(
        lax.dot_general(pieces(x), selector, (((1,), (1,)), ((), ())), preferred_element_type=F32)
    )


def split(x):
    return [x[:, k * GH : (k + 1) * GH] for k in range(NB)]


def write_blocks(blocks, place_ref, near_ref, far_ref, mid_ref):
    core, odd = place_ref[0], place_ref[1]
    ahead, next_up, next_down, behind = (blocks[k] for k in (3, 2, 1, 0))
    near_ref[0] = jnp.where(odd == 1, behind, ahead)
    near_ref[1] = jnp.where(odd == 1, next_down, next_up)
    far_ref[0] = jnp.where(odd == 1, ahead, behind)
    far_ref[1] = jnp.where(odd == 1, next_up, next_down)
    mid_ref[...] = jnp.where(core == 1, next_down, next_up)


def read_blocks(place_ref, near_ref, far_ref, mid_ref):
    core, odd = place_ref[0], place_ref[1]
    near, far, first, second = near_ref[0], far_ref[0], mid_ref[0], mid_ref[1]
    return [
        jnp.where(odd == 1, far, near),
        jnp.where(core == 1, second, first),
        jnp.where(core == 1, first, second),
        jnp.where(odd == 1, near, far),
    ]


def lanes_of(values):
    lane = lax.broadcasted_iota(jnp.int32, (1, GH), 1)
    row = jnp.zeros((1, GH), F32)
    for at, value in enumerate(values):
        row = row + jnp.where(lane == at, value, 0.0)
    return row


def total(x):
    return jnp.sum(jnp.sum(x, axis=0, keepdims=True), axis=1, keepdims=True)


def send_kernel(place_ref, count_ref, field_ref, index_ref, near_ref, far_ref, mid_ref, share_ref, padded_ref):
    for k in range(NB):
        rows = lax.broadcasted_iota(jnp.int32, (F, GH), 0)
        lanes = lax.broadcasted_iota(jnp.int32, (1, GH), 1)
        face = jnp.where(lanes < count_ref[0, k], index_ref[k : k + 1, :], -1)
        share_ref[:, k * GH : (k + 1) * GH] = jnp.where(rows == face, 1.0, 0.0).astype(BF16)
    padded_ref[TR:, :] = jnp.zeros((TP - TR, F), F32)
    padded_ref[:TR, :] = field_ref[...]
    write_blocks(split(pick(padded_ref[...], share_ref[...])), place_ref, near_ref, far_ref, mid_ref)


def fill_selector(map_ref, sel_ref, first):
    slots = sel_ref.shape[0]
    for s in range(SIDES):
        rows = lax.broadcasted_iota(jnp.int32, (slots, E), 0) + first
        sel_ref[:, s * E : (s + 1) * E] = jnp.where(rows == map_ref[s : s + 1, :], 1.0, 0.0).astype(BF16)


def select_kernel(map_ref, field_ref, matrix_ref, ghost_sel_ref, local_ref, held_ref, sel_ref, sem):
    copy = pltpu.make_async_copy(matrix_ref, held_ref, sem)
    copy.start()
    fill_selector(map_ref, sel_ref, 0)
    local_ref[...] = pick(field_ref[...], sel_ref[...])
    fill_selector(map_ref, ghost_sel_ref, F)
    copy.wait()


def product_kernel(place_ref, near_ref, far_ref, mid_ref, sel_ref, matrix_ref, local_ref, *refs):
    near_out, far_out, mid_out, spread_ref, pick_ref, ghost_ref, prod_ref = refs[-7:]
    for k, block in enumerate(read_blocks(place_ref, near_ref, far_ref, mid_ref)):
        ghost_ref[:, k * GH : (k + 1) * GH] = block
    pick_ref[...] = local_ref[...] + pick(ghost_ref[...], sel_ref[...])
    for t in range(E // 128):
        acc = jnp.zeros((DOFS, 128), F32)
        for j in range(DOFS):
            s, c = divmod(j, TR)
            row = pick_ref[c : c + 1, s * E + t * 128 : s * E + (t + 1) * 128]
            acc = acc + matrix_ref[j, :, t * 128 : (t + 1) * 128].astype(F32) * row
        prod_ref[:, t * 128 : (t + 1) * 128] = acc
    spread_ref[TR:, :] = jnp.zeros((TP - TR, PICKS), F32)
    for s in range(SIDES):
        spread_ref[:TR, s * E : (s + 1) * E] = prod_ref[s * TR : (s + 1) * TR, :]
    parts = split(spread_out(spread_ref[...], sel_ref[...]))
    write_blocks(parts[::-1], place_ref, near_out, far_out, mid_out)
    if len(refs) == 10:
        first_ref, second_ref, row_ref = refs[:3]
        lane = lax.broadcasted_iota(jnp.int32, (1, GH), 1)
        energy = total(spread_ref[...] * pick_ref[...])
        row = first_ref[...] + second_ref[...] + jnp.where(lane == 3, energy, 0.0)
        row_ref[...] = jnp.broadcast_to(row[None], row_ref.shape)


def diagonal_of(mass_ref, absorbing_ref, impedance_ref):
    return mass_ref[...] + absorbing_ref[...].astype(F32) * impedance_ref[...]


def own_kernel(spread_ref, map_ref, field_ref, mass_ref, absorbing_ref, impedance_ref, *refs):
    own_ref, sel_ref = refs[-2:]
    fill_selector(map_ref, sel_ref, 0)
    field = field_ref[...]
    damped = diagonal_of(mass_ref, absorbing_ref, impedance_ref) * field
    if len(refs) == 4:
        pick_ref, sums_ref = refs[:2]
        energy = total(damped * field) + total(pick_ref[...] * spread_ref[...])
        sums_ref[...] = lanes_of([total(field * field), energy])
    own_ref[...] = spread_out(spread_ref[...], sel_ref[...]) + damped


def combine_kernel(place_ref, own_ref, near_ref, far_ref, mid_ref, share_ref, image_ref, near_out, far_out, mid_out, back_ref):
    for k, block in enumerate(read_blocks(place_ref, near_ref, far_ref, mid_ref)[::-1]):
        back_ref[:, k * GH : (k + 1) * GH] = block
    image = own_ref[...] + spread_out(back_ref[...], share_ref[...])
    image_ref[...] = image
    write_blocks(split(pick(image, share_ref[...])), place_ref, near_out, far_out, mid_out)


def local_kernel(image_ref, map_ref, mass_ref, absorbing_ref, impedance_ref, local_ref, sums_ref, sel_ref):
    fill_selector(map_ref, sel_ref, 0)
    image = image_ref[...]
    local_ref[...] = pick(image, sel_ref[...])
    square = image * image
    weighted = diagonal_of(mass_ref, absorbing_ref, impedance_ref) * square
    sums_ref[...] = lanes_of([0.0, 0.0, total(square), total(weighted)])


def final_kernel(
    place_ref, own_ref, near_ref, far_ref, mid_ref, share_ref, field_ref, image_ref, sums_ref, solution_ref, residual_ref, back_ref
):
    for k, block in enumerate(read_blocks(place_ref, near_ref, far_ref, mid_ref)[::-1]):
        back_ref[:, k * GH : (k + 1) * GH] = block
    second = own_ref[...] + spread_out(back_ref[...], share_ref[...])
    field, image = field_ref[:TR], image_ref[:TR]
    row = jnp.sum(sums_ref[...], axis=0)
    s0, s1, s2, s3 = (row[:, k : k + 1] for k in range(4))
    step0 = s0 / s1
    ratio = (step0 * step0 * s2 - s0) / s0
    grow = 1.0 + ratio
    curvature = grow * grow * s1 - 2.0 * step0 * grow * s2 + step0 * step0 * s3
    step1 = ratio * s0 / curvature
    along = step0 + step1 * grow
    solution_ref[...] = along * field - (step0 * step1) * image
    residual_ref[...] = field - along * image + (step0 * step1) * second[:TR]


MESSAGE = (VMEM((2, TP, GH), F32), VMEM((2, TP, GH), F32), VMEM((TP, GH), F32))
WIDE = VMEM((TP, PICKS), F32)
FACES = VMEM((TP, F), F32)
GHOSTS = VMEM((TP, SHARED), F32)
ROW = VMEM((1, GH), F32)


OWN_SELECTOR = VMEM((F, PICKS), BF16)
ANY = pl.ANY


def call(kernel, out_shape, *args, scratch=(), scalars=1, held=VMEM, last=VMEM):
    spaces = [SMEM] * scalars + [VMEM] * (len(args) - scalars - 1) + [last]
    args = [
        a if m is SMEM else pltpu.with_memory_space_constraint(a, pltpu.HBM if m is ANY else held)
        for a, m in zip(args, spaces)
    ]
    return pl.pallas_call(
        kernel,
        in_specs=[pl.BlockSpec(memory_space=m) for m in spaces],
        out_specs=jax.tree.map(lambda _: pl.BlockSpec(memory_space=VMEM), out_shape),
        out_shape=out_shape,
        scratch_shapes=scratch,
        compiler_params=pltpu.CompilerParams(vmem_limit_bytes=16 * 1024 * 1024),
    )(*args)


def shards(
    right_side, element_matrix, face_map, share_index, share_count, face_mass, absorbing, impedance
):
    count = lax.axis_size(DOM)
    here = lax.axis_index(DOM).astype(jnp.int32)
    core, odd = here & 1, (here >> 1) & 1
    place = jnp.stack([core, odd])
    diagonal = [x.reshape(1, F) for x in (face_mass, absorbing, impedance)]
    chips = range(count // 2)
    far_of = [(((c + 1) ^ 1) - 1) % (count // 2) for c in chips]

    def swap(value, partner):
        return lax.ppermute(value, DOM, [(2 * c + b, 2 * partner[c] + b) for c in chips for b in range(2)])

    def exchange(near, far, mid, beside):
        got_far = swap(far, far_of)
        got_near = swap(near, [c ^ 1 for c in chips])
        got_near, got_far, beside = lax.optimization_barrier((got_near, got_far, beside()))
        onward = jnp.where(core == odd, got_near[1], got_far[1])
        pair = jnp.stack([mid, onward])
        got_mid = lax.ppermute(pair, DOM, [(i, i ^ 1) for i in range(count)])
        return (got_near, got_far, got_mid), beside

    *sent, share, padded = call(
        send_kernel,
        MESSAGE + (VMEM((F, SHARED), BF16), FACES),
        place,
        share_count,
        right_side,
        share_index[0],
        scalars=2,
        held=pltpu.HBM,
    )

    def select():
        return call(
            select_kernel,
            (VMEM((SHARED, PICKS), BF16), WIDE, VMEM((DOFS, DOFS, E), BF16)),
            face_map,
            padded,
            element_matrix,
            scratch=[OWN_SELECTOR, pltpu.SemaphoreType.DMA],
            scalars=0,
            last=ANY,
        )

    got, (selector, local, matrix) = exchange(*sent, select)
    scratch = [GHOSTS, VMEM((DOFS, E), F32)]
    *sent, spread, picked = call(
        product_kernel, MESSAGE + (WIDE, WIDE), place, *got, selector, matrix, local, scratch=scratch
    )

    def own0():
        return call(
            own_kernel, (ROW, FACES), spread, face_map, padded, *diagonal, picked, scratch=[OWN_SELECTOR], scalars=0
        )

    got, (sums0, own) = exchange(*sent, own0)
    image, *sent = call(combine_kernel, (FACES,) + MESSAGE, place, own, *got, share, scratch=[GHOSTS])

    def local1():
        return call(local_kernel, (WIDE, ROW), image, face_map, *diagonal, scratch=[OWN_SELECTOR], scalars=0)

    got, (local, sums1) = exchange(*sent, local1)
    row, *sent, spread = call(
        product_kernel,
        (jax.ShapeDtypeStruct((count, 1, GH), F32),) + MESSAGE + (WIDE,),
        place,
        *got,
        selector,
        matrix,
        local,
        sums0,
        sums1,
        scratch=[WIDE] + scratch,
    )
    row = lax.all_to_all(row, DOM, 0, 0)

    def own1():
        return call(own_kernel, FACES, spread, face_map, image, *diagonal, scratch=[OWN_SELECTOR], scalars=0)

    got, own = exchange(*sent, own1)
    out = jax.ShapeDtypeStruct((TR, F), F32)
    return call(final_kernel, (out, out), place, own, *got, share, padded, image, row, scratch=[GHOSTS])


def solution(mesh):
    line = P(DOM)
    in_specs = (
        P(None, DOM),
        P(None, None, DOM),
        P(None, DOM),
        P(DOM, None, None),
        P(DOM, None),
        line,
        line,
        line,
    )
    out_specs = (P(None, DOM), P(None, DOM))
    return jax.shard_map(shards, mesh=mesh, in_specs=in_specs, out_specs=out_specs, check_vma=False)
```

time: 204 us -> 68.2 us (0.33)
  blocking collectives: 98.1 us -> 0 us
  other arithmetic: 21.3 us -> 0.11 us
  matrix products: 20.2 us -> 0 us
  Pallas kernels: 0 us -> 16.7 us
  starting transfers between devices: 47.3 us -> 36.9 us
  waiting for transfers between devices: 2.25 us -> 12.1 us
  between operations: 7.17 us -> 0.81 us
  local copies, waits for them, and re-layouts: 6.39 us -> 1.37 us
    psum x8 -> x0, blocking collectives: 98.1 us -> none  [by_axis(): return functools.reduce(lax.psum, axes, value)]
    dot_general x4 -> x0, matrix products: 20.2 us -> none  [the longest x2 11.2 us: operate(): lax.dot_general(spread, selector, (((1,), (1,)), ((), ())), precision=lax...]
    pallas_call x0 -> x9, Pallas kernels: none -> 16.7 us  [call(): pl.pallas_call(kernel, in_specs=[pl.BlockSpec(memory_space=m) for m in sp...]
    ppermute x16 -> x12, starting transfers between devices: 47.3 us -> 32.9 us  [the longest x8 27.1 us: swap(): lax.ppermute(value, DOM, [(2 * c + b, 2 * partner[c] + b) for c in chips...]
    reduce_sum x5 -> x0, other arithmetic: 10.1 us -> none  [the longest x2 8.08 us: operate(): jnp.sum(element_matrix.astype(jnp.float32) * picked[None, :, :], axis=1)]
    scatter-add x2 -> x0, other arithmetic: 7.41 us -> none  [operate(): summed[:, :own_faces].at[:, send_rows].add(returned.transpose(1, 0, 2))]
    all_to_all x0 -> x1, waiting for transfers between devices: none -> 6.12 us  [shards(): row = lax.all_to_all(row, DOM, 0, 0)]
    all_to_all x0 -> x1, starting transfers between devices: none -> 4.01 us  [shards(): row = lax.all_to_all(row, DOM, 0, 0)]
  transfers between devices with their start and end apart: 16 -> 13, of which waited for: 3 -> 7; matrix products, arithmetic and copies ran while one was open for 2% -> 0% of each run, Pallas kernels for 0% -> 9%
where the time goes in v2:
time: 68.2 us; the launch traced here: 67.9 us
  starting transfers between devices  36.9 us (54%)
  Pallas kernels  16.7 us (24%)
  waiting for transfers between devices  12.1 us (18%)
  local copies, waits for them, and re-layouts  1.37 us (2%)
  between operations  0.81 us (1%)
    ppermute x8, starting transfers between devices, swap(): lax.ppermute(value, DOM, [(2 * c + b, 2 * partner[c] + b) for c in chips...  27.1 us
    pallas_call x9, Pallas kernels, call(): pl.pallas_call(kernel, in_specs=[pl.BlockSpec(memory_space=m) for m in sp...  16.7 us
    all_to_all x1, waiting for transfers between devices, shards(): row = lax.all_to_all(row, DOM, 0, 0)  6.12 us
    ppermute x4, starting transfers between devices, exchange(): got_mid = lax.ppermute(pair, DOM, [(i, i ^ 1) for i in range(count)])  5.74 us
    all_to_all x1, starting transfers between devices, shards(): row = lax.all_to_all(row, DOM, 0, 0)  4.01 us
    ppermute x4, waiting for transfers between devices, exchange(): got_mid = lax.ppermute(pair, DOM, [(i, i ^ 1) for i in range(count)])  3.4 us
    ppermute x8, waiting for transfers between devices, swap(): lax.ppermute(value, DOM, [(2 * c + b, 2 * partner[c] + b) for c in chips...  2.56 us
    unnamed x12, local copies, waits for them, and re-layouts  1.37 us
  transfers between devices with their start and end apart: 13, of which 7 were waited for; matrix products, arithmetic and copies ran while one was open for 0% of the time, Pallas kernels for 9%

profile of v2, /device:TPU:1, one launch (start us, length us, event | category | flops | bytes accessed | tf_op | source)
XLA Modules:
  0.0 67.9 jit_solution(5876347695160203256)
XLA Ops:
  1.4 1.4 %shard_map.95 = (f32[2,24,128]{2,1,0:T(8,128)S(1)}, f32[2,24,128]{2,1,0:T(8,128)S(1)}, f32[24,128]{1,0:T(8,128)S(1)}, bf16[1024,512]{1,0:T(8,128)(2,1)S(1)}, f32[24,1024]{1,0:T(8,128)S(1)}) custom-call(s32[2]{0:T(128)S(1)} %pad_add_fusion.place_ref, s32[1,4]{1,0:T(1,128)S(1)} %copy-done.5, f32[18,1024]{1,0:T(8,128)} %field_ref.1, s32[4,128]{1,0:T(4,128)} %bitcast.23), custom_call_target="tpu_custom_call" | custom-call | tf_op jit(solution)/shard_map/pallas_call | solution.py:206
  2.8 2.1 %collective-permute-start = (f32[2,24,128]{2,1,0:T(8,128)S(1)}, f32[2,24,128]{2,1,0:T(8,128)S(1)}, u32[]{:S(2)}, u32[]{:S(2)}) collective-permute-start(f32[2,24,128]{2,1,0:T(8,128)S(1)} %get-tuple-element.44), channel_id=1, source_target_pairs={{0,2},{1,3},{2,0},{3,1},{4,6},{5,7},{6,4},{7,5},{8,10},{9,11},{10,... | collective-permute-start | bytes 73736 | tf_op jit(solution)/shard_map/ppermute | solution.py:228
  4.9 7.7 %collective-permute-start.1 = (f32[2,24,128]{2,1,0:T(8,128)S(1)}, f32[2,24,128]{2,1,0:T(8,128)S(1)}, u32[]{:S(2)}, u32[]{:S(2)}) collective-permute-start(f32[2,24,128]{2,1,0:T(8,128)S(1)} %get-tuple-element.45), channel_id=1, source_target_pairs={{0,126},{1,127},{2,4},{3,5},{4,2},{5,3},{6,8},{7,9},{8,6},{9,7},{1... | collective-permute-start | bytes 73736 | tf_op jit(solution)/shard_map/ppermute | solution.py:228
  13.3 2.6 %shard_map.96 = (bf16[512,2048]{1,0:T(8,128)(2,1)S(1)}, f32[24,2048]{1,0:T(8,128)S(1)}, bf16[72,72,512]{2,1,0:T(8,128)(2,1)S(1)}) custom-call(s32[4,512]{1,0:T(4,128)S(1)} %copy-done, f32[24,1024]{1,0:T(8,128)S(1)} %get-tuple-element.46.field_ref, bf16[72,72,512]{2,1,0:T(8,128)(2,1)} %matrix_ref.1), custom_call_target="tpu_custom_call" | custom-call | tf_op jit(solution)/shard_map/pallas_call | solution.py:206
  15.9 1.3 %collective-permute-start.2 = (f32[2,24,128]{2,1,0:T(8,128)S(1)}, f32[2,24,128]{2,1,0:T(8,128)S(1)}, u32[]{:S(2)}, u32[]{:S(2)}) collective-permute-start(f32[2,24,128]{2,1,0:T(8,128)S(1)} %pad_maximum_fusion), channel_id=1, source_target_pairs={{0,1},{1,0},{2,3},{3,2},{4,5},{5,4},{6,7},{7,6},{8,9},{9,8},{10,11... | collective-permute-start | bytes 73736 | tf_op jit(solution)/shard_map/ppermute | solution.py:236
  18.1 2.8 %shard_map.97 = (f32[2,24,128]{2,1,0:T(8,128)S(1)}, f32[2,24,128]{2,1,0:T(8,128)S(1)}, f32[24,128]{1,0:T(8,128)S(1)}, f32[24,2048]{1,0:T(8,128)S(1)}, f32[24,2048]{1,0:T(8,128)S(1)}) custom-call(s32[2]{0:T(128)S(1)} %pad_add_fusion.place_ref, f32[2,24,128]{2,1,0:T(8,128)S(1)} %collective-permute-done.near_ref, ...), custom_call_target="tpu_custom_call" | custom-call | tf_op jit(solution)/shard_map/pallas_call | solution.py:206
  21.1 5.7 %collective-permute-start.4 = (f32[2,24,128]{2,1,0:T(8,128)S(1)}, f32[2,24,128]{2,1,0:T(8,128)S(1)}, u32[]{:S(2)}, u32[]{:S(2)}) collective-permute-start(f32[2,24,128]{2,1,0:T(8,128)S(1)} %get-tuple-element.57), channel_id=1, source_target_pairs={{0,126},{1,127},{2,4},{3,5},{4,2},{5,3},{6,8},{7,9},{8,6},{9,7},{1... | collective-permute-start | bytes 73736 | tf_op jit(solution)/shard_map/ppermute | solution.py:228
  26.8 1.4 %shard_map.98 = (f32[1,128]{1,0:T(1,128)S(1)}, f32[24,1024]{1,0:T(8,128)S(1)}) custom-call(f32[24,2048]{1,0:T(8,128)S(1)} %get-tuple-element.58.spread_ref, s32[4,512]{1,0:T(4,128)S(1)} %copy-done, f32[24,1024]{1,0:T(8,128)S(1)} %get-tuple-element.46.field_ref, f32[1,1024]{1,0:T(1,128)S(1)} %bitcast.10, s32[1,1024]{1,0:T(1,128)S(1)} %bitcast.13, ...), custom_call_target="tpu_custom_call" | custom-call | tf_op jit(solution)/shard_map/pallas_call | solution.py:206
  28.2 1.0 %collective-permute-done.4.far_ref = f32[2,24,128]{2,1,0:T(8,128)S(1)} collective-permute-done((f32[2,24,128]{2,1,0:T(8,128)S(1)}, f32[2,24,128]{2,1,0:T(8,128)S(1)}, u32[]{:S(2)}, u32[]{:S(2)}) %collective-permute-start.4) | collective-permute-done | bytes 24608 | tf_op jit(solution)/shard_map/ppermute | solution.py:228
  29.3 1.6 %collective-permute-start.5 = (f32[2,24,128]{2,1,0:T(8,128)S(1)}, f32[2,24,128]{2,1,0:T(8,128)S(1)}, u32[]{:S(2)}, u32[]{:S(2)}) collective-permute-start(f32[2,24,128]{2,1,0:T(8,128)S(1)} %pad_maximum_fusion.1), channel_id=1, source_target_pairs={{0,1},{1,0},{2,3},{3,2},{4,5},{5,4},{6,7},{7,6},{8,9},{9,8},{10,11... | collective-permute-start | bytes 73736 | tf_op jit(solution)/shard_map/ppermute | solution.py:236
  30.8 0.8 %collective-permute-done.5.mid_ref = f32[2,24,128]{2,1,0:T(8,128)S(1)} collective-permute-done((f32[2,24,128]{2,1,0:T(8,128)S(1)}, f32[2,24,128]{2,1,0:T(8,128)S(1)}, u32[]{:S(2)}, u32[]{:S(2)}) %collective-permute-start.5) | collective-permute-done | bytes 24608 | tf_op jit(solution)/shard_map/ppermute | solution.py:236
  31.7 1.2 %shard_map.99 = (f32[24,1024]{1,0:T(8,128)S(1)}, f32[2,24,128]{2,1,0:T(8,128)S(1)}, f32[2,24,128]{2,1,0:T(8,128)S(1)}, f32[24,128]{1,0:T(8,128)S(1)}) custom-call(s32[2]{0:T(128)S(1)} %pad_add_fusion.place_ref, f32[24,1024]{1,0:T(8,128)S(1)} %get-tuple-element.62.own_ref, f32[2,24,128]{2,1,0:T(8,128)S(1)} %collective-permute-done.3.near_ref, ...), custom_call_target="tpu_custom_call" | custom-call | tf_op jit(solution)/shard_map/pallas_call | solution.py:206
  32.9 5.7 %collective-permute-start.7 = (f32[2,24,128]{2,1,0:T(8,128)S(1)}, f32[2,24,128]{2,1,0:T(8,128)S(1)}, u32[]{:S(2)}, u32[]{:S(2)}) collective-permute-start(f32[2,24,128]{2,1,0:T(8,128)S(1)} %get-tuple-element.68), channel_id=1, source_target_pairs={{0,126},{1,127},{2,4},{3,5},{4,2},{5,3},{6,8},{7,9},{8,6},{9,7},{1... | collective-permute-start | bytes 73736 | tf_op jit(solution)/shard_map/ppermute | solution.py:228
  38.7 0.9 %shard_map.100 = (f32[24,2048]{1,0:T(8,128)S(1)}, f32[1,128]{1,0:T(1,128)S(1)}) custom-call(f32[24,1024]{1,0:T(8,128)S(1)} %get-tuple-element.69.image_ref.field_ref, s32[4,512]{1,0:T(4,128)S(1)} %copy-done.1, f32[1,1024]{1,0:T(1,128)S(1)} %bitcast.11, s32[1,1024]{1,0:T(1,128)S(1)} %bitcast.14, f32[1,1024]{1,0:T(1,128)S(1)} %bitcast.17), custom_call_target="tpu_custom_call" | custom-call | tf_op jit(solution)/shard_map/pallas_call | solution.py:206
  39.6 1.5 %collective-permute-done.7.far_ref = f32[2,24,128]{2,1,0:T(8,128)S(1)} collective-permute-done((f32[2,24,128]{2,1,0:T(8,128)S(1)}, f32[2,24,128]{2,1,0:T(8,128)S(1)}, u32[]{:S(2)}, u32[]{:S(2)}) %collective-permute-start.7) | collective-permute-done | bytes 24608 | tf_op jit(solution)/shard_map/ppermute | solution.py:228
  41.1 1.6 %collective-permute-start.8 = (f32[2,24,128]{2,1,0:T(8,128)S(1)}, f32[2,24,128]{2,1,0:T(8,128)S(1)}, u32[]{:S(2)}, u32[]{:S(2)}) collective-permute-start(f32[2,24,128]{2,1,0:T(8,128)S(1)} %pad_maximum_fusion.2), channel_id=1, source_target_pairs={{0,1},{1,0},{2,3},{3,2},{4,5},{5,4},{6,7},{7,6},{8,9},{9,8},{10,11... | collective-permute-start | bytes 73736 | tf_op jit(solution)/shard_map/ppermute | solution.py:236
  42.7 0.8 %collective-permute-done.8.mid_ref = f32[2,24,128]{2,1,0:T(8,128)S(1)} collective-permute-done((f32[2,24,128]{2,1,0:T(8,128)S(1)}, f32[2,24,128]{2,1,0:T(8,128)S(1)}, u32[]{:S(2)}, u32[]{:S(2)}) %collective-permute-start.8) | collective-permute-done | bytes 24608 | tf_op jit(solution)/shard_map/ppermute | solution.py:236
  43.6 3.4 %shard_map.101 = (f32[128,1,128]{2,1,0:T(1,128)}, f32[2,24,128]{2,1,0:T(8,128)S(1)}, f32[2,24,128]{2,1,0:T(8,128)S(1)}, f32[24,128]{1,0:T(8,128)S(1)}, f32[24,2048]{1,0:T(8,128)S(1)}) custom-call(s32[2]{0:T(128)S(1)} %pad_add_fusion.place_ref, f32[2,24,128]{2,1,0:T(8,128)S(1)} %collective-permute-done.6.near_ref, ...), custom_call_target="tpu_custom_call" | custom-call | tf_op jit(solution)/shard_map/pallas_call | solution.py:206
  46.9 5.7 %collective-permute-start.10 = (f32[2,24,128]{2,1,0:T(8,128)S(1)}, f32[2,24,128]{2,1,0:T(8,128)S(1)}, u32[]{:S(2)}, u32[]{:S(2)}) collective-permute-start(f32[2,24,128]{2,1,0:T(8,128)S(1)} %get-tuple-element.79), channel_id=1, source_target_pairs={{0,126},{1,127},{2,4},{3,5},{4,2},{5,3},{6,8},{7,9},{8,6},{9,7},{1... | collective-permute-start | bytes 73736 | tf_op jit(solution)/shard_map/ppermute | solution.py:228
  52.6 4.0 %all-to-all-start = ((f32[128,1,128]{2,1,0:T(1,128)}), f32[128,1,128]{2,1,0:T(1,128)S(1)}, u32[]{:S(2)}, u32[]{:S(2)}) async-start(f32[128,1,128]{2,1,0:T(1,128)} %get-tuple-element.85), calls=%async_computation | async-start | bytes 131072 | tf_op jit(solution)/shard_map/all_to_all | solution.py:292
  56.6 1.4 %shard_map.102.own_ref = f32[24,1024]{1,0:T(8,128)S(1)} custom-call(f32[24,2048]{1,0:T(8,128)S(1)} %get-tuple-element.80.spread_ref, s32[4,512]{1,0:T(4,128)S(1)} %copy-done.1, f32[24,1024]{1,0:T(8,128)S(1)} %get-tuple-element.69.image_ref.field_ref, f32[1,1024]{1,0:T(1,128)S(1)} %bitcast.12, s32[1,1024]{1,0:T(1,128)S(1)} %bitcast.15, f32[1,1024]{1,0:T(1,128)S(1)} %bitcast.18), custom_call_target="tpu_custom_call" | custom-call | tf_op jit(solution)/shard_map/pallas_call | solution.py:206
  58.1 1.3 %collective-permute-start.11 = (f32[2,24,128]{2,1,0:T(8,128)S(1)}, f32[2,24,128]{2,1,0:T(8,128)S(1)}, u32[]{:S(2)}, u32[]{:S(2)}) collective-permute-start(f32[2,24,128]{2,1,0:T(8,128)S(1)} %pad_maximum_fusion.3), channel_id=1, source_target_pairs={{0,1},{1,0},{2,3},{3,2},{4,5},{5,4},{6,7},{7,6},{8,9},{9,8},{10,11... | collective-permute-start | bytes 73736 | tf_op jit(solution)/shard_map/ppermute | solution.py:236
  60.2 6.1 %all-to-all-done.sums_ref = f32[128,1,128]{2,1,0:T(1,128)S(1)} async-done(((f32[128,1,128]{2,1,0:T(1,128)}), f32[128,1,128]{2,1,0:T(1,128)S(1)}, u32[]{:S(2)}, u32[]{:S(2)}) %all-to-all-start) | async-done | bytes 65568 | tf_op jit(solution)/shard_map/all_to_all | solution.py:292
  66.3 1.6 %shard_map.103 = (f32[18,1024]{1,0:T(8,128)}, f32[18,1024]{1,0:T(8,128)}) custom-call(s32[2]{0:T(128)S(1)} %pad_add_fusion.place_ref, f32[24,1024]{1,0:T(8,128)S(1)} %shard_map.102.own_ref, f32[2,24,128]{2,1,0:T(8,128)S(1)} %collective-permute-done.9.near_ref, f32[2,24,128]{2,1,0:T(8,128)S(1)} %collective-permute-done.10.far_ref, ...), custom_call_target="tpu_custom_call" | custom-call | tf_op jit(solution)/shard_map/pallas_call | solution.py:206
  (32 shorter events, 3.4 us)
Async XLA Ops:
  0.7 0.7 copy-start.5
  2.8 13.1 %collective-permute-start = (f32[2,24,128]{2,1,0:T(8,128)S(1)}, f32[2,24,128]{2,1,0:T(8,128)S(1)}, u32[]{:S(2)}, u32[]{:S(2)}) collective-permute-start(f32[2,24,128]{2,1,0:T(8,128)S(1)} %get-tuple-element.44), channel_id=1, source_target_pairs={{0,2},{1,3},{2,0},{3,1},{4,6},{5,7},{6,4},{7,5},{8,10},{9,11},{10,... | collective-permute-start | bytes 73736 | tf_op jit(solution)/shard_map/ppermute | solution.py:228
  4.9 11.0 %collective-permute-start.1 = (f32[2,24,128]{2,1,0:T(8,128)S(1)}, f32[2,24,128]{2,1,0:T(8,128)S(1)}, u32[]{:S(2)}, u32[]{:S(2)}) collective-permute-start(f32[2,24,128]{2,1,0:T(8,128)S(1)} %get-tuple-element.45), channel_id=1, source_target_pairs={{0,126},{1,127},{2,4},{3,5},{4,2},{5,3},{6,8},{7,9},{8,6},{9,7},{1... | collective-permute-start | bytes 73736 | tf_op jit(solution)/shard_map/ppermute | solution.py:228
  12.6 0.7 %copy-start = (s32[4,512]{1,0:T(4,128)S(1)}, s32[4,512]{1,0:T(4,128)}, u32[]{:S(2)}) copy-start(s32[4,512]{1,0:T(4,128)} %map_ref.7) | copy-start | bytes 24580
  13.3 13.5 %copy-start.2 = (f32[1024]{0:T(1024)S(1)}, f32[1024]{0:T(1024)}, u32[]{:S(2)}) copy-start(f32[1024]{0:T(1024)} %param.13) | copy-start | bytes 12292
  13.3 13.5 %copy-start.3 = (s32[1024]{0:T(1024)S(1)}, s32[1024]{0:T(1024)}, u32[]{:S(2)}) copy-start(s32[1024]{0:T(1024)} %param.14) | copy-start | bytes 12292
  13.3 13.5 %copy-start.4 = (f32[1024]{0:T(1024)S(1)}, f32[1024]{0:T(1024)}, u32[]{:S(2)}) copy-start(f32[1024]{0:T(1024)} %param.15) | copy-start | bytes 12292
  15.9 22.8 %copy-start.1 = (s32[4,512]{1,0:T(4,128)S(1)}, s32[4,512]{1,0:T(4,128)}, u32[]{:S(2)}) copy-start(s32[4,512]{1,0:T(4,128)} %map_ref.7) | copy-start | bytes 24580
  15.9 2.2 %collective-permute-start.2 = (f32[2,24,128]{2,1,0:T(8,128)S(1)}, f32[2,24,128]{2,1,0:T(8,128)S(1)}, u32[]{:S(2)}, u32[]{:S(2)}) collective-permute-start(f32[2,24,128]{2,1,0:T(8,128)S(1)} %pad_maximum_fusion), channel_id=1, source_target_pairs={{0,1},{1,0},{2,3},{3,2},{4,5},{5,4},{6,7},{7,6},{8,9},{9,8},{10,11... | collective-permute-start | bytes 73736 | tf_op jit(solution)/shard_map/ppermute | solution.py:236
  21.0 7.3 %collective-permute-start.3 = (f32[2,24,128]{2,1,0:T(8,128)S(1)}, f32[2,24,128]{2,1,0:T(8,128)S(1)}, u32[]{:S(2)}, u32[]{:S(2)}) collective-permute-start(f32[2,24,128]{2,1,0:T(8,128)S(1)} %get-tuple-element.56), channel_id=1, source_target_pairs={{0,2},{1,3},{2,0},{3,1},{4,6},{5,7},{6,4},{7,5},{8,10},{9,11},{10,... | collective-permute-start | bytes 73736 | tf_op jit(solution)/shard_map/ppermute | solution.py:228
  21.1 8.2 %collective-permute-start.4 = (f32[2,24,128]{2,1,0:T(8,128)S(1)}, f32[2,24,128]{2,1,0:T(8,128)S(1)}, u32[]{:S(2)}, u32[]{:S(2)}) collective-permute-start(f32[2,24,128]{2,1,0:T(8,128)S(1)} %get-tuple-element.57), channel_id=1, source_target_pairs={{0,126},{1,127},{2,4},{3,5},{4,2},{5,3},{6,8},{7,9},{8,6},{9,7},{1... | collective-permute-start | bytes 73736 | tf_op jit(solution)/shard_map/ppermute | solution.py:228
  29.3 2.4 %collective-permute-start.5 = (f32[2,24,128]{2,1,0:T(8,128)S(1)}, f32[2,24,128]{2,1,0:T(8,128)S(1)}, u32[]{:S(2)}, u32[]{:S(2)}) collective-permute-start(f32[2,24,128]{2,1,0:T(8,128)S(1)} %pad_maximum_fusion.1), channel_id=1, source_target_pairs={{0,1},{1,0},{2,3},{3,2},{4,5},{5,4},{6,7},{7,6},{8,9},{9,8},{10,11... | collective-permute-start | bytes 73736 | tf_op jit(solution)/shard_map/ppermute | solution.py:236
  32.9 6.7 %collective-permute-start.6 = (f32[2,24,128]{2,1,0:T(8,128)S(1)}, f32[2,24,128]{2,1,0:T(8,128)S(1)}, u32[]{:S(2)}, u32[]{:S(2)}) collective-permute-start(f32[2,24,128]{2,1,0:T(8,128)S(1)} %get-tuple-element.67), channel_id=1, source_target_pairs={{0,2},{1,3},{2,0},{3,1},{4,6},{5,7},{6,4},{7,5},{8,10},{9,11},{10,... | collective-permute-start | bytes 73736 | tf_op jit(solution)/shard_map/ppermute | solution.py:228
  32.9 8.2 %collective-permute-start.7 = (f32[2,24,128]{2,1,0:T(8,128)S(1)}, f32[2,24,128]{2,1,0:T(8,128)S(1)}, u32[]{:S(2)}, u32[]{:S(2)}) collective-permute-start(f32[2,24,128]{2,1,0:T(8,128)S(1)} %get-tuple-element.68), channel_id=1, source_target_pairs={{0,126},{1,127},{2,4},{3,5},{4,2},{5,3},{6,8},{7,9},{8,6},{9,7},{1... | collective-permute-start | bytes 73736 | tf_op jit(solution)/shard_map/ppermute | solution.py:228
  41.1 2.4 %collective-permute-start.8 = (f32[2,24,128]{2,1,0:T(8,128)S(1)}, f32[2,24,128]{2,1,0:T(8,128)S(1)}, u32[]{:S(2)}, u32[]{:S(2)}) collective-permute-start(f32[2,24,128]{2,1,0:T(8,128)S(1)} %pad_maximum_fusion.2), channel_id=1, source_target_pairs={{0,1},{1,0},{2,3},{3,2},{4,5},{5,4},{6,7},{7,6},{8,9},{9,8},{10,11... | collective-permute-start | bytes 73736 | tf_op jit(solution)/shard_map/ppermute | solution.py:236
  46.9 11.1 %collective-permute-start.9 = (f32[2,24,128]{2,1,0:T(8,128)S(1)}, f32[2,24,128]{2,1,0:T(8,128)S(1)}, u32[]{:S(2)}, u32[]{:S(2)}) collective-permute-start(f32[2,24,128]{2,1,0:T(8,128)S(1)} %get-tuple-element.78), channel_id=1, source_target_pairs={{0,2},{1,3},{2,0},{3,1},{4,6},{5,7},{6,4},{7,5},{8,10},{9,11},{10,... | collective-permute-start | bytes 73736 | tf_op jit(solution)/shard_map/ppermute | solution.py:228
  46.9 11.1 %collective-permute-start.10 = (f32[2,24,128]{2,1,0:T(8,128)S(1)}, f32[2,24,128]{2,1,0:T(8,128)S(1)}, u32[]{:S(2)}, u32[]{:S(2)}) collective-permute-start(f32[2,24,128]{2,1,0:T(8,128)S(1)} %get-tuple-element.79), channel_id=1, source_target_pairs={{0,126},{1,127},{2,4},{3,5},{4,2},{5,3},{6,8},{7,9},{8,6},{9,7},{1... | collective-permute-start | bytes 73736 | tf_op jit(solution)/shard_map/ppermute | solution.py:228
  52.6 13.7 %all-to-all-start = ((f32[128,1,128]{2,1,0:T(1,128)}), f32[128,1,128]{2,1,0:T(1,128)S(1)}, u32[]{:S(2)}, u32[]{:S(2)}) async-start(f32[128,1,128]{2,1,0:T(1,128)} %get-tuple-element.85), calls=%async_computation | async-start | bytes 131072 | tf_op jit(solution)/shard_map/all_to_all | solution.py:292
  58.1 2.1 %collective-permute-start.11 = (f32[2,24,128]{2,1,0:T(8,128)S(1)}, f32[2,24,128]{2,1,0:T(8,128)S(1)}, u32[]{:S(2)}, u32[]{:S(2)}) collective-permute-start(f32[2,24,128]{2,1,0:T(8,128)S(1)} %pad_maximum_fusion.3), channel_id=1, source_target_pairs={{0,1},{1,0},{2,3},{3,2},{4,5},{5,4},{6,7},{7,6},{8,9},{9,8},{10,11... | collective-permute-start | bytes 73736 | tf_op jit(solution)/shard_map/ppermute | solution.py:236

commit v3 on v2

--- a/solution.py
+++ b/solution.py
@@ -86,7 +86,7 @@
     for k in range(NB):
         rows = lax.broadcasted_iota(jnp.int32, (F, GH), 0)
         lanes = lax.broadcasted_iota(jnp.int32, (1, GH), 1)
-        face = jnp.where(lanes < count_ref[0, k], index_ref[k : k + 1, :], -1)
+        face = jnp.where(lanes < count_ref[:, k : k + 1], index_ref[k : k + 1, :], -1)
         share_ref[:, k * GH : (k + 1) * GH] = jnp.where(rows == face, 1.0, 0.0).astype(BF16)
     padded_ref[TR:, :] = jnp.zeros((TP - TR, F), F32)
     padded_ref[:TR, :] = field_ref[...]
@@ -221,15 +221,19 @@
     core, odd = here & 1, (here >> 1) & 1
     place = jnp.stack([core, odd])
     diagonal = [x.reshape(1, F) for x in (face_mass, absorbing, impedance)]
-    chips = range(count // 2)
-    far_of = [(((c + 1) ^ 1) - 1) % (count // 2) for c in chips]
-
-    def swap(value, partner):
-        return lax.ppermute(value, DOM, [(2 * c + b, 2 * partner[c] + b) for c in chips for b in range(2)])
+    chips = count // 2
+
+    def swap(value, partner_of):
+        pairs = []
+        for i in range(count):
+            c, b = divmod(i, 2)
+            partner = partner_of(c)
+            pairs.append((i, 2 * partner + b if 0 <= partner < chips else i ^ 1))
+        return lax.ppermute(value, DOM, pairs)
 
     def exchange(near, far, mid, beside):
-        got_far = swap(far, far_of)
-        got_near = swap(near, [c ^ 1 for c in chips])
+        got_far = swap(far, lambda c: ((c + 1) ^ 1) - 1)
+        got_near = swap(near, lambda c: c ^ 1)
         got_near, got_far, beside = lax.optimization_barrier((got_near, got_far, beside()))
         onward = jnp.where(core == odd, got_near[1], got_far[1])
         pair = jnp.stack([mid, onward])
@@ -243,7 +247,6 @@
         share_count,
         right_side,
         share_index[0],
-        scalars=2,
         held=pltpu.HBM,
     )
 

time: 68.2 us -> 63 us (0.924)
  starting transfers between devices: 36.9 us -> 34.5 us
  waiting for transfers between devices: 12.1 us -> 9.88 us
    all_to_all x1, starting transfers between devices: 4.01 us -> 17.6 us  [shards(): row = lax.all_to_all(row, DOM, 0, 0)]
    ppermute x8, starting transfers between devices: 27.1 us -> 14.2 us  [swap(): return lax.ppermute(value, DOM, pairs)]
    ppermute x4, starting transfers between devices: 5.74 us -> 2.6 us  [exchange(): got_mid = lax.ppermute(pair, DOM, [(i, i ^ 1) for i in range(count)])]
    ppermute x8, waiting for transfers between devices: 2.56 us -> 0.03 us  [swap(): return lax.ppermute(value, DOM, pairs)]
    unnamed x12 -> x10, local copies, waits for them, and re-layouts: 1.37 us -> 0.71 us
  transfers between devices with their start and end apart: 13 -> 13, of which waited for: 7 -> 5; matrix products, arithmetic and copies ran while one was open for 0% -> 0% of each run, Pallas kernels for 9% -> 10%
where the time goes in v3:
time: 63 us; the launch traced here: 62.7 us
  starting transfers between devices  34.5 us (55%)
  Pallas kernels  16.7 us (27%)
  waiting for transfers between devices  9.88 us (16%)
  between operations  0.85 us (1%)
  local copies, waits for them, and re-layouts  0.71 us (1%)
    all_to_all x1, starting transfers between devices, shards(): row = lax.all_to_all(row, DOM, 0, 0)  17.6 us
    pallas_call x9, Pallas kernels, call(): pl.pallas_call(kernel, in_specs=[pl.BlockSpec(memory_space=m) for m in sp...  16.7 us
    ppermute x8, starting transfers between devices, swap(): return lax.ppermute(value, DOM, pairs)  14.2 us
    all_to_all x1, waiting for transfers between devices, shards(): row = lax.all_to_all(row, DOM, 0, 0)  6.12 us
    ppermute x4, waiting for transfers between devices, exchange(): got_mid = lax.ppermute(pair, DOM, [(i, i ^ 1) for i in range(count)])  3.73 us
    ppermute x4, starting transfers between devices, exchange(): got_mid = lax.ppermute(pair, DOM, [(i, i ^ 1) for i in range(count)])  2.6 us
  transfers between devices with their start and end apart: 13, of which 5 were waited for; matrix products, arithmetic and copies ran while one was open for 0% of the time, Pallas kernels for 10%

profile of v3, /device:TPU:1, one launch (start us, length us, event | category | flops | bytes accessed | tf_op | source)
XLA Modules:
  0.0 62.7 jit_solution(12671464213300770740)
XLA Ops:
  0.7 1.4 %shard_map.95 = (f32[2,24,128]{2,1,0:T(8,128)S(1)}, f32[2,24,128]{2,1,0:T(8,128)S(1)}, f32[24,128]{1,0:T(8,128)S(1)}, bf16[1024,512]{1,0:T(8,128)(2,1)S(1)}, f32[24,1024]{1,0:T(8,128)S(1)}) custom-call(s32[2]{0:T(128)S(1)} %pad_add_fusion.place_ref, s32[1,4]{1,0:T(1,128)} %count_ref.1, f32[18,1024]{1,0:T(8,128)} %field_ref.1, s32[4,128]{1,0:T(4,128)} %bitcast.23), custom_call_target="tpu_custom_call" | custom-call | tf_op jit(solution)/shard_map/pallas_call | solution.py:206
  2.2 2.1 %collective-permute-start = (f32[2,24,128]{2,1,0:T(8,128)S(1)}, f32[2,24,128]{2,1,0:T(8,128)S(1)}, u32[]{:S(2)}, u32[]{:S(2)}) collective-permute-start(f32[2,24,128]{2,1,0:T(8,128)S(1)} %get-tuple-element.44), channel_id=1, source_target_pairs={{0,2},{1,3},{2,0},{3,1},{4,6},{5,7},{6,4},{7,5},{8,10},{9,11},{10,... | collective-permute-start | bytes 73736 | tf_op jit(solution)/shard_map/ppermute | solution.py:232
  4.3 1.0 %collective-permute-start.1 = (f32[2,24,128]{2,1,0:T(8,128)S(1)}, f32[2,24,128]{2,1,0:T(8,128)S(1)}, u32[]{:S(2)}, u32[]{:S(2)}) collective-permute-start(f32[2,24,128]{2,1,0:T(8,128)S(1)} %get-tuple-element.45), channel_id=1, source_target_pairs={{0,1},{1,0},{2,4},{3,5},{4,2},{5,3},{6,8},{7,9},{8,6},{9,7},{10,12... | collective-permute-start | bytes 73736 | tf_op jit(solution)/shard_map/ppermute | solution.py:232
  5.2 0.7 %copy-done = s32[4,512]{1,0:T(4,128)S(1)} copy-done((s32[4,512]{1,0:T(4,128)S(1)}, s32[4,512]{1,0:T(4,128)}, u32[]{:S(2)}) %copy-start) | copy-done | bytes 8216
  5.9 2.6 %shard_map.96 = (bf16[512,2048]{1,0:T(8,128)(2,1)S(1)}, f32[24,2048]{1,0:T(8,128)S(1)}, bf16[72,72,512]{2,1,0:T(8,128)(2,1)S(1)}) custom-call(s32[4,512]{1,0:T(4,128)S(1)} %copy-done, f32[24,1024]{1,0:T(8,128)S(1)} %get-tuple-element.46.field_ref, bf16[72,72,512]{2,1,0:T(8,128)(2,1)} %matrix_ref.1), custom_call_target="tpu_custom_call" | custom-call | tf_op jit(solution)/shard_map/pallas_call | solution.py:206
  8.6 1.2 %collective-permute-done.2.mid_ref = f32[2,24,128]{2,1,0:T(8,128)S(1)} collective-permute-done((f32[2,24,128]{2,1,0:T(8,128)S(1)}, f32[2,24,128]{2,1,0:T(8,128)S(1)}, u32[]{:S(2)}, u32[]{:S(2)}) %collective-permute-start.2) | collective-permute-done | bytes 24608 | tf_op jit(solution)/shard_map/ppermute | solution.py:240
  9.8 2.9 %shard_map.97 = (f32[2,24,128]{2,1,0:T(8,128)S(1)}, f32[2,24,128]{2,1,0:T(8,128)S(1)}, f32[24,128]{1,0:T(8,128)S(1)}, f32[24,2048]{1,0:T(8,128)S(1)}, f32[24,2048]{1,0:T(8,128)S(1)}) custom-call(s32[2]{0:T(128)S(1)} %pad_add_fusion.place_ref, f32[2,24,128]{2,1,0:T(8,128)S(1)} %collective-permute-done.near_ref, ...), custom_call_target="tpu_custom_call" | custom-call | tf_op jit(solution)/shard_map/pallas_call | solution.py:206
  12.7 2.1 %collective-permute-start.3 = (f32[2,24,128]{2,1,0:T(8,128)S(1)}, f32[2,24,128]{2,1,0:T(8,128)S(1)}, u32[]{:S(2)}, u32[]{:S(2)}) collective-permute-start(f32[2,24,128]{2,1,0:T(8,128)S(1)} %get-tuple-element.56), channel_id=1, source_target_pairs={{0,2},{1,3},{2,0},{3,1},{4,6},{5,7},{6,4},{7,5},{8,10},{9,11},{10,... | collective-permute-start | bytes 73736 | tf_op jit(solution)/shard_map/ppermute | solution.py:232
  15.5 1.4 %shard_map.98 = (f32[1,128]{1,0:T(1,128)S(1)}, f32[24,1024]{1,0:T(8,128)S(1)}) custom-call(f32[24,2048]{1,0:T(8,128)S(1)} %get-tuple-element.58.spread_ref, s32[4,512]{1,0:T(4,128)S(1)} %copy-done, f32[24,1024]{1,0:T(8,128)S(1)} %get-tuple-element.46.field_ref, f32[1,1024]{1,0:T(1,128)S(1)} %bitcast.10, s32[1,1024]{1,0:T(1,128)S(1)} %bitcast.13, ...), custom_call_target="tpu_custom_call" | custom-call | tf_op jit(solution)/shard_map/pallas_call | solution.py:206
  17.4 0.9 %collective-permute-done.5.mid_ref = f32[2,24,128]{2,1,0:T(8,128)S(1)} collective-permute-done((f32[2,24,128]{2,1,0:T(8,128)S(1)}, f32[2,24,128]{2,1,0:T(8,128)S(1)}, u32[]{:S(2)}, u32[]{:S(2)}) %collective-permute-start.5) | collective-permute-done | bytes 24608 | tf_op jit(solution)/shard_map/ppermute | solution.py:240
  18.2 1.2 %shard_map.99 = (f32[24,1024]{1,0:T(8,128)S(1)}, f32[2,24,128]{2,1,0:T(8,128)S(1)}, f32[2,24,128]{2,1,0:T(8,128)S(1)}, f32[24,128]{1,0:T(8,128)S(1)}) custom-call(s32[2]{0:T(128)S(1)} %pad_add_fusion.place_ref, f32[24,1024]{1,0:T(8,128)S(1)} %get-tuple-element.62.own_ref, f32[2,24,128]{2,1,0:T(8,128)S(1)} %collective-permute-done.3.near_ref, ...), custom_call_target="tpu_custom_call" | custom-call | tf_op jit(solution)/shard_map/pallas_call | solution.py:206
  19.4 3.2 %collective-permute-start.6 = (f32[2,24,128]{2,1,0:T(8,128)S(1)}, f32[2,24,128]{2,1,0:T(8,128)S(1)}, u32[]{:S(2)}, u32[]{:S(2)}) collective-permute-start(f32[2,24,128]{2,1,0:T(8,128)S(1)} %get-tuple-element.67), channel_id=1, source_target_pairs={{0,2},{1,3},{2,0},{3,1},{4,6},{5,7},{6,4},{7,5},{8,10},{9,11},{10,... | collective-permute-start | bytes 73736 | tf_op jit(solution)/shard_map/ppermute | solution.py:232
  23.2 0.9 %shard_map.100 = (f32[24,2048]{1,0:T(8,128)S(1)}, f32[1,128]{1,0:T(1,128)S(1)}) custom-call(f32[24,1024]{1,0:T(8,128)S(1)} %get-tuple-element.69.image_ref.field_ref, s32[4,512]{1,0:T(4,128)S(1)} %copy-done.1, f32[1,1024]{1,0:T(1,128)S(1)} %bitcast.11, s32[1,1024]{1,0:T(1,128)S(1)} %bitcast.14, f32[1,1024]{1,0:T(1,128)S(1)} %bitcast.17), custom_call_target="tpu_custom_call" | custom-call | tf_op jit(solution)/shard_map/pallas_call | solution.py:206
  24.2 0.9 %collective-permute-start.8 = (f32[2,24,128]{2,1,0:T(8,128)S(1)}, f32[2,24,128]{2,1,0:T(8,128)S(1)}, u32[]{:S(2)}, u32[]{:S(2)}) collective-permute-start(f32[2,24,128]{2,1,0:T(8,128)S(1)} %pad_maximum_fusion.2), channel_id=1, source_target_pairs={{0,1},{1,0},{2,3},{3,2},{4,5},{5,4},{6,7},{7,6},{8,9},{9,8},{10,11... | collective-permute-start | bytes 73736 | tf_op jit(solution)/shard_map/ppermute | solution.py:240
  25.1 0.8 %collective-permute-done.8.mid_ref = f32[2,24,128]{2,1,0:T(8,128)S(1)} collective-permute-done((f32[2,24,128]{2,1,0:T(8,128)S(1)}, f32[2,24,128]{2,1,0:T(8,128)S(1)}, u32[]{:S(2)}, u32[]{:S(2)}) %collective-permute-start.8) | collective-permute-done | bytes 24608 | tf_op jit(solution)/shard_map/ppermute | solution.py:240
  26.0 3.4 %shard_map.101 = (f32[128,1,128]{2,1,0:T(1,128)}, f32[2,24,128]{2,1,0:T(8,128)S(1)}, f32[2,24,128]{2,1,0:T(8,128)S(1)}, f32[24,128]{1,0:T(8,128)S(1)}, f32[24,2048]{1,0:T(8,128)S(1)}) custom-call(s32[2]{0:T(128)S(1)} %pad_add_fusion.place_ref, f32[2,24,128]{2,1,0:T(8,128)S(1)} %collective-permute-done.6.near_ref, ...), custom_call_target="tpu_custom_call" | custom-call | tf_op jit(solution)/shard_map/pallas_call | solution.py:206
  29.4 3.9 %collective-permute-start.9 = (f32[2,24,128]{2,1,0:T(8,128)S(1)}, f32[2,24,128]{2,1,0:T(8,128)S(1)}, u32[]{:S(2)}, u32[]{:S(2)}) collective-permute-start(f32[2,24,128]{2,1,0:T(8,128)S(1)} %get-tuple-element.78), channel_id=1, source_target_pairs={{0,2},{1,3},{2,0},{3,1},{4,6},{5,7},{6,4},{7,5},{8,10},{9,11},{10,... | collective-permute-start | bytes 73736 | tf_op jit(solution)/shard_map/ppermute | solution.py:232
  33.3 0.6 collective-permute-start.10
  33.9 17.6 %all-to-all-start = ((f32[128,1,128]{2,1,0:T(1,128)}), f32[128,1,128]{2,1,0:T(1,128)S(1)}, u32[]{:S(2)}, u32[]{:S(2)}) async-start(f32[128,1,128]{2,1,0:T(1,128)} %get-tuple-element.85), calls=%async_computation | async-start | bytes 131072 | tf_op jit(solution)/shard_map/all_to_all | solution.py:295
  51.6 1.4 %shard_map.102.own_ref = f32[24,1024]{1,0:T(8,128)S(1)} custom-call(f32[24,2048]{1,0:T(8,128)S(1)} %get-tuple-element.80.spread_ref, s32[4,512]{1,0:T(4,128)S(1)} %copy-done.1, f32[24,1024]{1,0:T(8,128)S(1)} %get-tuple-element.69.image_ref.field_ref, f32[1,1024]{1,0:T(1,128)S(1)} %bitcast.12, s32[1,1024]{1,0:T(1,128)S(1)} %bitcast.15, f32[1,1024]{1,0:T(1,128)S(1)} %bitcast.18), custom_call_target="tpu_custom_call" | custom-call | tf_op jit(solution)/shard_map/pallas_call | solution.py:206
  53.0 1.1 %collective-permute-start.11 = (f32[2,24,128]{2,1,0:T(8,128)S(1)}, f32[2,24,128]{2,1,0:T(8,128)S(1)}, u32[]{:S(2)}, u32[]{:S(2)}) collective-permute-start(f32[2,24,128]{2,1,0:T(8,128)S(1)} %pad_maximum_fusion.3), channel_id=1, source_target_pairs={{0,1},{1,0},{2,3},{3,2},{4,5},{5,4},{6,7},{7,6},{8,9},{9,8},{10,11... | collective-permute-start | bytes 73736 | tf_op jit(solution)/shard_map/ppermute | solution.py:240
  54.1 0.8 %collective-permute-done.11.mid_ref = f32[2,24,128]{2,1,0:T(8,128)S(1)} collective-permute-done((f32[2,24,128]{2,1,0:T(8,128)S(1)}, f32[2,24,128]{2,1,0:T(8,128)S(1)}, u32[]{:S(2)}, u32[]{:S(2)}) %collective-permute-start.11) | collective-permute-done | bytes 24608 | tf_op jit(solution)/shard_map/ppermute | solution.py:240
  55.0 6.1 %all-to-all-done.sums_ref = f32[128,1,128]{2,1,0:T(1,128)S(1)} async-done(((f32[128,1,128]{2,1,0:T(1,128)}), f32[128,1,128]{2,1,0:T(1,128)S(1)}, u32[]{:S(2)}, u32[]{:S(2)}) %all-to-all-start) | async-done | bytes 65568 | tf_op jit(solution)/shard_map/all_to_all | solution.py:295
  61.1 1.6 %shard_map.103 = (f32[18,1024]{1,0:T(8,128)}, f32[18,1024]{1,0:T(8,128)}) custom-call(s32[2]{0:T(128)S(1)} %pad_add_fusion.place_ref, f32[24,1024]{1,0:T(8,128)S(1)} %shard_map.102.own_ref, f32[2,24,128]{2,1,0:T(8,128)S(1)} %collective-permute-done.9.near_ref, f32[2,24,128]{2,1,0:T(8,128)S(1)} %collective-permute-done.10.far_ref, ...), custom_call_target="tpu_custom_call" | custom-call | tf_op jit(solution)/shard_map/pallas_call | solution.py:206
  (30 shorter events, 1.9 us)
Async XLA Ops:
  2.2 6.3 %collective-permute-start = (f32[2,24,128]{2,1,0:T(8,128)S(1)}, f32[2,24,128]{2,1,0:T(8,128)S(1)}, u32[]{:S(2)}, u32[]{:S(2)}) collective-permute-start(f32[2,24,128]{2,1,0:T(8,128)S(1)} %get-tuple-element.44), channel_id=1, source_target_pairs={{0,2},{1,3},{2,0},{3,1},{4,6},{5,7},{6,4},{7,5},{8,10},{9,11},{10,... | collective-permute-start | bytes 73736 | tf_op jit(solution)/shard_map/ppermute | solution.py:232
  4.3 4.2 %collective-permute-start.1 = (f32[2,24,128]{2,1,0:T(8,128)S(1)}, f32[2,24,128]{2,1,0:T(8,128)S(1)}, u32[]{:S(2)}, u32[]{:S(2)}) collective-permute-start(f32[2,24,128]{2,1,0:T(8,128)S(1)} %get-tuple-element.45), channel_id=1, source_target_pairs={{0,1},{1,0},{2,4},{3,5},{4,2},{5,3},{6,8},{7,9},{8,6},{9,7},{10,12... | collective-permute-start | bytes 73736 | tf_op jit(solution)/shard_map/ppermute | solution.py:232
  5.2 0.7 %copy-start = (s32[4,512]{1,0:T(4,128)S(1)}, s32[4,512]{1,0:T(4,128)}, u32[]{:S(2)}) copy-start(s32[4,512]{1,0:T(4,128)} %map_ref.7) | copy-start | bytes 24580
  5.9 9.5 %copy-start.2 = (f32[1024]{0:T(1024)S(1)}, f32[1024]{0:T(1024)}, u32[]{:S(2)}) copy-start(f32[1024]{0:T(1024)} %param.13) | copy-start | bytes 12292
  5.9 9.5 %copy-start.3 = (s32[1024]{0:T(1024)S(1)}, s32[1024]{0:T(1024)}, u32[]{:S(2)}) copy-start(s32[1024]{0:T(1024)} %param.14) | copy-start | bytes 12292
  5.9 9.5 %copy-start.4 = (f32[1024]{0:T(1024)S(1)}, f32[1024]{0:T(1024)}, u32[]{:S(2)}) copy-start(f32[1024]{0:T(1024)} %param.15) | copy-start | bytes 12292
  8.5 14.7 %copy-start.1 = (s32[4,512]{1,0:T(4,128)S(1)}, s32[4,512]{1,0:T(4,128)}, u32[]{:S(2)}) copy-start(s32[4,512]{1,0:T(4,128)} %map_ref.7) | copy-start | bytes 24580
  8.6 1.3 %collective-permute-start.2 = (f32[2,24,128]{2,1,0:T(8,128)S(1)}, f32[2,24,128]{2,1,0:T(8,128)S(1)}, u32[]{:S(2)}, u32[]{:S(2)}) collective-permute-start(f32[2,24,128]{2,1,0:T(8,128)S(1)} %pad_maximum_fusion), channel_id=1, source_target_pairs={{0,1},{1,0},{2,3},{3,2},{4,5},{5,4},{6,7},{7,6},{8,9},{9,8},{10,11... | collective-permute-start | bytes 73736 | tf_op jit(solution)/shard_map/ppermute | solution.py:240
  12.7 4.2 %collective-permute-start.3 = (f32[2,24,128]{2,1,0:T(8,128)S(1)}, f32[2,24,128]{2,1,0:T(8,128)S(1)}, u32[]{:S(2)}, u32[]{:S(2)}) collective-permute-start(f32[2,24,128]{2,1,0:T(8,128)S(1)} %get-tuple-element.56), channel_id=1, source_target_pairs={{0,2},{1,3},{2,0},{3,1},{4,6},{5,7},{6,4},{7,5},{8,10},{9,11},{10,... | collective-permute-start | bytes 73736 | tf_op jit(solution)/shard_map/ppermute | solution.py:232
  14.8 2.1 %collective-permute-start.4 = (f32[2,24,128]{2,1,0:T(8,128)S(1)}, f32[2,24,128]{2,1,0:T(8,128)S(1)}, u32[]{:S(2)}, u32[]{:S(2)}) collective-permute-start(f32[2,24,128]{2,1,0:T(8,128)S(1)} %get-tuple-element.57), channel_id=1, source_target_pairs={{0,1},{1,0},{2,4},{3,5},{4,2},{5,3},{6,8},{7,9},{8,6},{9,7},{10,12... | collective-permute-start | bytes 73736 | tf_op jit(solution)/shard_map/ppermute | solution.py:232
  16.9 1.3 %collective-permute-start.5 = (f32[2,24,128]{2,1,0:T(8,128)S(1)}, f32[2,24,128]{2,1,0:T(8,128)S(1)}, u32[]{:S(2)}, u32[]{:S(2)}) collective-permute-start(f32[2,24,128]{2,1,0:T(8,128)S(1)} %pad_maximum_fusion.1), channel_id=1, source_target_pairs={{0,1},{1,0},{2,3},{3,2},{4,5},{5,4},{6,7},{7,6},{8,9},{9,8},{10,11... | collective-permute-start | bytes 73736 | tf_op jit(solution)/shard_map/ppermute | solution.py:240
  19.4 4.8 %collective-permute-start.6 = (f32[2,24,128]{2,1,0:T(8,128)S(1)}, f32[2,24,128]{2,1,0:T(8,128)S(1)}, u32[]{:S(2)}, u32[]{:S(2)}) collective-permute-start(f32[2,24,128]{2,1,0:T(8,128)S(1)} %get-tuple-element.67), channel_id=1, source_target_pairs={{0,2},{1,3},{2,0},{3,1},{4,6},{5,7},{6,4},{7,5},{8,10},{9,11},{10,... | collective-permute-start | bytes 73736 | tf_op jit(solution)/shard_map/ppermute | solution.py:232
  22.6 1.6 %collective-permute-start.7 = (f32[2,24,128]{2,1,0:T(8,128)S(1)}, f32[2,24,128]{2,1,0:T(8,128)S(1)}, u32[]{:S(2)}, u32[]{:S(2)}) collective-permute-start(f32[2,24,128]{2,1,0:T(8,128)S(1)} %get-tuple-element.68), channel_id=1, source_target_pairs={{0,1},{1,0},{2,4},{3,5},{4,2},{5,3},{6,8},{7,9},{8,6},{9,7},{10,12... | collective-permute-start | bytes 73736 | tf_op jit(solution)/shard_map/ppermute | solution.py:232
  24.2 1.8 %collective-permute-start.8 = (f32[2,24,128]{2,1,0:T(8,128)S(1)}, f32[2,24,128]{2,1,0:T(8,128)S(1)}, u32[]{:S(2)}, u32[]{:S(2)}) collective-permute-start(f32[2,24,128]{2,1,0:T(8,128)S(1)} %pad_maximum_fusion.2), channel_id=1, source_target_pairs={{0,1},{1,0},{2,3},{3,2},{4,5},{5,4},{6,7},{7,6},{8,9},{9,8},{10,11... | collective-permute-start | bytes 73736 | tf_op jit(solution)/shard_map/ppermute | solution.py:240
  29.4 23.6 %collective-permute-start.9 = (f32[2,24,128]{2,1,0:T(8,128)S(1)}, f32[2,24,128]{2,1,0:T(8,128)S(1)}, u32[]{:S(2)}, u32[]{:S(2)}) collective-permute-start(f32[2,24,128]{2,1,0:T(8,128)S(1)} %get-tuple-element.78), channel_id=1, source_target_pairs={{0,2},{1,3},{2,0},{3,1},{4,6},{5,7},{6,4},{7,5},{8,10},{9,11},{10,... | collective-permute-start | bytes 73736 | tf_op jit(solution)/shard_map/ppermute | solution.py:232
  33.3 19.7 %collective-permute-start.10 = (f32[2,24,128]{2,1,0:T(8,128)S(1)}, f32[2,24,128]{2,1,0:T(8,128)S(1)}, u32[]{:S(2)}, u32[]{:S(2)}) collective-permute-start(f32[2,24,128]{2,1,0:T(8,128)S(1)} %get-tuple-element.79), channel_id=1, source_target_pairs={{0,1},{1,0},{2,4},{3,5},{4,2},{5,3},{6,8},{7,9},{8,6},{9,7},{10,12... | collective-permute-start | bytes 73736 | tf_op jit(solution)/shard_map/ppermute | solution.py:232
  33.9 27.2 %all-to-all-start = ((f32[128,1,128]{2,1,0:T(1,128)}), f32[128,1,128]{2,1,0:T(1,128)S(1)}, u32[]{:S(2)}, u32[]{:S(2)}) async-start(f32[128,1,128]{2,1,0:T(1,128)} %get-tuple-element.85), calls=%async_computation | async-start | bytes 131072 | tf_op jit(solution)/shard_map/all_to_all | solution.py:295
  53.0 2.0 %collective-permute-start.11 = (f32[2,24,128]{2,1,0:T(8,128)S(1)}, f32[2,24,128]{2,1,0:T(8,128)S(1)}, u32[]{:S(2)}, u32[]{:S(2)}) collective-permute-start(f32[2,24,128]{2,1,0:T(8,128)S(1)} %pad_maximum_fusion.3), channel_id=1, source_target_pairs={{0,1},{1,0},{2,3},{3,2},{4,5},{5,4},{6,7},{7,6},{8,9},{9,8},{10,11... | collective-permute-start | bytes 73736 | tf_op jit(solution)/shard_map/ppermute | solution.py:240

commit v4 on v3

--- a/solution.py
+++ b/solution.py
@@ -20,7 +20,6 @@
 F32 = jnp.float32
 BF16 = jnp.bfloat16
 VMEM = pltpu.VMEM
-SMEM = pltpu.SMEM
 
 
 def pieces(x):
@@ -45,12 +44,17 @@
     )
 
 
+def place():
+    here = lax.axis_index(DOM).astype(jnp.int32)
+    return here & 1, (here >> 1) & 1
+
+
 def split(x):
     return [x[:, k * GH : (k + 1) * GH] for k in range(NB)]
 
 
-def write_blocks(blocks, place_ref, near_ref, far_ref, mid_ref):
-    core, odd = place_ref[0], place_ref[1]
+def write_blocks(blocks, near_ref, far_ref, mid_ref):
+    core, odd = place()
     ahead, next_up, next_down, behind = (blocks[k] for k in (3, 2, 1, 0))
     near_ref[0] = jnp.where(odd == 1, behind, ahead)
     near_ref[1] = jnp.where(odd == 1, next_down, next_up)
@@ -59,8 +63,8 @@
     mid_ref[...] = jnp.where(core == 1, next_down, next_up)
 
 
-def read_blocks(place_ref, near_ref, far_ref, mid_ref):
-    core, odd = place_ref[0], place_ref[1]
+def read_blocks(near_ref, far_ref, mid_ref):
+    core, odd = place()
     near, far, first, second = near_ref[0], far_ref[0], mid_ref[0], mid_ref[1]
     return [
         jnp.where(odd == 1, far, near),
@@ -82,7 +86,7 @@
     return jnp.sum(jnp.sum(x, axis=0, keepdims=True), axis=1, keepdims=True)
 
 
-def send_kernel(place_ref, count_ref, field_ref, index_ref, near_ref, far_ref, mid_ref, share_ref, padded_ref):
+def send_kernel(count_ref, field_ref, index_ref, near_ref, far_ref, mid_ref, share_ref, padded_ref):
     for k in range(NB):
         rows = lax.broadcasted_iota(jnp.int32, (F, GH), 0)
         lanes = lax.broadcasted_iota(jnp.int32, (1, GH), 1)
@@ -90,7 +94,7 @@
         share_ref[:, k * GH : (k + 1) * GH] = jnp.where(rows == face, 1.0, 0.0).astype(BF16)
     padded_ref[TR:, :] = jnp.zeros((TP - TR, F), F32)
     padded_ref[:TR, :] = field_ref[...]
-    write_blocks(split(pick(padded_ref[...], share_ref[...])), place_ref, near_ref, far_ref, mid_ref)
+    write_blocks(split(pick(padded_ref[...], share_ref[...])), near_ref, far_ref, mid_ref)
 
 
 def fill_selector(map_ref, sel_ref, first):
@@ -109,9 +113,9 @@
     copy.wait()
 
 
-def product_kernel(place_ref, near_ref, far_ref, mid_ref, sel_ref, matrix_ref, local_ref, *refs):
+def product_kernel(near_ref, far_ref, mid_ref, sel_ref, matrix_ref, local_ref, *refs):
     near_out, far_out, mid_out, spread_ref, pick_ref, ghost_ref, prod_ref = refs[-7:]
-    for k, block in enumerate(read_blocks(place_ref, near_ref, far_ref, mid_ref)):
+    for k, block in enumerate(read_blocks(near_ref, far_ref, mid_ref)):
         ghost_ref[:, k * GH : (k + 1) * GH] = block
     pick_ref[...] = local_ref[...] + pick(ghost_ref[...], sel_ref[...])
     for t in range(E // 128):
@@ -125,7 +129,7 @@
     for s in range(SIDES):
         spread_ref[:TR, s * E : (s + 1) * E] = prod_ref[s * TR : (s + 1) * TR, :]
     parts = split(spread_out(spread_ref[...], sel_ref[...]))
-    write_blocks(parts[::-1], place_ref, near_out, far_out, mid_out)
+    write_blocks(parts[::-1], near_out, far_out, mid_out)
     if len(refs) == 10:
         first_ref, second_ref, row_ref = refs[:3]
         lane = lax.broadcasted_iota(jnp.int32, (1, GH), 1)
@@ -150,12 +154,12 @@
     own_ref[...] = spread_out(spread_ref[...], sel_ref[...]) + damped
 
 
-def combine_kernel(place_ref, own_ref, near_ref, far_ref, mid_ref, share_ref, image_ref, near_out, far_out, mid_out, back_ref):
-    for k, block in enumerate(read_blocks(place_ref, near_ref, far_ref, mid_ref)[::-1]):
+def combine_kernel(own_ref, near_ref, far_ref, mid_ref, share_ref, image_ref, near_out, far_out, mid_out, back_ref):
+    for k, block in enumerate(read_blocks(near_ref, far_ref, mid_ref)[::-1]):
         back_ref[:, k * GH : (k + 1) * GH] = block
     image = own_ref[...] + spread_out(back_ref[...], share_ref[...])
     image_ref[...] = image
-    write_blocks(split(pick(image, share_ref[...])), place_ref, near_out, far_out, mid_out)
+    write_blocks(split(pick(image, share_ref[...])), near_out, far_out, mid_out)
 
 
 def local_kernel(image_ref, map_ref, mass_ref, absorbing_ref, impedance_ref, local_ref, sums_ref, sel_ref):
@@ -168,9 +172,9 @@
 
 
 def final_kernel(
-    place_ref, own_ref, near_ref, far_ref, mid_ref, share_ref, field_ref, image_ref, sums_ref, solution_ref, residual_ref, back_ref
+    own_ref, near_ref, far_ref, mid_ref, share_ref, field_ref, image_ref, sums_ref, solution_ref, residual_ref, back_ref
 ):
-    for k, block in enumerate(read_blocks(place_ref, near_ref, far_ref, mid_ref)[::-1]):
+    for k, block in enumerate(read_blocks(near_ref, far_ref, mid_ref)[::-1]):
         back_ref[:, k * GH : (k + 1) * GH] = block
     second = own_ref[...] + spread_out(back_ref[...], share_ref[...])
     field, image = field_ref[:TR], image_ref[:TR]
@@ -197,12 +201,9 @@
 ANY = pl.ANY
 
 
-def call(kernel, out_shape, *args, scratch=(), scalars=1, held=VMEM, last=VMEM):
-    spaces = [SMEM] * scalars + [VMEM] * (len(args) - scalars - 1) + [last]
-    args = [
-        a if m is SMEM else pltpu.with_memory_space_constraint(a, pltpu.HBM if m is ANY else held)
-        for a, m in zip(args, spaces)
-    ]
+def call(kernel, out_shape, *args, scratch=(), held=VMEM, last=VMEM):
+    spaces = [VMEM] * (len(args) - 1) + [last]
+    args = [pltpu.with_memory_space_constraint(a, pltpu.HBM if m is ANY else held) for a, m in zip(args, spaces)]
     return pl.pallas_call(
         kernel,
         in_specs=[pl.BlockSpec(memory_space=m) for m in spaces],
@@ -217,9 +218,7 @@
     right_side, element_matrix, face_map, share_index, share_count, face_mass, absorbing, impedance
 ):
     count = lax.axis_size(DOM)
-    here = lax.axis_index(DOM).astype(jnp.int32)
-    core, odd = here & 1, (here >> 1) & 1
-    place = jnp.stack([core, odd])
+    core, odd = place()
     diagonal = [x.reshape(1, F) for x in (face_mass, absorbing, impedance)]
     chips = count // 2
 
@@ -241,13 +240,7 @@
         return (got_near, got_far, got_mid), beside
 
     *sent, share, padded = call(
-        send_kernel,
-        MESSAGE + (VMEM((F, SHARED), BF16), FACES),
-        place,
-        share_count,
-        right_side,
-        share_index[0],
-        held=pltpu.HBM,
+        send_kernel, MESSAGE + (VMEM((F, SHARED), BF16), FACES), share_count, right_side, share_index[0], held=pltpu.HBM
     )
 
     def select():
@@ -258,32 +251,26 @@
             padded,
             element_matrix,
             scratch=[OWN_SELECTOR, pltpu.SemaphoreType.DMA],
-            scalars=0,
             last=ANY,
         )
 
     got, (selector, local, matrix) = exchange(*sent, select)
     scratch = [GHOSTS, VMEM((DOFS, E), F32)]
-    *sent, spread, picked = call(
-        product_kernel, MESSAGE + (WIDE, WIDE), place, *got, selector, matrix, local, scratch=scratch
-    )
+    *sent, spread, picked = call(product_kernel, MESSAGE + (WIDE, WIDE), *got, selector, matrix, local, scratch=scratch)
 
     def own0():
-        return call(
-            own_kernel, (ROW, FACES), spread, face_map, padded, *diagonal, picked, scratch=[OWN_SELECTOR], scalars=0
-        )
+        return call(own_kernel, (ROW, FACES), spread, face_map, padded, *diagonal, picked, scratch=[OWN_SELECTOR])
 
     got, (sums0, own) = exchange(*sent, own0)
-    image, *sent = call(combine_kernel, (FACES,) + MESSAGE, place, own, *got, share, scratch=[GHOSTS])
+    image, *sent = call(combine_kernel, (FACES,) + MESSAGE, own, *got, share, scratch=[GHOSTS])
 
     def local1():
-        return call(local_kernel, (WIDE, ROW), image, face_map, *diagonal, scratch=[OWN_SELECTOR], scalars=0)
+        return call(local_kernel, (WIDE, ROW), image, face_map, *diagonal, scratch=[OWN_SELECTOR])
 
     got, (local, sums1) = exchange(*sent, local1)
     row, *sent, spread = call(
         product_kernel,
         (jax.ShapeDtypeStruct((count, 1, GH), F32),) + MESSAGE + (WIDE,),
-        place,
         *got,
         selector,
         matrix,
@@ -295,11 +282,11 @@
     row = lax.all_to_all(row, DOM, 0, 0)
 
     def own1():
-        return call(own_kernel, FACES, spread, face_map, image, *diagonal, scratch=[OWN_SELECTOR], scalars=0)
+        return call(own_kernel, FACES, spread, face_map, image, *diagonal, scratch=[OWN_SELECTOR])
 
     got, own = exchange(*sent, own1)
     out = jax.ShapeDtypeStruct((TR, F), F32)
-    return call(final_kernel, (out, out), place, own, *got, share, padded, image, row, scratch=[GHOSTS])
+    return call(final_kernel, (out, out), own, *got, share, padded, image, row, scratch=[GHOSTS])
 
 
 def solution(mesh):

time: 63 us -> 60.9 us (0.967)
  Pallas kernels: 16.7 us -> 14.7 us
    pallas_call x9, Pallas kernels: 16.7 us -> 14.7 us  [call(): pl.pallas_call(kernel, in_specs=[pl.BlockSpec(memory_space=m) for m in sp...]
where the time goes in v4:
time: 60.9 us; the launch traced here: 60.6 us
  starting transfers between devices  34.5 us (57%)
  Pallas kernels  14.7 us (24%)
  waiting for transfers between devices  9.88 us (16%)
  between operations  0.84 us (1%)
  local copies, waits for them, and re-layouts  0.71 us (1%)
    all_to_all x1, starting transfers between devices, shards(): row = lax.all_to_all(row, DOM, 0, 0)  17.6 us
    pallas_call x9, Pallas kernels, call(): pl.pallas_call(kernel, in_specs=[pl.BlockSpec(memory_space=m) for m in sp...  14.7 us
    ppermute x8, starting transfers between devices, swap(): return lax.ppermute(value, DOM, pairs)  14.2 us
    all_to_all x1, waiting for transfers between devices, shards(): row = lax.all_to_all(row, DOM, 0, 0)  6.12 us
    ppermute x4, waiting for transfers between devices, exchange(): got_mid = lax.ppermute(pair, DOM, [(i, i ^ 1) for i in range(count)])  3.73 us
    ppermute x4, starting transfers between devices, exchange(): got_mid = lax.ppermute(pair, DOM, [(i, i ^ 1) for i in range(count)])  2.6 us
  transfers between devices with their start and end apart: 13, of which 5 were waited for; matrix products, arithmetic and copies ran while one was open for 0% of the time, Pallas kernels for 10%

profile of v4, /device:TPU:1, one launch (start us, length us, event | category | flops | bytes accessed | tf_op | source)
XLA Modules:
  0.0 60.6 jit_solution(4319827159252840347)
XLA Ops:
  0.6 1.4 %shard_map.95 = (f32[2,24,128]{2,1,0:T(8,128)S(1)}, f32[2,24,128]{2,1,0:T(8,128)S(1)}, f32[24,128]{1,0:T(8,128)S(1)}, bf16[1024,512]{1,0:T(8,128)(2,1)S(1)}, f32[24,1024]{1,0:T(8,128)S(1)}) custom-call(s32[1,4]{1,0:T(1,128)} %count_ref.1, f32[18,1024]{1,0:T(8,128)} %field_ref.1, s32[4,128]{1,0:T(4,128)} %bitcast.21), custom_call_target="tpu_custom_call" | custom-call | tf_op jit(solution)/shard_map/pallas_call | solution.py:207
  2.1 2.1 %collective-permute-start = (f32[2,24,128]{2,1,0:T(8,128)S(1)}, f32[2,24,128]{2,1,0:T(8,128)S(1)}, u32[]{:S(2)}, u32[]{:S(2)}) collective-permute-start(f32[2,24,128]{2,1,0:T(8,128)S(1)} %get-tuple-element.44), channel_id=1, source_target_pairs={{0,2},{1,3},{2,0},{3,1},{4,6},{5,7},{6,4},{7,5},{8,10},{9,11},{10,... | collective-permute-start | bytes 73736 | tf_op jit(solution)/shard_map/ppermute | solution.py:231
  4.2 1.0 %collective-permute-start.1 = (f32[2,24,128]{2,1,0:T(8,128)S(1)}, f32[2,24,128]{2,1,0:T(8,128)S(1)}, u32[]{:S(2)}, u32[]{:S(2)}) collective-permute-start(f32[2,24,128]{2,1,0:T(8,128)S(1)} %get-tuple-element.45), channel_id=1, source_target_pairs={{0,1},{1,0},{2,4},{3,5},{4,2},{5,3},{6,8},{7,9},{8,6},{9,7},{10,12... | collective-permute-start | bytes 73736 | tf_op jit(solution)/shard_map/ppermute | solution.py:231
  5.1 0.7 %copy-done = s32[4,512]{1,0:T(4,128)S(1)} copy-done((s32[4,512]{1,0:T(4,128)S(1)}, s32[4,512]{1,0:T(4,128)}, u32[]{:S(2)}) %copy-start) | copy-done | bytes 8216
  5.8 2.6 %shard_map.96 = (bf16[512,2048]{1,0:T(8,128)(2,1)S(1)}, f32[24,2048]{1,0:T(8,128)S(1)}, bf16[72,72,512]{2,1,0:T(8,128)(2,1)S(1)}) custom-call(s32[4,512]{1,0:T(4,128)S(1)} %copy-done, f32[24,1024]{1,0:T(8,128)S(1)} %get-tuple-element.46.field_ref, bf16[72,72,512]{2,1,0:T(8,128)(2,1)} %matrix_ref.1), custom_call_target="tpu_custom_call" | custom-call | tf_op jit(solution)/shard_map/pallas_call | solution.py:207
  8.6 1.2 %collective-permute-done.2.mid_ref = f32[2,24,128]{2,1,0:T(8,128)S(1)} collective-permute-done((f32[2,24,128]{2,1,0:T(8,128)S(1)}, f32[2,24,128]{2,1,0:T(8,128)S(1)}, u32[]{:S(2)}, u32[]{:S(2)}) %collective-permute-start.2) | collective-permute-done | bytes 24608 | tf_op jit(solution)/shard_map/ppermute | solution.py:239
  9.7 2.4 %shard_map.97 = (f32[2,24,128]{2,1,0:T(8,128)S(1)}, f32[2,24,128]{2,1,0:T(8,128)S(1)}, f32[24,128]{1,0:T(8,128)S(1)}, f32[24,2048]{1,0:T(8,128)S(1)}, f32[24,2048]{1,0:T(8,128)S(1)}) custom-call(f32[2,24,128]{2,1,0:T(8,128)S(1)} %collective-permute-done.near_ref, f32[2,24,128]{2,1,0:T(8,128)S(1)} %collective-permute-done.1.far_ref, ...), custom_call_target="tpu_custom_call" | custom-call | tf_op jit(solution)/shard_map/pallas_call | solution.py:207
  12.1 2.1 %collective-permute-start.3 = (f32[2,24,128]{2,1,0:T(8,128)S(1)}, f32[2,24,128]{2,1,0:T(8,128)S(1)}, u32[]{:S(2)}, u32[]{:S(2)}) collective-permute-start(f32[2,24,128]{2,1,0:T(8,128)S(1)} %get-tuple-element.56), channel_id=1, source_target_pairs={{0,2},{1,3},{2,0},{3,1},{4,6},{5,7},{6,4},{7,5},{8,10},{9,11},{10,... | collective-permute-start | bytes 73736 | tf_op jit(solution)/shard_map/ppermute | solution.py:231
  14.3 0.6 %collective-permute-start.4 = (f32[2,24,128]{2,1,0:T(8,128)S(1)}, f32[2,24,128]{2,1,0:T(8,128)S(1)}, u32[]{:S(2)}, u32[]{:S(2)}) collective-permute-start(f32[2,24,128]{2,1,0:T(8,128)S(1)} %get-tuple-element.57), channel_id=1, source_target_pairs={{0,1},{1,0},{2,4},{3,5},{4,2},{5,3},{6,8},{7,9},{8,6},{9,7},{10,12... | collective-permute-start | bytes 73736 | tf_op jit(solution)/shard_map/ppermute | solution.py:231
  14.9 1.4 %shard_map.98 = (f32[1,128]{1,0:T(1,128)S(1)}, f32[24,1024]{1,0:T(8,128)S(1)}) custom-call(f32[24,2048]{1,0:T(8,128)S(1)} %get-tuple-element.58.spread_ref, s32[4,512]{1,0:T(4,128)S(1)} %copy-done, f32[24,1024]{1,0:T(8,128)S(1)} %get-tuple-element.46.field_ref, f32[1,1024]{1,0:T(1,128)S(1)} %bitcast.8, s32[1,1024]{1,0:T(1,128)S(1)} %bitcast.11, ...), custom_call_target="tpu_custom_call" | custom-call | tf_op jit(solution)/shard_map/pallas_call | solution.py:207
  16.8 0.9 %collective-permute-done.5.mid_ref = f32[2,24,128]{2,1,0:T(8,128)S(1)} collective-permute-done((f32[2,24,128]{2,1,0:T(8,128)S(1)}, f32[2,24,128]{2,1,0:T(8,128)S(1)}, u32[]{:S(2)}, u32[]{:S(2)}) %collective-permute-start.5) | collective-permute-done | bytes 24608 | tf_op jit(solution)/shard_map/ppermute | solution.py:239
  18.3 3.2 %collective-permute-start.6 = (f32[2,24,128]{2,1,0:T(8,128)S(1)}, f32[2,24,128]{2,1,0:T(8,128)S(1)}, u32[]{:S(2)}, u32[]{:S(2)}) collective-permute-start(f32[2,24,128]{2,1,0:T(8,128)S(1)} %get-tuple-element.67), channel_id=1, source_target_pairs={{0,2},{1,3},{2,0},{3,1},{4,6},{5,7},{6,4},{7,5},{8,10},{9,11},{10,... | collective-permute-start | bytes 73736 | tf_op jit(solution)/shard_map/ppermute | solution.py:231
  21.5 0.6 %collective-permute-start.7 = (f32[2,24,128]{2,1,0:T(8,128)S(1)}, f32[2,24,128]{2,1,0:T(8,128)S(1)}, u32[]{:S(2)}, u32[]{:S(2)}) collective-permute-start(f32[2,24,128]{2,1,0:T(8,128)S(1)} %get-tuple-element.68), channel_id=1, source_target_pairs={{0,1},{1,0},{2,4},{3,5},{4,2},{5,3},{6,8},{7,9},{8,6},{9,7},{10,12... | collective-permute-start | bytes 73736 | tf_op jit(solution)/shard_map/ppermute | solution.py:231
  22.1 0.9 %shard_map.100 = (f32[24,2048]{1,0:T(8,128)S(1)}, f32[1,128]{1,0:T(1,128)S(1)}) custom-call(f32[24,1024]{1,0:T(8,128)S(1)} %get-tuple-element.69.image_ref.field_ref, s32[4,512]{1,0:T(4,128)S(1)} %copy-done.1, f32[1,1024]{1,0:T(1,128)S(1)} %bitcast.9, s32[1,1024]{1,0:T(1,128)S(1)} %bitcast.12, f32[1,1024]{1,0:T(1,128)S(1)} %bitcast.15), custom_call_target="tpu_custom_call" | custom-call | tf_op jit(solution)/shard_map/pallas_call | solution.py:207
  23.1 0.9 %collective-permute-start.8 = (f32[2,24,128]{2,1,0:T(8,128)S(1)}, f32[2,24,128]{2,1,0:T(8,128)S(1)}, u32[]{:S(2)}, u32[]{:S(2)}) collective-permute-start(f32[2,24,128]{2,1,0:T(8,128)S(1)} %pad_maximum_fusion.2), channel_id=1, source_target_pairs={{0,1},{1,0},{2,3},{3,2},{4,5},{5,4},{6,7},{7,6},{8,9},{9,8},{10,11... | collective-permute-start | bytes 73736 | tf_op jit(solution)/shard_map/ppermute | solution.py:239
  24.0 0.8 %collective-permute-done.8.mid_ref = f32[2,24,128]{2,1,0:T(8,128)S(1)} collective-permute-done((f32[2,24,128]{2,1,0:T(8,128)S(1)}, f32[2,24,128]{2,1,0:T(8,128)S(1)}, u32[]{:S(2)}, u32[]{:S(2)}) %collective-permute-start.8) | collective-permute-done | bytes 24608 | tf_op jit(solution)/shard_map/ppermute | solution.py:239
  24.9 2.9 %shard_map.101 = (f32[128,1,128]{2,1,0:T(1,128)}, f32[2,24,128]{2,1,0:T(8,128)S(1)}, f32[2,24,128]{2,1,0:T(8,128)S(1)}, f32[24,128]{1,0:T(8,128)S(1)}, f32[24,2048]{1,0:T(8,128)S(1)}) custom-call(f32[2,24,128]{2,1,0:T(8,128)S(1)} %collective-permute-done.6.near_ref, f32[2,24,128]{2,1,0:T(8,128)S(1)} %collective-permute-done.7.far_ref, ...), custom_call_target="tpu_custom_call" | custom-call | tf_op jit(solution)/shard_map/pallas_call | solution.py:207
  27.8 3.9 %collective-permute-start.9 = (f32[2,24,128]{2,1,0:T(8,128)S(1)}, f32[2,24,128]{2,1,0:T(8,128)S(1)}, u32[]{:S(2)}, u32[]{:S(2)}) collective-permute-start(f32[2,24,128]{2,1,0:T(8,128)S(1)} %get-tuple-element.78), channel_id=1, source_target_pairs={{0,2},{1,3},{2,0},{3,1},{4,6},{5,7},{6,4},{7,5},{8,10},{9,11},{10,... | collective-permute-start | bytes 73736 | tf_op jit(solution)/shard_map/ppermute | solution.py:231
  32.4 17.6 %all-to-all-start = ((f32[128,1,128]{2,1,0:T(1,128)}), f32[128,1,128]{2,1,0:T(1,128)S(1)}, u32[]{:S(2)}, u32[]{:S(2)}) async-start(f32[128,1,128]{2,1,0:T(1,128)} %get-tuple-element.85), calls=%async_computation | async-start | bytes 131072 | tf_op jit(solution)/shard_map/all_to_all | solution.py:282
  50.0 1.4 %shard_map.102.own_ref = f32[24,1024]{1,0:T(8,128)S(1)} custom-call(f32[24,2048]{1,0:T(8,128)S(1)} %get-tuple-element.80.spread_ref, s32[4,512]{1,0:T(4,128)S(1)} %copy-done.1, f32[24,1024]{1,0:T(8,128)S(1)} %get-tuple-element.69.image_ref.field_ref, f32[1,1024]{1,0:T(1,128)S(1)} %bitcast.10, s32[1,1024]{1,0:T(1,128)S(1)} %bitcast.13, f32[1,1024]{1,0:T(1,128)S(1)} %bitcast.16), custom_call_target="tpu_custom_call" | custom-call | tf_op jit(solution)/shard_map/pallas_call | solution.py:207
  51.4 1.1 %collective-permute-start.11 = (f32[2,24,128]{2,1,0:T(8,128)S(1)}, f32[2,24,128]{2,1,0:T(8,128)S(1)}, u32[]{:S(2)}, u32[]{:S(2)}) collective-permute-start(f32[2,24,128]{2,1,0:T(8,128)S(1)} %pad_maximum_fusion.3), channel_id=1, source_target_pairs={{0,1},{1,0},{2,3},{3,2},{4,5},{5,4},{6,7},{7,6},{8,9},{9,8},{10,11... | collective-permute-start | bytes 73736 | tf_op jit(solution)/shard_map/ppermute | solution.py:239
  52.6 0.8 %collective-permute-done.11.mid_ref = f32[2,24,128]{2,1,0:T(8,128)S(1)} collective-permute-done((f32[2,24,128]{2,1,0:T(8,128)S(1)}, f32[2,24,128]{2,1,0:T(8,128)S(1)}, u32[]{:S(2)}, u32[]{:S(2)}) %collective-permute-start.11) | collective-permute-done | bytes 24608 | tf_op jit(solution)/shard_map/ppermute | solution.py:239
  53.4 6.1 %all-to-all-done.sums_ref = f32[128,1,128]{2,1,0:T(1,128)S(1)} async-done(((f32[128,1,128]{2,1,0:T(1,128)}), f32[128,1,128]{2,1,0:T(1,128)S(1)}, u32[]{:S(2)}, u32[]{:S(2)}) %all-to-all-start) | async-done | bytes 65568 | tf_op jit(solution)/shard_map/all_to_all | solution.py:282
  59.5 1.1 %shard_map.103 = (f32[18,1024]{1,0:T(8,128)}, f32[18,1024]{1,0:T(8,128)}) custom-call(f32[24,1024]{1,0:T(8,128)S(1)} %shard_map.102.own_ref, f32[2,24,128]{2,1,0:T(8,128)S(1)} %collective-permute-done.9.near_ref, f32[2,24,128]{2,1,0:T(8,128)S(1)} %collective-permute-done.10.far_ref, f32[2,24,128]{2,1,0:T(8,128)S(1)} %collective-permute-done.11.mid_ref, ...), custom_call_target="tpu_custom_call" | custom-call | tf_op jit(solution)/shard_map/pallas_call | solution.py:207
  (29 shorter events, 1.8 us)
Async XLA Ops:
  2.1 6.3 %collective-permute-start = (f32[2,24,128]{2,1,0:T(8,128)S(1)}, f32[2,24,128]{2,1,0:T(8,128)S(1)}, u32[]{:S(2)}, u32[]{:S(2)}) collective-permute-start(f32[2,24,128]{2,1,0:T(8,128)S(1)} %get-tuple-element.44), channel_id=1, source_target_pairs={{0,2},{1,3},{2,0},{3,1},{4,6},{5,7},{6,4},{7,5},{8,10},{9,11},{10,... | collective-permute-start | bytes 73736 | tf_op jit(solution)/shard_map/ppermute | solution.py:231
  4.2 4.2 %collective-permute-start.1 = (f32[2,24,128]{2,1,0:T(8,128)S(1)}, f32[2,24,128]{2,1,0:T(8,128)S(1)}, u32[]{:S(2)}, u32[]{:S(2)}) collective-permute-start(f32[2,24,128]{2,1,0:T(8,128)S(1)} %get-tuple-element.45), channel_id=1, source_target_pairs={{0,1},{1,0},{2,4},{3,5},{4,2},{5,3},{6,8},{7,9},{8,6},{9,7},{10,12... | collective-permute-start | bytes 73736 | tf_op jit(solution)/shard_map/ppermute | solution.py:231
  5.1 0.7 %copy-start = (s32[4,512]{1,0:T(4,128)S(1)}, s32[4,512]{1,0:T(4,128)}, u32[]{:S(2)}) copy-start(s32[4,512]{1,0:T(4,128)} %map_ref.7) | copy-start | bytes 24580
  5.8 9.1 %copy-start.2 = (f32[1024]{0:T(1024)S(1)}, f32[1024]{0:T(1024)}, u32[]{:S(2)}) copy-start(f32[1024]{0:T(1024)} %param.13) | copy-start | bytes 12292
  5.8 9.1 %copy-start.3 = (s32[1024]{0:T(1024)S(1)}, s32[1024]{0:T(1024)}, u32[]{:S(2)}) copy-start(s32[1024]{0:T(1024)} %param.14) | copy-start | bytes 12292
  5.8 9.1 %copy-start.4 = (f32[1024]{0:T(1024)S(1)}, f32[1024]{0:T(1024)}, u32[]{:S(2)}) copy-start(f32[1024]{0:T(1024)} %param.15) | copy-start | bytes 12292
  8.4 13.7 %copy-start.1 = (s32[4,512]{1,0:T(4,128)S(1)}, s32[4,512]{1,0:T(4,128)}, u32[]{:S(2)}) copy-start(s32[4,512]{1,0:T(4,128)} %map_ref.7) | copy-start | bytes 24580
  8.5 1.3 %collective-permute-start.2 = (f32[2,24,128]{2,1,0:T(8,128)S(1)}, f32[2,24,128]{2,1,0:T(8,128)S(1)}, u32[]{:S(2)}, u32[]{:S(2)}) collective-permute-start(f32[2,24,128]{2,1,0:T(8,128)S(1)} %pad_maximum_fusion), channel_id=1, source_target_pairs={{0,1},{1,0},{2,3},{3,2},{4,5},{5,4},{6,7},{7,6},{8,9},{9,8},{10,11... | collective-permute-start | bytes 73736 | tf_op jit(solution)/shard_map/ppermute | solution.py:239
  12.1 4.2 %collective-permute-start.3 = (f32[2,24,128]{2,1,0:T(8,128)S(1)}, f32[2,24,128]{2,1,0:T(8,128)S(1)}, u32[]{:S(2)}, u32[]{:S(2)}) collective-permute-start(f32[2,24,128]{2,1,0:T(8,128)S(1)} %get-tuple-element.56), channel_id=1, source_target_pairs={{0,2},{1,3},{2,0},{3,1},{4,6},{5,7},{6,4},{7,5},{8,10},{9,11},{10,... | collective-permute-start | bytes 73736 | tf_op jit(solution)/shard_map/ppermute | solution.py:231
  14.3 2.1 %collective-permute-start.4 = (f32[2,24,128]{2,1,0:T(8,128)S(1)}, f32[2,24,128]{2,1,0:T(8,128)S(1)}, u32[]{:S(2)}, u32[]{:S(2)}) collective-permute-start(f32[2,24,128]{2,1,0:T(8,128)S(1)} %get-tuple-element.57), channel_id=1, source_target_pairs={{0,1},{1,0},{2,4},{3,5},{4,2},{5,3},{6,8},{7,9},{8,6},{9,7},{10,12... | collective-permute-start | bytes 73736 | tf_op jit(solution)/shard_map/ppermute | solution.py:231
  16.4 1.3 %collective-permute-start.5 = (f32[2,24,128]{2,1,0:T(8,128)S(1)}, f32[2,24,128]{2,1,0:T(8,128)S(1)}, u32[]{:S(2)}, u32[]{:S(2)}) collective-permute-start(f32[2,24,128]{2,1,0:T(8,128)S(1)} %pad_maximum_fusion.1), channel_id=1, source_target_pairs={{0,1},{1,0},{2,3},{3,2},{4,5},{5,4},{6,7},{7,6},{8,9},{9,8},{10,11... | collective-permute-start | bytes 73736 | tf_op jit(solution)/shard_map/ppermute | solution.py:239
  18.3 4.8 %collective-permute-start.6 = (f32[2,24,128]{2,1,0:T(8,128)S(1)}, f32[2,24,128]{2,1,0:T(8,128)S(1)}, u32[]{:S(2)}, u32[]{:S(2)}) collective-permute-start(f32[2,24,128]{2,1,0:T(8,128)S(1)} %get-tuple-element.67), channel_id=1, source_target_pairs={{0,2},{1,3},{2,0},{3,1},{4,6},{5,7},{6,4},{7,5},{8,10},{9,11},{10,... | collective-permute-start | bytes 73736 | tf_op jit(solution)/shard_map/ppermute | solution.py:231
  21.5 1.6 %collective-permute-start.7 = (f32[2,24,128]{2,1,0:T(8,128)S(1)}, f32[2,24,128]{2,1,0:T(8,128)S(1)}, u32[]{:S(2)}, u32[]{:S(2)}) collective-permute-start(f32[2,24,128]{2,1,0:T(8,128)S(1)} %get-tuple-element.68), channel_id=1, source_target_pairs={{0,1},{1,0},{2,4},{3,5},{4,2},{5,3},{6,8},{7,9},{8,6},{9,7},{10,12... | collective-permute-start | bytes 73736 | tf_op jit(solution)/shard_map/ppermute | solution.py:231
  23.1 1.8 %collective-permute-start.8 = (f32[2,24,128]{2,1,0:T(8,128)S(1)}, f32[2,24,128]{2,1,0:T(8,128)S(1)}, u32[]{:S(2)}, u32[]{:S(2)}) collective-permute-start(f32[2,24,128]{2,1,0:T(8,128)S(1)} %pad_maximum_fusion.2), channel_id=1, source_target_pairs={{0,1},{1,0},{2,3},{3,2},{4,5},{5,4},{6,7},{7,6},{8,9},{9,8},{10,11... | collective-permute-start | bytes 73736 | tf_op jit(solution)/shard_map/ppermute | solution.py:239
  27.8 23.6 %collective-permute-start.9 = (f32[2,24,128]{2,1,0:T(8,128)S(1)}, f32[2,24,128]{2,1,0:T(8,128)S(1)}, u32[]{:S(2)}, u32[]{:S(2)}) collective-permute-start(f32[2,24,128]{2,1,0:T(8,128)S(1)} %get-tuple-element.78), channel_id=1, source_target_pairs={{0,2},{1,3},{2,0},{3,1},{4,6},{5,7},{6,4},{7,5},{8,10},{9,11},{10,... | collective-permute-start | bytes 73736 | tf_op jit(solution)/shard_map/ppermute | solution.py:231
  31.7 19.7 %collective-permute-start.10 = (f32[2,24,128]{2,1,0:T(8,128)S(1)}, f32[2,24,128]{2,1,0:T(8,128)S(1)}, u32[]{:S(2)}, u32[]{:S(2)}) collective-permute-start(f32[2,24,128]{2,1,0:T(8,128)S(1)} %get-tuple-element.79), channel_id=1, source_target_pairs={{0,1},{1,0},{2,4},{3,5},{4,2},{5,3},{6,8},{7,9},{8,6},{9,7},{10,12... | collective-permute-start | bytes 73736 | tf_op jit(solution)/shard_map/ppermute | solution.py:231
  32.4 27.2 %all-to-all-start = ((f32[128,1,128]{2,1,0:T(1,128)}), f32[128,1,128]{2,1,0:T(1,128)S(1)}, u32[]{:S(2)}, u32[]{:S(2)}) async-start(f32[128,1,128]{2,1,0:T(1,128)} %get-tuple-element.85), calls=%async_computation | async-start | bytes 131072 | tf_op jit(solution)/shard_map/all_to_all | solution.py:282
  51.4 2.0 %collective-permute-start.11 = (f32[2,24,128]{2,1,0:T(8,128)S(1)}, f32[2,24,128]{2,1,0:T(8,128)S(1)}, u32[]{:S(2)}, u32[]{:S(2)}) collective-permute-start(f32[2,24,128]{2,1,0:T(8,128)S(1)} %pad_maximum_fusion.3), channel_id=1, source_target_pairs={{0,1},{1,0},{2,3},{3,2},{4,5},{5,4},{6,7},{7,6},{8,9},{9,8},{10,11... | collective-permute-start | bytes 73736 | tf_op jit(solution)/shard_map/ppermute | solution.py:239

commit v5 on v4

--- a/solution.py
+++ b/solution.py
@@ -83,10 +83,13 @@
 
 
 def total(x):
-    return jnp.sum(jnp.sum(x, axis=0, keepdims=True), axis=1, keepdims=True)
-
-
-def send_kernel(count_ref, field_ref, index_ref, near_ref, far_ref, mid_ref, share_ref, padded_ref):
+    folded = sum(x[:, at : at + 128] for at in range(0, x.shape[1], 128))
+    folded = sum(folded[at : at + 8] for at in range(0, x.shape[0], 8))
+    return jnp.sum(jnp.sum(folded, axis=0, keepdims=True), axis=1, keepdims=True)
+
+
+def send_kernel(count_ref, field_ref, index_ref, map_ref, mass_ref, absorbing_ref, impedance_ref, *refs):
+    near_ref, far_ref, mid_ref, share_ref, padded_ref, map_out, diagonal_ref = refs
     for k in range(NB):
         rows = lax.broadcasted_iota(jnp.int32, (F, GH), 0)
         lanes = lax.broadcasted_iota(jnp.int32, (1, GH), 1)
@@ -95,6 +98,8 @@
     padded_ref[TR:, :] = jnp.zeros((TP - TR, F), F32)
     padded_ref[:TR, :] = field_ref[...]
     write_blocks(split(pick(padded_ref[...], share_ref[...])), near_ref, far_ref, mid_ref)
+    map_out[...] = map_ref[...]
+    diagonal_ref[...] = mass_ref[...] + absorbing_ref[...].astype(F32) * impedance_ref[...]
 
 
 def fill_selector(map_ref, sel_ref, first):
@@ -104,17 +109,21 @@
         sel_ref[:, s * E : (s + 1) * E] = jnp.where(rows == map_ref[s : s + 1, :], 1.0, 0.0).astype(BF16)
 
 
-def select_kernel(map_ref, field_ref, matrix_ref, ghost_sel_ref, local_ref, held_ref, sel_ref, sem):
+def select_kernel(map_ref, field_ref, matrix_ref, ghost_sel_ref, local_ref, wide_ref, sel_ref, held_ref, sem):
     copy = pltpu.make_async_copy(matrix_ref, held_ref, sem)
     copy.start()
     fill_selector(map_ref, sel_ref, 0)
     local_ref[...] = pick(field_ref[...], sel_ref[...])
     fill_selector(map_ref, ghost_sel_ref, F)
     copy.wait()
+    for j in range(DOFS):
+        for t in range(E // 128):
+            wide_ref[t, j] = held_ref[j, :, t * 128 : (t + 1) * 128].astype(F32)
 
 
 def product_kernel(near_ref, far_ref, mid_ref, sel_ref, matrix_ref, local_ref, *refs):
-    near_out, far_out, mid_out, spread_ref, pick_ref, ghost_ref, prod_ref = refs[-7:]
+    last = len(refs) > 7
+    near_out, far_out, mid_out, spread_ref, pick_ref, ghost_ref, prod_ref = refs[3:10] if last else refs
     for k, block in enumerate(read_blocks(near_ref, far_ref, mid_ref)):
         ghost_ref[:, k * GH : (k + 1) * GH] = block
     pick_ref[...] = local_ref[...] + pick(ghost_ref[...], sel_ref[...])
@@ -123,30 +132,37 @@
         for j in range(DOFS):
             s, c = divmod(j, TR)
             row = pick_ref[c : c + 1, s * E + t * 128 : s * E + (t + 1) * 128]
-            acc = acc + matrix_ref[j, :, t * 128 : (t + 1) * 128].astype(F32) * row
+            acc = acc + matrix_ref[t, j] * row
         prod_ref[:, t * 128 : (t + 1) * 128] = acc
     spread_ref[TR:, :] = jnp.zeros((TP - TR, PICKS), F32)
     for s in range(SIDES):
         spread_ref[:TR, s * E : (s + 1) * E] = prod_ref[s * TR : (s + 1) * TR, :]
-    parts = split(spread_out(spread_ref[...], sel_ref[...]))
-    write_blocks(parts[::-1], near_out, far_out, mid_out)
-    if len(refs) == 10:
-        first_ref, second_ref, row_ref = refs[:3]
+    if last:
+        first_ref, second_ref, row_out = refs[:3]
+        row_ref, sem = refs[10:]
         lane = lax.broadcasted_iota(jnp.int32, (1, GH), 1)
         energy = total(spread_ref[...] * pick_ref[...])
         row = first_ref[...] + second_ref[...] + jnp.where(lane == 3, energy, 0.0)
         row_ref[...] = jnp.broadcast_to(row[None], row_ref.shape)
-
-
-def diagonal_of(mass_ref, absorbing_ref, impedance_ref):
-    return mass_ref[...] + absorbing_ref[...].astype(F32) * impedance_ref[...]
-
-
-def own_kernel(spread_ref, map_ref, field_ref, mass_ref, absorbing_ref, impedance_ref, *refs):
+        copy = pltpu.make_async_copy(row_ref, row_out, sem)
+        copy.start()
+
+    def send_back():
+        parts = split(spread_out(spread_ref[...], sel_ref[...]))
+        write_blocks(parts[::-1], near_out, far_out, mid_out)
+
+    if last:
+        pl.when(lax.axis_index(DOM) >= 0)(send_back)
+        copy.wait()
+    else:
+        send_back()
+
+
+def own_kernel(spread_ref, map_ref, field_ref, diagonal_ref, *refs):
     own_ref, sel_ref = refs[-2:]
     fill_selector(map_ref, sel_ref, 0)
     field = field_ref[...]
-    damped = diagonal_of(mass_ref, absorbing_ref, impedance_ref) * field
+    damped = diagonal_ref[...] * field
     if len(refs) == 4:
         pick_ref, sums_ref = refs[:2]
         energy = total(damped * field) + total(pick_ref[...] * spread_ref[...])
@@ -162,12 +178,12 @@
     write_blocks(split(pick(image, share_ref[...])), near_out, far_out, mid_out)
 
 
-def local_kernel(image_ref, map_ref, mass_ref, absorbing_ref, impedance_ref, local_ref, sums_ref, sel_ref):
+def local_kernel(image_ref, map_ref, diagonal_ref, local_ref, sums_ref, sel_ref):
     fill_selector(map_ref, sel_ref, 0)
     image = image_ref[...]
     local_ref[...] = pick(image, sel_ref[...])
     square = image * image
-    weighted = diagonal_of(mass_ref, absorbing_ref, impedance_ref) * square
+    weighted = diagonal_ref[...] * square
     sums_ref[...] = lanes_of([0.0, 0.0, total(square), total(weighted)])
 
 
@@ -201,13 +217,13 @@
 ANY = pl.ANY
 
 
-def call(kernel, out_shape, *args, scratch=(), held=VMEM, last=VMEM):
+def call(kernel, out_shape, *args, scratch=(), held=VMEM, last=VMEM, first=VMEM):
     spaces = [VMEM] * (len(args) - 1) + [last]
     args = [pltpu.with_memory_space_constraint(a, pltpu.HBM if m is ANY else held) for a, m in zip(args, spaces)]
     return pl.pallas_call(
         kernel,
         in_specs=[pl.BlockSpec(memory_space=m) for m in spaces],
-        out_specs=jax.tree.map(lambda _: pl.BlockSpec(memory_space=VMEM), out_shape),
+        out_specs=tuple(pl.BlockSpec(memory_space=VMEM if at else first) for at in range(len(out_shape))),
         out_shape=out_shape,
         scratch_shapes=scratch,
         compiler_params=pltpu.CompilerParams(vmem_limit_bytes=16 * 1024 * 1024),
@@ -219,7 +235,6 @@
 ):
     count = lax.axis_size(DOM)
     core, odd = place()
-    diagonal = [x.reshape(1, F) for x in (face_mass, absorbing, impedance)]
     chips = count // 2
 
     def swap(value, partner_of):
@@ -239,18 +254,27 @@
         got_mid = lax.ppermute(pair, DOM, [(i, i ^ 1) for i in range(count)])
         return (got_near, got_far, got_mid), beside
 
-    *sent, share, padded = call(
-        send_kernel, MESSAGE + (VMEM((F, SHARED), BF16), FACES), share_count, right_side, share_index[0], held=pltpu.HBM
+    *sent, share, padded, held_map, diagonal = call(
+        send_kernel,
+        MESSAGE + (VMEM((F, SHARED), BF16), FACES, VMEM((SIDES, E), jnp.int32), VMEM((1, F), F32)),
+        share_count,
+        right_side,
+        share_index[0],
+        face_map,
+        face_mass.reshape(1, F),
+        absorbing.reshape(1, F),
+        impedance.reshape(1, F),
+        held=pltpu.HBM,
     )
 
     def select():
         return call(
             select_kernel,
-            (VMEM((SHARED, PICKS), BF16), WIDE, VMEM((DOFS, DOFS, E), BF16)),
-            face_map,
+            (VMEM((SHARED, PICKS), BF16), WIDE, VMEM((E // 128, DOFS, DOFS, 128), F32)),
+            held_map,
             padded,
             element_matrix,
-            scratch=[OWN_SELECTOR, pltpu.SemaphoreType.DMA],
+            scratch=[OWN_SELECTOR, VMEM((DOFS, DOFS, E), BF16), pltpu.SemaphoreType.DMA],
             last=ANY,
         )
 
@@ -259,13 +283,13 @@
     *sent, spread, picked = call(product_kernel, MESSAGE + (WIDE, WIDE), *got, selector, matrix, local, scratch=scratch)
 
     def own0():
-        return call(own_kernel, (ROW, FACES), spread, face_map, padded, *diagonal, picked, scratch=[OWN_SELECTOR])
+        return call(own_kernel, (ROW, FACES), spread, held_map, padded, diagonal, picked, scratch=[OWN_SELECTOR])
 
     got, (sums0, own) = exchange(*sent, own0)
     image, *sent = call(combine_kernel, (FACES,) + MESSAGE, own, *got, share, scratch=[GHOSTS])
 
     def local1():
-        return call(local_kernel, (WIDE, ROW), image, face_map, *diagonal, scratch=[OWN_SELECTOR])
+        return call(local_kernel, (WIDE, ROW), image, held_map, diagonal, scratch=[OWN_SELECTOR])
 
     got, (local, sums1) = exchange(*sent, local1)
     row, *sent, spread = call(
@@ -277,14 +301,15 @@
         local,
         sums0,
         sums1,
-        scratch=[WIDE] + scratch,
+        scratch=[WIDE] + scratch + [VMEM((count, 1, GH), F32), pltpu.SemaphoreType.DMA],
+        first=ANY,
     )
     row = lax.all_to_all(row, DOM, 0, 0)
 
     def own1():
-        return call(own_kernel, FACES, spread, face_map, image, *diagonal, scratch=[OWN_SELECTOR])
-
-    got, own = exchange(*sent, own1)
+        return call(own_kernel, (FACES,), spread, held_map, image, diagonal, scratch=[OWN_SELECTOR])
+
+    got, (own,) = exchange(*sent, own1)
     out = jax.ShapeDtypeStruct((TR, F), F32)
     return call(final_kernel, (out, out), own, *got, share, padded, image, row, scratch=[GHOSTS])
 

time: 60.9 us -> 59.7 us (0.980)
  local copies, waits for them, and re-layouts: 0.71 us -> 0 us
  Pallas kernels: 14.7 us -> 14 us
    pallas_call x9, Pallas kernels: 14.7 us -> 14 us  [call(): pl.pallas_call(kernel, in_specs=[pl.BlockSpec(memory_space=m) for m in sp...]
    unnamed x10 -> x0, local copies, waits for them, and re-layouts: 0.71 us -> none
  transfers between devices with their start and end apart: 13 -> 13, of which waited for: 5 -> 5; matrix products, arithmetic and copies ran while one was open for 0% -> 0% of each run, Pallas kernels for 10% -> 12%
where the time goes in v5:
time: 59.7 us; the launch traced here: 59.5 us
  starting transfers between devices  34.8 us (58%)
  Pallas kernels  14 us (23%)
  waiting for transfers between devices  9.88 us (17%)
  between operations  0.83 us (1%)
    all_to_all x1, starting transfers between devices, shards(): row = lax.all_to_all(row, DOM, 0, 0)  17.7 us
    ppermute x8, starting transfers between devices, swap(): return lax.ppermute(value, DOM, pairs)  14.4 us
    pallas_call x9, Pallas kernels, call(): pl.pallas_call(kernel, in_specs=[pl.BlockSpec(memory_space=m) for m in sp...  14 us
    all_to_all x1, waiting for transfers between devices, shards(): row = lax.all_to_all(row, DOM, 0, 0)  6.12 us
    ppermute x4, waiting for transfers between devices, exchange(): got_mid = lax.ppermute(pair, DOM, [(i, i ^ 1) for i in range(count)])  3.73 us
    ppermute x4, starting transfers between devices, exchange(): got_mid = lax.ppermute(pair, DOM, [(i, i ^ 1) for i in range(count)])  2.66 us
  transfers between devices with their start and end apart: 13, of which 5 were waited for; matrix products, arithmetic and copies ran while one was open for 0% of the time, Pallas kernels for 12%

profile of v5, /device:TPU:1, one launch (start us, length us, event | category | flops | bytes accessed | tf_op | source)
XLA Modules:
  0.0 59.5 jit_solution(3972573858060303321)
XLA Ops:
  0.6 1.4 %shard_map.95 = (f32[2,24,128]{2,1,0:T(8,128)S(1)}, f32[2,24,128]{2,1,0:T(8,128)S(1)}, f32[24,128]{1,0:T(8,128)S(1)}, bf16[1024,512]{1,0:T(8,128)(2,1)S(1)}, f32...) custom-call(s32[1,4]{1,0:T(1,128)} %count_ref.1, f32[18,1024]{1,0:T(8,128)} %field_ref.1, ...), custom_call_target="tpu_custom_call" | custom-call | tf_op jit(solution)/shard_map/pallas_call | solution.py:223
  2.1 2.1 %collective-permute-start = (f32[2,24,128]{2,1,0:T(8,128)S(1)}, f32[2,24,128]{2,1,0:T(8,128)S(1)}, u32[]{:S(2)}, u32[]{:S(2)}) collective-permute-start(f32[2,24,128]{2,1,0:T(8,128)S(1)} %get-tuple-element.46), channel_id=1, source_target_pairs={{0,2},{1,3},{2,0},{3,1},{4,6},{5,7},{6,4},{7,5},{8,10},{9,11},{10,... | collective-permute-start | bytes 73736 | tf_op jit(solution)/shard_map/ppermute | solution.py:246
  4.2 1.0 %collective-permute-start.1 = (f32[2,24,128]{2,1,0:T(8,128)S(1)}, f32[2,24,128]{2,1,0:T(8,128)S(1)}, u32[]{:S(2)}, u32[]{:S(2)}) collective-permute-start(f32[2,24,128]{2,1,0:T(8,128)S(1)} %get-tuple-element.47), channel_id=1, source_target_pairs={{0,1},{1,0},{2,4},{3,5},{4,2},{5,3},{6,8},{7,9},{8,6},{9,7},{10,12... | collective-permute-start | bytes 73736 | tf_op jit(solution)/shard_map/ppermute | solution.py:246
  5.2 3.2 %shard_map.96 = (bf16[512,2048]{1,0:T(8,128)(2,1)S(1)}, f32[24,2048]{1,0:T(8,128)S(1)}, f32[4,72,72,128]{3,2,1,0:T(8,128)S(1)}) custom-call(s32[4,512]{1,0:T(4,128)S(1)} %get-tuple-element.48.map_ref, f32[24,1024]{1,0:T(8,128)S(1)} %get-tuple-element.49.field_ref, bf16[72,72,512]{2,1,0:T(8,128)(2,1)} %matrix_ref.1), custom_call_target="tpu_custom_call" | custom-call | tf_op jit(solution)/shard_map/pallas_call | solution.py:223
  8.5 1.2 %collective-permute-done.2.mid_ref = f32[2,24,128]{2,1,0:T(8,128)S(1)} collective-permute-done((f32[2,24,128]{2,1,0:T(8,128)S(1)}, f32[2,24,128]{2,1,0:T(8,128)S(1)}, u32[]{:S(2)}, u32[]{:S(2)}) %collective-permute-start.2) | collective-permute-done | bytes 24608 | tf_op jit(solution)/shard_map/ppermute | solution.py:254
  9.7 1.9 %shard_map.97 = (f32[2,24,128]{2,1,0:T(8,128)S(1)}, f32[2,24,128]{2,1,0:T(8,128)S(1)}, f32[24,128]{1,0:T(8,128)S(1)}, f32[24,2048]{1,0:T(8,128)S(1)}, f32[24,2048]{1,0:T(8,128)S(1)}) custom-call(f32[2,24,128]{2,1,0:T(8,128)S(1)} %collective-permute-done.near_ref, f32[2,24,128]{2,1,0:T(8,128)S(1)} %collective-permute-done.1.far_ref, ...), custom_call_target="tpu_custom_call" | custom-call | tf_op jit(solution)/shard_map/pallas_call | solution.py:223
  11.6 2.1 %collective-permute-start.3 = (f32[2,24,128]{2,1,0:T(8,128)S(1)}, f32[2,24,128]{2,1,0:T(8,128)S(1)}, u32[]{:S(2)}, u32[]{:S(2)}) collective-permute-start(f32[2,24,128]{2,1,0:T(8,128)S(1)} %get-tuple-element.59), channel_id=1, source_target_pairs={{0,2},{1,3},{2,0},{3,1},{4,6},{5,7},{6,4},{7,5},{8,10},{9,11},{10,... | collective-permute-start | bytes 73736 | tf_op jit(solution)/shard_map/ppermute | solution.py:246
  13.7 0.6 %collective-permute-start.4 = (f32[2,24,128]{2,1,0:T(8,128)S(1)}, f32[2,24,128]{2,1,0:T(8,128)S(1)}, u32[]{:S(2)}, u32[]{:S(2)}) collective-permute-start(f32[2,24,128]{2,1,0:T(8,128)S(1)} %get-tuple-element.60), channel_id=1, source_target_pairs={{0,1},{1,0},{2,4},{3,5},{4,2},{5,3},{6,8},{7,9},{8,6},{9,7},{10,12... | collective-permute-start | bytes 73736 | tf_op jit(solution)/shard_map/ppermute | solution.py:246
  14.4 1.4 %shard_map.98 = (f32[1,128]{1,0:T(1,128)S(1)}, f32[24,1024]{1,0:T(8,128)S(1)}) custom-call(f32[24,2048]{1,0:T(8,128)S(1)} %get-tuple-element.61.spread_ref, s32[4,512]{1,0:T(4,128)S(1)} %get-tuple-element.48.map_ref, f32[24,1024]{1,0:T(8,128)S(1)} %get-tuple-element.49.field_ref, f32[1,1024]{1,0:T(1,128)S(1)} %get-tuple-element.62.diagonal_ref, ...), custom_call_target="tpu_custom_call" | custom-call | tf_op jit(solution)/shard_map/pallas_call | solution.py:223
  16.3 0.8 %collective-permute-done.5.mid_ref = f32[2,24,128]{2,1,0:T(8,128)S(1)} collective-permute-done((f32[2,24,128]{2,1,0:T(8,128)S(1)}, f32[2,24,128]{2,1,0:T(8,128)S(1)}, u32[]{:S(2)}, u32[]{:S(2)}) %collective-permute-start.5) | collective-permute-done | bytes 24608 | tf_op jit(solution)/shard_map/ppermute | solution.py:254
  17.7 3.3 %collective-permute-start.6 = (f32[2,24,128]{2,1,0:T(8,128)S(1)}, f32[2,24,128]{2,1,0:T(8,128)S(1)}, u32[]{:S(2)}, u32[]{:S(2)}) collective-permute-start(f32[2,24,128]{2,1,0:T(8,128)S(1)} %get-tuple-element.71), channel_id=1, source_target_pairs={{0,2},{1,3},{2,0},{3,1},{4,6},{5,7},{6,4},{7,5},{8,10},{9,11},{10,... | collective-permute-start | bytes 73736 | tf_op jit(solution)/shard_map/ppermute | solution.py:246
  21.0 0.6 %collective-permute-start.7 = (f32[2,24,128]{2,1,0:T(8,128)S(1)}, f32[2,24,128]{2,1,0:T(8,128)S(1)}, u32[]{:S(2)}, u32[]{:S(2)}) collective-permute-start(f32[2,24,128]{2,1,0:T(8,128)S(1)} %get-tuple-element.72), channel_id=1, source_target_pairs={{0,1},{1,0},{2,4},{3,5},{4,2},{5,3},{6,8},{7,9},{8,6},{9,7},{10,12... | collective-permute-start | bytes 73736 | tf_op jit(solution)/shard_map/ppermute | solution.py:246
  21.7 0.9 %shard_map.100 = (f32[24,2048]{1,0:T(8,128)S(1)}, f32[1,128]{1,0:T(1,128)S(1)}) custom-call(f32[24,1024]{1,0:T(8,128)S(1)} %get-tuple-element.73.image_ref.field_ref, s32[4,512]{1,0:T(4,128)S(1)} %get-tuple-element.48.map_ref, f32[1,1024]{1,0:T(1,128)S(1)} %get-tuple-element.62.diagonal_ref), custom_call_target="tpu_custom_call" | custom-call | tf_op jit(solution)/shard_map/pallas_call | solution.py:223
  22.6 1.0 %collective-permute-start.8 = (f32[2,24,128]{2,1,0:T(8,128)S(1)}, f32[2,24,128]{2,1,0:T(8,128)S(1)}, u32[]{:S(2)}, u32[]{:S(2)}) collective-permute-start(f32[2,24,128]{2,1,0:T(8,128)S(1)} %pad_maximum_fusion.2), channel_id=1, source_target_pairs={{0,1},{1,0},{2,3},{3,2},{4,5},{5,4},{6,7},{7,6},{8,9},{9,8},{10,11... | collective-permute-start | bytes 73736 | tf_op jit(solution)/shard_map/ppermute | solution.py:254
  23.6 0.8 %collective-permute-done.8.mid_ref = f32[2,24,128]{2,1,0:T(8,128)S(1)} collective-permute-done((f32[2,24,128]{2,1,0:T(8,128)S(1)}, f32[2,24,128]{2,1,0:T(8,128)S(1)}, u32[]{:S(2)}, u32[]{:S(2)}) %collective-permute-start.8) | collective-permute-done | bytes 24608 | tf_op jit(solution)/shard_map/ppermute | solution.py:254
  24.4 2.1 %shard_map.101 = (f32[128,1,128]{2,1,0:T(1,128)}, f32[2,24,128]{2,1,0:T(8,128)S(1)}, f32[2,24,128]{2,1,0:T(8,128)S(1)}, f32[24,128]{1,0:T(8,128)S(1)}, f32[24,2048]{1,0:T(8,128)S(1)}) custom-call(f32[2,24,128]{2,1,0:T(8,128)S(1)} %collective-permute-done.6.near_ref, f32[2,24,128]{2,1,0:T(8,128)S(1)} %collective-permute-done.7.far_ref, ...), custom_call_target="tpu_custom_call" | custom-call | tf_op jit(solution)/shard_map/pallas_call | solution.py:223
  26.5 4.0 %collective-permute-start.9 = (f32[2,24,128]{2,1,0:T(8,128)S(1)}, f32[2,24,128]{2,1,0:T(8,128)S(1)}, u32[]{:S(2)}, u32[]{:S(2)}) collective-permute-start(f32[2,24,128]{2,1,0:T(8,128)S(1)} %get-tuple-element.82), channel_id=1, source_target_pairs={{0,2},{1,3},{2,0},{3,1},{4,6},{5,7},{6,4},{7,5},{8,10},{9,11},{10,... | collective-permute-start | bytes 73736 | tf_op jit(solution)/shard_map/ppermute | solution.py:246
  30.5 0.6 %collective-permute-start.10 = (f32[2,24,128]{2,1,0:T(8,128)S(1)}, f32[2,24,128]{2,1,0:T(8,128)S(1)}, u32[]{:S(2)}, u32[]{:S(2)}) collective-permute-start(f32[2,24,128]{2,1,0:T(8,128)S(1)} %get-tuple-element.83), channel_id=1, source_target_pairs={{0,1},{1,0},{2,4},{3,5},{4,2},{5,3},{6,8},{7,9},{8,6},{9,7},{10,12... | collective-permute-start | bytes 73736 | tf_op jit(solution)/shard_map/ppermute | solution.py:246
  31.1 17.7 %all-to-all-start = ((f32[128,1,128]{2,1,0:T(1,128)}), f32[128,1,128]{2,1,0:T(1,128)S(1)}, u32[]{:S(2)}, u32[]{:S(2)}) async-start(f32[128,1,128]{2,1,0:T(1,128)} %get-tuple-element.89), calls=%async_computation | async-start | bytes 131072 | tf_op jit(solution)/shard_map/all_to_all | solution.py:307
  48.8 1.4 %shard_map.102.own_ref = f32[24,1024]{1,0:T(8,128)S(1)} custom-call(f32[24,2048]{1,0:T(8,128)S(1)} %get-tuple-element.84.spread_ref, s32[4,512]{1,0:T(4,128)S(1)} %get-tuple-element.48.map_ref, f32[24,1024]{1,0:T(8,128)S(1)} %get-tuple-element.73.image_ref.field_ref, f32[1,1024]{1,0:T(1,128)S(1)} %get-tuple-element.62.diagonal_ref), custom_call_target="tpu_custom_call" | custom-call | tf_op jit(solution)/shard_map/pallas_call | solution.py:223
  50.3 1.1 %collective-permute-start.11 = (f32[2,24,128]{2,1,0:T(8,128)S(1)}, f32[2,24,128]{2,1,0:T(8,128)S(1)}, u32[]{:S(2)}, u32[]{:S(2)}) collective-permute-start(f32[2,24,128]{2,1,0:T(8,128)S(1)} %pad_maximum_fusion.3), channel_id=1, source_target_pairs={{0,1},{1,0},{2,3},{3,2},{4,5},{5,4},{6,7},{7,6},{8,9},{9,8},{10,11... | collective-permute-start | bytes 73736 | tf_op jit(solution)/shard_map/ppermute | solution.py:254
  51.4 0.8 %collective-permute-done.11.mid_ref = f32[2,24,128]{2,1,0:T(8,128)S(1)} collective-permute-done((f32[2,24,128]{2,1,0:T(8,128)S(1)}, f32[2,24,128]{2,1,0:T(8,128)S(1)}, u32[]{:S(2)}, u32[]{:S(2)}) %collective-permute-start.11) | collective-permute-done | bytes 24608 | tf_op jit(solution)/shard_map/ppermute | solution.py:254
  52.3 6.1 %all-to-all-done.sums_ref = f32[128,1,128]{2,1,0:T(1,128)S(1)} async-done(((f32[128,1,128]{2,1,0:T(1,128)}), f32[128,1,128]{2,1,0:T(1,128)S(1)}, u32[]{:S(2)}, u32[]{:S(2)}) %all-to-all-start) | async-done | bytes 65568 | tf_op jit(solution)/shard_map/all_to_all | solution.py:307
  58.4 1.1 %shard_map.103 = (f32[18,1024]{1,0:T(8,128)}, f32[18,1024]{1,0:T(8,128)}) custom-call(f32[24,1024]{1,0:T(8,128)S(1)} %shard_map.102.own_ref, f32[2,24,128]{2,1,0:T(8,128)S(1)} %collective-permute-done.9.near_ref, f32[2,24,128]{2,1,0:T(8,128)S(1)} %collective-permute-done.10.far_ref, f32[2,24,128]{2,1,0:T(8,128)S(1)} %collective-permute-done.11.mid_ref, ...), custom_call_target="tpu_custom_call" | custom-call | tf_op jit(solution)/shard_map/pallas_call | solution.py:223
  (19 shorter events, 1.2 us)
Async XLA Ops:
  2.1 6.3 %collective-permute-start = (f32[2,24,128]{2,1,0:T(8,128)S(1)}, f32[2,24,128]{2,1,0:T(8,128)S(1)}, u32[]{:S(2)}, u32[]{:S(2)}) collective-permute-start(f32[2,24,128]{2,1,0:T(8,128)S(1)} %get-tuple-element.46), channel_id=1, source_target_pairs={{0,2},{1,3},{2,0},{3,1},{4,6},{5,7},{6,4},{7,5},{8,10},{9,11},{10,... | collective-permute-start | bytes 73736 | tf_op jit(solution)/shard_map/ppermute | solution.py:246
  4.2 4.2 %collective-permute-start.1 = (f32[2,24,128]{2,1,0:T(8,128)S(1)}, f32[2,24,128]{2,1,0:T(8,128)S(1)}, u32[]{:S(2)}, u32[]{:S(2)}) collective-permute-start(f32[2,24,128]{2,1,0:T(8,128)S(1)} %get-tuple-element.47), channel_id=1, source_target_pairs={{0,1},{1,0},{2,4},{3,5},{4,2},{5,3},{6,8},{7,9},{8,6},{9,7},{10,12... | collective-permute-start | bytes 73736 | tf_op jit(solution)/shard_map/ppermute | solution.py:246
  8.4 1.3 %collective-permute-start.2 = (f32[2,24,128]{2,1,0:T(8,128)S(1)}, f32[2,24,128]{2,1,0:T(8,128)S(1)}, u32[]{:S(2)}, u32[]{:S(2)}) collective-permute-start(f32[2,24,128]{2,1,0:T(8,128)S(1)} %pad_maximum_fusion), channel_id=1, source_target_pairs={{0,1},{1,0},{2,3},{3,2},{4,5},{5,4},{6,7},{7,6},{8,9},{9,8},{10,11... | collective-permute-start | bytes 73736 | tf_op jit(solution)/shard_map/ppermute | solution.py:254
  11.6 4.2 %collective-permute-start.3 = (f32[2,24,128]{2,1,0:T(8,128)S(1)}, f32[2,24,128]{2,1,0:T(8,128)S(1)}, u32[]{:S(2)}, u32[]{:S(2)}) collective-permute-start(f32[2,24,128]{2,1,0:T(8,128)S(1)} %get-tuple-element.59), channel_id=1, source_target_pairs={{0,2},{1,3},{2,0},{3,1},{4,6},{5,7},{6,4},{7,5},{8,10},{9,11},{10,... | collective-permute-start | bytes 73736 | tf_op jit(solution)/shard_map/ppermute | solution.py:246
  13.7 2.0 %collective-permute-start.4 = (f32[2,24,128]{2,1,0:T(8,128)S(1)}, f32[2,24,128]{2,1,0:T(8,128)S(1)}, u32[]{:S(2)}, u32[]{:S(2)}) collective-permute-start(f32[2,24,128]{2,1,0:T(8,128)S(1)} %get-tuple-element.60), channel_id=1, source_target_pairs={{0,1},{1,0},{2,4},{3,5},{4,2},{5,3},{6,8},{7,9},{8,6},{9,7},{10,12... | collective-permute-start | bytes 73736 | tf_op jit(solution)/shard_map/ppermute | solution.py:246
  15.8 1.3 %collective-permute-start.5 = (f32[2,24,128]{2,1,0:T(8,128)S(1)}, f32[2,24,128]{2,1,0:T(8,128)S(1)}, u32[]{:S(2)}, u32[]{:S(2)}) collective-permute-start(f32[2,24,128]{2,1,0:T(8,128)S(1)} %pad_maximum_fusion.1), channel_id=1, source_target_pairs={{0,1},{1,0},{2,3},{3,2},{4,5},{5,4},{6,7},{7,6},{8,9},{9,8},{10,11... | collective-permute-start | bytes 73736 | tf_op jit(solution)/shard_map/ppermute | solution.py:254
  17.7 4.8 %collective-permute-start.6 = (f32[2,24,128]{2,1,0:T(8,128)S(1)}, f32[2,24,128]{2,1,0:T(8,128)S(1)}, u32[]{:S(2)}, u32[]{:S(2)}) collective-permute-start(f32[2,24,128]{2,1,0:T(8,128)S(1)} %get-tuple-element.71), channel_id=1, source_target_pairs={{0,2},{1,3},{2,0},{3,1},{4,6},{5,7},{6,4},{7,5},{8,10},{9,11},{10,... | collective-permute-start | bytes 73736 | tf_op jit(solution)/shard_map/ppermute | solution.py:246
  21.0 1.5 %collective-permute-start.7 = (f32[2,24,128]{2,1,0:T(8,128)S(1)}, f32[2,24,128]{2,1,0:T(8,128)S(1)}, u32[]{:S(2)}, u32[]{:S(2)}) collective-permute-start(f32[2,24,128]{2,1,0:T(8,128)S(1)} %get-tuple-element.72), channel_id=1, source_target_pairs={{0,1},{1,0},{2,4},{3,5},{4,2},{5,3},{6,8},{7,9},{8,6},{9,7},{10,12... | collective-permute-start | bytes 73736 | tf_op jit(solution)/shard_map/ppermute | solution.py:246
  22.6 1.8 %collective-permute-start.8 = (f32[2,24,128]{2,1,0:T(8,128)S(1)}, f32[2,24,128]{2,1,0:T(8,128)S(1)}, u32[]{:S(2)}, u32[]{:S(2)}) collective-permute-start(f32[2,24,128]{2,1,0:T(8,128)S(1)} %pad_maximum_fusion.2), channel_id=1, source_target_pairs={{0,1},{1,0},{2,3},{3,2},{4,5},{5,4},{6,7},{7,6},{8,9},{9,8},{10,11... | collective-permute-start | bytes 73736 | tf_op jit(solution)/shard_map/ppermute | solution.py:254
  26.5 23.8 %collective-permute-start.9 = (f32[2,24,128]{2,1,0:T(8,128)S(1)}, f32[2,24,128]{2,1,0:T(8,128)S(1)}, u32[]{:S(2)}, u32[]{:S(2)}) collective-permute-start(f32[2,24,128]{2,1,0:T(8,128)S(1)} %get-tuple-element.82), channel_id=1, source_target_pairs={{0,2},{1,3},{2,0},{3,1},{4,6},{5,7},{6,4},{7,5},{8,10},{9,11},{10,... | collective-permute-start | bytes 73736 | tf_op jit(solution)/shard_map/ppermute | solution.py:246
  30.5 19.8 %collective-permute-start.10 = (f32[2,24,128]{2,1,0:T(8,128)S(1)}, f32[2,24,128]{2,1,0:T(8,128)S(1)}, u32[]{:S(2)}, u32[]{:S(2)}) collective-permute-start(f32[2,24,128]{2,1,0:T(8,128)S(1)} %get-tuple-element.83), channel_id=1, source_target_pairs={{0,1},{1,0},{2,4},{3,5},{4,2},{5,3},{6,8},{7,9},{8,6},{9,7},{10,12... | collective-permute-start | bytes 73736 | tf_op jit(solution)/shard_map/ppermute | solution.py:246
  31.1 27.3 %all-to-all-start = ((f32[128,1,128]{2,1,0:T(1,128)}), f32[128,1,128]{2,1,0:T(1,128)S(1)}, u32[]{:S(2)}, u32[]{:S(2)}) async-start(f32[128,1,128]{2,1,0:T(1,128)} %get-tuple-element.89), calls=%async_computation | async-start | bytes 131072 | tf_op jit(solution)/shard_map/all_to_all | solution.py:307
  50.3 2.0 %collective-permute-start.11 = (f32[2,24,128]{2,1,0:T(8,128)S(1)}, f32[2,24,128]{2,1,0:T(8,128)S(1)}, u32[]{:S(2)}, u32[]{:S(2)}) collective-permute-start(f32[2,24,128]{2,1,0:T(8,128)S(1)} %pad_maximum_fusion.3), channel_id=1, source_target_pairs={{0,1},{1,0},{2,3},{3,2},{4,5},{5,4},{6,7},{7,6},{8,9},{9,8},{10,11... | collective-permute-start | bytes 73736 | tf_op jit(solution)/shard_map/ppermute | solution.py:254

commit v6 on v5

--- a/solution.py
+++ b/solution.py
@@ -72,6 +72,27 @@
         jnp.where(core == 1, first, second),
         jnp.where(odd == 1, near, far),
     ]
+
+
+def quotient(a, b):
+    q = a / b
+    return q + (a - q * b) / b
+
+
+def exact_product(a, b):
+    def halves(x):
+        scaled = 4097.0 * x
+        high = scaled - (scaled - x)
+        return high, x - high
+
+    product = a * b
+    (ah, al), (bh, bl) = halves(a), halves(b)
+    return product, ((ah * bh - product) + ah * bl + al * bh) + al * bl
+
+
+def determinant(a, b, c):
+    (first, first_rest), (second, second_rest) = exact_product(a, c), exact_product(b, b)
+    return (first - second) + (first_rest - second_rest)
 
 
 def lanes_of(values):
@@ -196,11 +217,11 @@
     field, image = field_ref[:TR], image_ref[:TR]
     row = jnp.sum(sums_ref[...], axis=0)
     s0, s1, s2, s3 = (row[:, k : k + 1] for k in range(4))
-    step0 = s0 / s1
-    ratio = (step0 * step0 * s2 - s0) / s0
+    step0 = quotient(s0, s1)
+    ratio = quotient(quotient(determinant(s0, s1, s2), s1), s1)
     grow = 1.0 + ratio
     curvature = grow * grow * s1 - 2.0 * step0 * grow * s2 + step0 * step0 * s3
-    step1 = ratio * s0 / curvature
+    step1 = quotient(ratio * s0, curvature)
     along = step0 + step1 * grow
     solution_ref[...] = along * field - (step0 * step1) * image
     residual_ref[...] = field - along * image + (step0 * step1) * second[:TR]

time: 59.7 us -> 59.7 us (level)
  no operation moved by 1% of the time
where the time goes in v6:
time: 59.7 us; the launch traced here: 59.5 us
  starting transfers between devices  34.8 us (58%)
  Pallas kernels  14 us (23%)
  waiting for transfers between devices  9.88 us (17%)
  between operations  0.83 us (1%)
    all_to_all x1, starting transfers between devices, shards(): row = lax.all_to_all(row, DOM, 0, 0)  17.7 us
    ppermute x8, starting transfers between devices, swap(): return lax.ppermute(value, DOM, pairs)  14.4 us
    pallas_call x9, Pallas kernels, call(): pl.pallas_call(kernel, in_specs=[pl.BlockSpec(memory_space=m) for m in sp...  14 us
    all_to_all x1, waiting for transfers between devices, shards(): row = lax.all_to_all(row, DOM, 0, 0)  6.12 us
    ppermute x4, waiting for transfers between devices, exchange(): got_mid = lax.ppermute(pair, DOM, [(i, i ^ 1) for i in range(count)])  3.73 us
    ppermute x4, starting transfers between devices, exchange(): got_mid = lax.ppermute(pair, DOM, [(i, i ^ 1) for i in range(count)])  2.66 us
  transfers between devices with their start and end apart: 13, of which 5 were waited for; matrix products, arithmetic and copies ran while one was open for 0% of the time, Pallas kernels for 12%

profile of v6, /device:TPU:1, one launch (start us, length us, event | category | flops | bytes accessed | tf_op | source)
XLA Modules:
  0.0 59.5 jit_solution(6723691587919695438)
XLA Ops:
  0.6 1.4 %shard_map.95 = (f32[2,24,128]{2,1,0:T(8,128)S(1)}, f32[2,24,128]{2,1,0:T(8,128)S(1)}, f32[24,128]{1,0:T(8,128)S(1)}, bf16[1024,512]{1,0:T(8,128)(2,1)S(1)}, f32...) custom-call(s32[1,4]{1,0:T(1,128)} %count_ref.1, f32[18,1024]{1,0:T(8,128)} %field_ref.1, ...), custom_call_target="tpu_custom_call" | custom-call | tf_op jit(solution)/shard_map/pallas_call | solution.py:244
  2.1 2.1 %collective-permute-start = (f32[2,24,128]{2,1,0:T(8,128)S(1)}, f32[2,24,128]{2,1,0:T(8,128)S(1)}, u32[]{:S(2)}, u32[]{:S(2)}) collective-permute-start(f32[2,24,128]{2,1,0:T(8,128)S(1)} %get-tuple-element.46), channel_id=1, source_target_pairs={{0,2},{1,3},{2,0},{3,1},{4,6},{5,7},{6,4},{7,5},{8,10},{9,11},{10,... | collective-permute-start | bytes 73736 | tf_op jit(solution)/shard_map/ppermute | solution.py:267
  4.2 1.0 %collective-permute-start.1 = (f32[2,24,128]{2,1,0:T(8,128)S(1)}, f32[2,24,128]{2,1,0:T(8,128)S(1)}, u32[]{:S(2)}, u32[]{:S(2)}) collective-permute-start(f32[2,24,128]{2,1,0:T(8,128)S(1)} %get-tuple-element.47), channel_id=1, source_target_pairs={{0,1},{1,0},{2,4},{3,5},{4,2},{5,3},{6,8},{7,9},{8,6},{9,7},{10,12... | collective-permute-start | bytes 73736 | tf_op jit(solution)/shard_map/ppermute | solution.py:267
  5.2 3.2 %shard_map.96 = (bf16[512,2048]{1,0:T(8,128)(2,1)S(1)}, f32[24,2048]{1,0:T(8,128)S(1)}, f32[4,72,72,128]{3,2,1,0:T(8,128)S(1)}) custom-call(s32[4,512]{1,0:T(4,128)S(1)} %get-tuple-element.48.map_ref, f32[24,1024]{1,0:T(8,128)S(1)} %get-tuple-element.49.field_ref, bf16[72,72,512]{2,1,0:T(8,128)(2,1)} %matrix_ref.1), custom_call_target="tpu_custom_call" | custom-call | tf_op jit(solution)/shard_map/pallas_call | solution.py:244
  8.5 1.2 %collective-permute-done.2.mid_ref = f32[2,24,128]{2,1,0:T(8,128)S(1)} collective-permute-done((f32[2,24,128]{2,1,0:T(8,128)S(1)}, f32[2,24,128]{2,1,0:T(8,128)S(1)}, u32[]{:S(2)}, u32[]{:S(2)}) %collective-permute-start.2) | collective-permute-done | bytes 24608 | tf_op jit(solution)/shard_map/ppermute | solution.py:275
  9.7 1.9 %shard_map.97 = (f32[2,24,128]{2,1,0:T(8,128)S(1)}, f32[2,24,128]{2,1,0:T(8,128)S(1)}, f32[24,128]{1,0:T(8,128)S(1)}, f32[24,2048]{1,0:T(8,128)S(1)}, f32[24,2048]{1,0:T(8,128)S(1)}) custom-call(f32[2,24,128]{2,1,0:T(8,128)S(1)} %collective-permute-done.near_ref, f32[2,24,128]{2,1,0:T(8,128)S(1)} %collective-permute-done.1.far_ref, ...), custom_call_target="tpu_custom_call" | custom-call | tf_op jit(solution)/shard_map/pallas_call | solution.py:244
  11.6 2.1 %collective-permute-start.3 = (f32[2,24,128]{2,1,0:T(8,128)S(1)}, f32[2,24,128]{2,1,0:T(8,128)S(1)}, u32[]{:S(2)}, u32[]{:S(2)}) collective-permute-start(f32[2,24,128]{2,1,0:T(8,128)S(1)} %get-tuple-element.59), channel_id=1, source_target_pairs={{0,2},{1,3},{2,0},{3,1},{4,6},{5,7},{6,4},{7,5},{8,10},{9,11},{10,... | collective-permute-start | bytes 73736 | tf_op jit(solution)/shard_map/ppermute | solution.py:267
  13.7 0.6 %collective-permute-start.4 = (f32[2,24,128]{2,1,0:T(8,128)S(1)}, f32[2,24,128]{2,1,0:T(8,128)S(1)}, u32[]{:S(2)}, u32[]{:S(2)}) collective-permute-start(f32[2,24,128]{2,1,0:T(8,128)S(1)} %get-tuple-element.60), channel_id=1, source_target_pairs={{0,1},{1,0},{2,4},{3,5},{4,2},{5,3},{6,8},{7,9},{8,6},{9,7},{10,12... | collective-permute-start | bytes 73736 | tf_op jit(solution)/shard_map/ppermute | solution.py:267
  14.4 1.4 %shard_map.98 = (f32[1,128]{1,0:T(1,128)S(1)}, f32[24,1024]{1,0:T(8,128)S(1)}) custom-call(f32[24,2048]{1,0:T(8,128)S(1)} %get-tuple-element.61.spread_ref, s32[4,512]{1,0:T(4,128)S(1)} %get-tuple-element.48.map_ref, f32[24,1024]{1,0:T(8,128)S(1)} %get-tuple-element.49.field_ref, f32[1,1024]{1,0:T(1,128)S(1)} %get-tuple-element.62.diagonal_ref, ...), custom_call_target="tpu_custom_call" | custom-call | tf_op jit(solution)/shard_map/pallas_call | solution.py:244
  16.3 0.8 %collective-permute-done.5.mid_ref = f32[2,24,128]{2,1,0:T(8,128)S(1)} collective-permute-done((f32[2,24,128]{2,1,0:T(8,128)S(1)}, f32[2,24,128]{2,1,0:T(8,128)S(1)}, u32[]{:S(2)}, u32[]{:S(2)}) %collective-permute-start.5) | collective-permute-done | bytes 24608 | tf_op jit(solution)/shard_map/ppermute | solution.py:275
  17.7 3.3 %collective-permute-start.6 = (f32[2,24,128]{2,1,0:T(8,128)S(1)}, f32[2,24,128]{2,1,0:T(8,128)S(1)}, u32[]{:S(2)}, u32[]{:S(2)}) collective-permute-start(f32[2,24,128]{2,1,0:T(8,128)S(1)} %get-tuple-element.71), channel_id=1, source_target_pairs={{0,2},{1,3},{2,0},{3,1},{4,6},{5,7},{6,4},{7,5},{8,10},{9,11},{10,... | collective-permute-start | bytes 73736 | tf_op jit(solution)/shard_map/ppermute | solution.py:267
  21.0 0.6 %collective-permute-start.7 = (f32[2,24,128]{2,1,0:T(8,128)S(1)}, f32[2,24,128]{2,1,0:T(8,128)S(1)}, u32[]{:S(2)}, u32[]{:S(2)}) collective-permute-start(f32[2,24,128]{2,1,0:T(8,128)S(1)} %get-tuple-element.72), channel_id=1, source_target_pairs={{0,1},{1,0},{2,4},{3,5},{4,2},{5,3},{6,8},{7,9},{8,6},{9,7},{10,12... | collective-permute-start | bytes 73736 | tf_op jit(solution)/shard_map/ppermute | solution.py:267
  21.7 0.9 %shard_map.100 = (f32[24,2048]{1,0:T(8,128)S(1)}, f32[1,128]{1,0:T(1,128)S(1)}) custom-call(f32[24,1024]{1,0:T(8,128)S(1)} %get-tuple-element.73.image_ref.field_ref, s32[4,512]{1,0:T(4,128)S(1)} %get-tuple-element.48.map_ref, f32[1,1024]{1,0:T(1,128)S(1)} %get-tuple-element.62.diagonal_ref), custom_call_target="tpu_custom_call" | custom-call | tf_op jit(solution)/shard_map/pallas_call | solution.py:244
  22.6 1.0 %collective-permute-start.8 = (f32[2,24,128]{2,1,0:T(8,128)S(1)}, f32[2,24,128]{2,1,0:T(8,128)S(1)}, u32[]{:S(2)}, u32[]{:S(2)}) collective-permute-start(f32[2,24,128]{2,1,0:T(8,128)S(1)} %pad_maximum_fusion.2), channel_id=1, source_target_pairs={{0,1},{1,0},{2,3},{3,2},{4,5},{5,4},{6,7},{7,6},{8,9},{9,8},{10,11... | collective-permute-start | bytes 73736 | tf_op jit(solution)/shard_map/ppermute | solution.py:275
  23.6 0.8 %collective-permute-done.8.mid_ref = f32[2,24,128]{2,1,0:T(8,128)S(1)} collective-permute-done((f32[2,24,128]{2,1,0:T(8,128)S(1)}, f32[2,24,128]{2,1,0:T(8,128)S(1)}, u32[]{:S(2)}, u32[]{:S(2)}) %collective-permute-start.8) | collective-permute-done | bytes 24608 | tf_op jit(solution)/shard_map/ppermute | solution.py:275
  24.4 2.1 %shard_map.101 = (f32[128,1,128]{2,1,0:T(1,128)}, f32[2,24,128]{2,1,0:T(8,128)S(1)}, f32[2,24,128]{2,1,0:T(8,128)S(1)}, f32[24,128]{1,0:T(8,128)S(1)}, f32[24,2048]{1,0:T(8,128)S(1)}) custom-call(f32[2,24,128]{2,1,0:T(8,128)S(1)} %collective-permute-done.6.near_ref, f32[2,24,128]{2,1,0:T(8,128)S(1)} %collective-permute-done.7.far_ref, ...), custom_call_target="tpu_custom_call" | custom-call | tf_op jit(solution)/shard_map/pallas_call | solution.py:244
  26.5 4.0 %collective-permute-start.9 = (f32[2,24,128]{2,1,0:T(8,128)S(1)}, f32[2,24,128]{2,1,0:T(8,128)S(1)}, u32[]{:S(2)}, u32[]{:S(2)}) collective-permute-start(f32[2,24,128]{2,1,0:T(8,128)S(1)} %get-tuple-element.82), channel_id=1, source_target_pairs={{0,2},{1,3},{2,0},{3,1},{4,6},{5,7},{6,4},{7,5},{8,10},{9,11},{10,... | collective-permute-start | bytes 73736 | tf_op jit(solution)/shard_map/ppermute | solution.py:267
  30.5 0.6 %collective-permute-start.10 = (f32[2,24,128]{2,1,0:T(8,128)S(1)}, f32[2,24,128]{2,1,0:T(8,128)S(1)}, u32[]{:S(2)}, u32[]{:S(2)}) collective-permute-start(f32[2,24,128]{2,1,0:T(8,128)S(1)} %get-tuple-element.83), channel_id=1, source_target_pairs={{0,1},{1,0},{2,4},{3,5},{4,2},{5,3},{6,8},{7,9},{8,6},{9,7},{10,12... | collective-permute-start | bytes 73736 | tf_op jit(solution)/shard_map/ppermute | solution.py:267
  31.1 17.7 %all-to-all-start = ((f32[128,1,128]{2,1,0:T(1,128)}), f32[128,1,128]{2,1,0:T(1,128)S(1)}, u32[]{:S(2)}, u32[]{:S(2)}) async-start(f32[128,1,128]{2,1,0:T(1,128)} %get-tuple-element.89), calls=%async_computation | async-start | bytes 131072 | tf_op jit(solution)/shard_map/all_to_all | solution.py:328
  48.8 1.4 %shard_map.102.own_ref = f32[24,1024]{1,0:T(8,128)S(1)} custom-call(f32[24,2048]{1,0:T(8,128)S(1)} %get-tuple-element.84.spread_ref, s32[4,512]{1,0:T(4,128)S(1)} %get-tuple-element.48.map_ref, f32[24,1024]{1,0:T(8,128)S(1)} %get-tuple-element.73.image_ref.field_ref, f32[1,1024]{1,0:T(1,128)S(1)} %get-tuple-element.62.diagonal_ref), custom_call_target="tpu_custom_call" | custom-call | tf_op jit(solution)/shard_map/pallas_call | solution.py:244
  50.3 1.1 %collective-permute-start.11 = (f32[2,24,128]{2,1,0:T(8,128)S(1)}, f32[2,24,128]{2,1,0:T(8,128)S(1)}, u32[]{:S(2)}, u32[]{:S(2)}) collective-permute-start(f32[2,24,128]{2,1,0:T(8,128)S(1)} %pad_maximum_fusion.3), channel_id=1, source_target_pairs={{0,1},{1,0},{2,3},{3,2},{4,5},{5,4},{6,7},{7,6},{8,9},{9,8},{10,11... | collective-permute-start | bytes 73736 | tf_op jit(solution)/shard_map/ppermute | solution.py:275
  51.4 0.8 %collective-permute-done.11.mid_ref = f32[2,24,128]{2,1,0:T(8,128)S(1)} collective-permute-done((f32[2,24,128]{2,1,0:T(8,128)S(1)}, f32[2,24,128]{2,1,0:T(8,128)S(1)}, u32[]{:S(2)}, u32[]{:S(2)}) %collective-permute-start.11) | collective-permute-done | bytes 24608 | tf_op jit(solution)/shard_map/ppermute | solution.py:275
  52.3 6.1 %all-to-all-done.sums_ref = f32[128,1,128]{2,1,0:T(1,128)S(1)} async-done(((f32[128,1,128]{2,1,0:T(1,128)}), f32[128,1,128]{2,1,0:T(1,128)S(1)}, u32[]{:S(2)}, u32[]{:S(2)}) %all-to-all-start) | async-done | bytes 65568 | tf_op jit(solution)/shard_map/all_to_all | solution.py:328
  58.4 1.1 %shard_map.103 = (f32[18,1024]{1,0:T(8,128)}, f32[18,1024]{1,0:T(8,128)}) custom-call(f32[24,1024]{1,0:T(8,128)S(1)} %shard_map.102.own_ref, f32[2,24,128]{2,1,0:T(8,128)S(1)} %collective-permute-done.9.near_ref, f32[2,24,128]{2,1,0:T(8,128)S(1)} %collective-permute-done.10.far_ref, f32[2,24,128]{2,1,0:T(8,128)S(1)} %collective-permute-done.11.mid_ref, ...), custom_call_target="tpu_custom_call" | custom-call | tf_op jit(solution)/shard_map/pallas_call | solution.py:244
  (19 shorter events, 1.2 us)
Async XLA Ops:
  2.1 6.3 %collective-permute-start = (f32[2,24,128]{2,1,0:T(8,128)S(1)}, f32[2,24,128]{2,1,0:T(8,128)S(1)}, u32[]{:S(2)}, u32[]{:S(2)}) collective-permute-start(f32[2,24,128]{2,1,0:T(8,128)S(1)} %get-tuple-element.46), channel_id=1, source_target_pairs={{0,2},{1,3},{2,0},{3,1},{4,6},{5,7},{6,4},{7,5},{8,10},{9,11},{10,... | collective-permute-start | bytes 73736 | tf_op jit(solution)/shard_map/ppermute | solution.py:267
  4.2 4.2 %collective-permute-start.1 = (f32[2,24,128]{2,1,0:T(8,128)S(1)}, f32[2,24,128]{2,1,0:T(8,128)S(1)}, u32[]{:S(2)}, u32[]{:S(2)}) collective-permute-start(f32[2,24,128]{2,1,0:T(8,128)S(1)} %get-tuple-element.47), channel_id=1, source_target_pairs={{0,1},{1,0},{2,4},{3,5},{4,2},{5,3},{6,8},{7,9},{8,6},{9,7},{10,12... | collective-permute-start | bytes 73736 | tf_op jit(solution)/shard_map/ppermute | solution.py:267
  8.4 1.3 %collective-permute-start.2 = (f32[2,24,128]{2,1,0:T(8,128)S(1)}, f32[2,24,128]{2,1,0:T(8,128)S(1)}, u32[]{:S(2)}, u32[]{:S(2)}) collective-permute-start(f32[2,24,128]{2,1,0:T(8,128)S(1)} %pad_maximum_fusion), channel_id=1, source_target_pairs={{0,1},{1,0},{2,3},{3,2},{4,5},{5,4},{6,7},{7,6},{8,9},{9,8},{10,11... | collective-permute-start | bytes 73736 | tf_op jit(solution)/shard_map/ppermute | solution.py:275
  11.6 4.2 %collective-permute-start.3 = (f32[2,24,128]{2,1,0:T(8,128)S(1)}, f32[2,24,128]{2,1,0:T(8,128)S(1)}, u32[]{:S(2)}, u32[]{:S(2)}) collective-permute-start(f32[2,24,128]{2,1,0:T(8,128)S(1)} %get-tuple-element.59), channel_id=1, source_target_pairs={{0,2},{1,3},{2,0},{3,1},{4,6},{5,7},{6,4},{7,5},{8,10},{9,11},{10,... | collective-permute-start | bytes 73736 | tf_op jit(solution)/shard_map/ppermute | solution.py:267
  13.7 2.0 %collective-permute-start.4 = (f32[2,24,128]{2,1,0:T(8,128)S(1)}, f32[2,24,128]{2,1,0:T(8,128)S(1)}, u32[]{:S(2)}, u32[]{:S(2)}) collective-permute-start(f32[2,24,128]{2,1,0:T(8,128)S(1)} %get-tuple-element.60), channel_id=1, source_target_pairs={{0,1},{1,0},{2,4},{3,5},{4,2},{5,3},{6,8},{7,9},{8,6},{9,7},{10,12... | collective-permute-start | bytes 73736 | tf_op jit(solution)/shard_map/ppermute | solution.py:267
  15.8 1.3 %collective-permute-start.5 = (f32[2,24,128]{2,1,0:T(8,128)S(1)}, f32[2,24,128]{2,1,0:T(8,128)S(1)}, u32[]{:S(2)}, u32[]{:S(2)}) collective-permute-start(f32[2,24,128]{2,1,0:T(8,128)S(1)} %pad_maximum_fusion.1), channel_id=1, source_target_pairs={{0,1},{1,0},{2,3},{3,2},{4,5},{5,4},{6,7},{7,6},{8,9},{9,8},{10,11... | collective-permute-start | bytes 73736 | tf_op jit(solution)/shard_map/ppermute | solution.py:275
  17.7 4.8 %collective-permute-start.6 = (f32[2,24,128]{2,1,0:T(8,128)S(1)}, f32[2,24,128]{2,1,0:T(8,128)S(1)}, u32[]{:S(2)}, u32[]{:S(2)}) collective-permute-start(f32[2,24,128]{2,1,0:T(8,128)S(1)} %get-tuple-element.71), channel_id=1, source_target_pairs={{0,2},{1,3},{2,0},{3,1},{4,6},{5,7},{6,4},{7,5},{8,10},{9,11},{10,... | collective-permute-start | bytes 73736 | tf_op jit(solution)/shard_map/ppermute | solution.py:267
  21.0 1.5 %collective-permute-start.7 = (f32[2,24,128]{2,1,0:T(8,128)S(1)}, f32[2,24,128]{2,1,0:T(8,128)S(1)}, u32[]{:S(2)}, u32[]{:S(2)}) collective-permute-start(f32[2,24,128]{2,1,0:T(8,128)S(1)} %get-tuple-element.72), channel_id=1, source_target_pairs={{0,1},{1,0},{2,4},{3,5},{4,2},{5,3},{6,8},{7,9},{8,6},{9,7},{10,12... | collective-permute-start | bytes 73736 | tf_op jit(solution)/shard_map/ppermute | solution.py:267
  22.6 1.8 %collective-permute-start.8 = (f32[2,24,128]{2,1,0:T(8,128)S(1)}, f32[2,24,128]{2,1,0:T(8,128)S(1)}, u32[]{:S(2)}, u32[]{:S(2)}) collective-permute-start(f32[2,24,128]{2,1,0:T(8,128)S(1)} %pad_maximum_fusion.2), channel_id=1, source_target_pairs={{0,1},{1,0},{2,3},{3,2},{4,5},{5,4},{6,7},{7,6},{8,9},{9,8},{10,11... | collective-permute-start | bytes 73736 | tf_op jit(solution)/shard_map/ppermute | solution.py:275
  26.5 23.8 %collective-permute-start.9 = (f32[2,24,128]{2,1,0:T(8,128)S(1)}, f32[2,24,128]{2,1,0:T(8,128)S(1)}, u32[]{:S(2)}, u32[]{:S(2)}) collective-permute-start(f32[2,24,128]{2,1,0:T(8,128)S(1)} %get-tuple-element.82), channel_id=1, source_target_pairs={{0,2},{1,3},{2,0},{3,1},{4,6},{5,7},{6,4},{7,5},{8,10},{9,11},{10,... | collective-permute-start | bytes 73736 | tf_op jit(solution)/shard_map/ppermute | solution.py:267
  30.5 19.8 %collective-permute-start.10 = (f32[2,24,128]{2,1,0:T(8,128)S(1)}, f32[2,24,128]{2,1,0:T(8,128)S(1)}, u32[]{:S(2)}, u32[]{:S(2)}) collective-permute-start(f32[2,24,128]{2,1,0:T(8,128)S(1)} %get-tuple-element.83), channel_id=1, source_target_pairs={{0,1},{1,0},{2,4},{3,5},{4,2},{5,3},{6,8},{7,9},{8,6},{9,7},{10,12... | collective-permute-start | bytes 73736 | tf_op jit(solution)/shard_map/ppermute | solution.py:267
  31.1 27.3 %all-to-all-start = ((f32[128,1,128]{2,1,0:T(1,128)}), f32[128,1,128]{2,1,0:T(1,128)S(1)}, u32[]{:S(2)}, u32[]{:S(2)}) async-start(f32[128,1,128]{2,1,0:T(1,128)} %get-tuple-element.89), calls=%async_computation | async-start | bytes 131072 | tf_op jit(solution)/shard_map/all_to_all | solution.py:328
  50.3 2.0 %collective-permute-start.11 = (f32[2,24,128]{2,1,0:T(8,128)S(1)}, f32[2,24,128]{2,1,0:T(8,128)S(1)}, u32[]{:S(2)}, u32[]{:S(2)}) collective-permute-start(f32[2,24,128]{2,1,0:T(8,128)S(1)} %pad_maximum_fusion.3), channel_id=1, source_target_pairs={{0,1},{1,0},{2,3},{3,2},{4,5},{5,4},{6,7},{7,6},{8,9},{9,8},{10,11... | collective-permute-start | bytes 73736 | tf_op jit(solution)/shard_map/ppermute | solution.py:275

commit v7 on v6

--- a/solution.py
+++ b/solution.py
@@ -22,10 +22,15 @@
 VMEM = pltpu.VMEM
 
 
+def upper(x):
+    scaled = 65537.0 * x
+    return scaled - (scaled - x)
+
+
 def pieces(x):
-    hi = x.astype(BF16).astype(F32)
+    hi = upper(x)
     rest = x - hi
-    mid = rest.astype(BF16).astype(F32)
+    mid = upper(rest)
     return jnp.concatenate([hi, mid, rest - mid], axis=0).astype(BF16)
 
 

time: 59.7 us -> 59.8 us (level)
  no operation moved by 1% of the time
where the time goes in v7:
time: 59.8 us; the launch traced here: 59.5 us
  starting transfers between devices  34.4 us (58%)
  Pallas kernels  14.4 us (24%)
  waiting for transfers between devices  9.87 us (17%)
  between operations  0.84 us (1%)
    all_to_all x1, starting transfers between devices, shards(): row = lax.all_to_all(row, DOM, 0, 0)  17.8 us
    pallas_call x9, Pallas kernels, call(): pl.pallas_call(kernel, in_specs=[pl.BlockSpec(memory_space=m) for m in sp...  14.4 us
    ppermute x8, starting transfers between devices, swap(): return lax.ppermute(value, DOM, pairs)  13.9 us
    all_to_all x1, waiting for transfers between devices, shards(): row = lax.all_to_all(row, DOM, 0, 0)  6.12 us
    ppermute x4, waiting for transfers between devices, exchange(): got_mid = lax.ppermute(pair, DOM, [(i, i ^ 1) for i in range(count)])  3.73 us
    ppermute x4, starting transfers between devices, exchange(): got_mid = lax.ppermute(pair, DOM, [(i, i ^ 1) for i in range(count)])  2.66 us
  transfers between devices with their start and end apart: 13, of which 5 were waited for; matrix products, arithmetic and copies ran while one was open for 0% of the time, Pallas kernels for 12%

profile of v7, /device:TPU:1, one launch (start us, length us, event | category | flops | bytes accessed | tf_op | source)
XLA Modules:
  0.0 59.5 jit_solution(12413270792441750810)
XLA Ops:
  0.6 1.5 %shard_map.95 = (f32[2,24,128]{2,1,0:T(8,128)S(1)}, f32[2,24,128]{2,1,0:T(8,128)S(1)}, f32[24,128]{1,0:T(8,128)S(1)}, bf16[1024,512]{1,0:T(8,128)(2,1)S(1)}, f32...) custom-call(s32[1,4]{1,0:T(1,128)} %count_ref.1, f32[18,1024]{1,0:T(8,128)} %field_ref.1, ...), custom_call_target="tpu_custom_call" | custom-call | tf_op jit(solution)/shard_map/pallas_call | solution.py:249
  2.1 2.1 %collective-permute-start = (f32[2,24,128]{2,1,0:T(8,128)S(1)}, f32[2,24,128]{2,1,0:T(8,128)S(1)}, u32[]{:S(2)}, u32[]{:S(2)}) collective-permute-start(f32[2,24,128]{2,1,0:T(8,128)S(1)} %get-tuple-element.46), channel_id=1, source_target_pairs={{0,2},{1,3},{2,0},{3,1},{4,6},{5,7},{6,4},{7,5},{8,10},{9,11},{10,... | collective-permute-start | bytes 73736 | tf_op jit(solution)/shard_map/ppermute | solution.py:272
  4.2 1.0 %collective-permute-start.1 = (f32[2,24,128]{2,1,0:T(8,128)S(1)}, f32[2,24,128]{2,1,0:T(8,128)S(1)}, u32[]{:S(2)}, u32[]{:S(2)}) collective-permute-start(f32[2,24,128]{2,1,0:T(8,128)S(1)} %get-tuple-element.47), channel_id=1, source_target_pairs={{0,1},{1,0},{2,4},{3,5},{4,2},{5,3},{6,8},{7,9},{8,6},{9,7},{10,12... | collective-permute-start | bytes 73736 | tf_op jit(solution)/shard_map/ppermute | solution.py:272
  5.2 3.7 %shard_map.96 = (bf16[512,2048]{1,0:T(8,128)(2,1)S(1)}, f32[24,2048]{1,0:T(8,128)S(1)}, f32[4,72,72,128]{3,2,1,0:T(8,128)S(1)}) custom-call(s32[4,512]{1,0:T(4,128)S(1)} %get-tuple-element.48.map_ref, f32[24,1024]{1,0:T(8,128)S(1)} %get-tuple-element.49.field_ref, bf16[72,72,512]{2,1,0:T(8,128)(2,1)} %matrix_ref.1), custom_call_target="tpu_custom_call" | custom-call | tf_op jit(solution)/shard_map/pallas_call | solution.py:249
  9.0 1.2 %collective-permute-done.2.mid_ref = f32[2,24,128]{2,1,0:T(8,128)S(1)} collective-permute-done((f32[2,24,128]{2,1,0:T(8,128)S(1)}, f32[2,24,128]{2,1,0:T(8,128)S(1)}, u32[]{:S(2)}, u32[]{:S(2)}) %collective-permute-start.2) | collective-permute-done | bytes 24608 | tf_op jit(solution)/shard_map/ppermute | solution.py:280
  10.1 1.9 %shard_map.97 = (f32[2,24,128]{2,1,0:T(8,128)S(1)}, f32[2,24,128]{2,1,0:T(8,128)S(1)}, f32[24,128]{1,0:T(8,128)S(1)}, f32[24,2048]{1,0:T(8,128)S(1)}, f32[24,2048]{1,0:T(8,128)S(1)}) custom-call(f32[2,24,128]{2,1,0:T(8,128)S(1)} %collective-permute-done.near_ref, f32[2,24,128]{2,1,0:T(8,128)S(1)} %collective-permute-done.1.far_ref, ...), custom_call_target="tpu_custom_call" | custom-call | tf_op jit(solution)/shard_map/pallas_call | solution.py:249
  12.1 2.1 %collective-permute-start.3 = (f32[2,24,128]{2,1,0:T(8,128)S(1)}, f32[2,24,128]{2,1,0:T(8,128)S(1)}, u32[]{:S(2)}, u32[]{:S(2)}) collective-permute-start(f32[2,24,128]{2,1,0:T(8,128)S(1)} %get-tuple-element.59), channel_id=1, source_target_pairs={{0,2},{1,3},{2,0},{3,1},{4,6},{5,7},{6,4},{7,5},{8,10},{9,11},{10,... | collective-permute-start | bytes 73736 | tf_op jit(solution)/shard_map/ppermute | solution.py:272
  14.2 0.6 %collective-permute-start.4 = (f32[2,24,128]{2,1,0:T(8,128)S(1)}, f32[2,24,128]{2,1,0:T(8,128)S(1)}, u32[]{:S(2)}, u32[]{:S(2)}) collective-permute-start(f32[2,24,128]{2,1,0:T(8,128)S(1)} %get-tuple-element.60), channel_id=1, source_target_pairs={{0,1},{1,0},{2,4},{3,5},{4,2},{5,3},{6,8},{7,9},{8,6},{9,7},{10,12... | collective-permute-start | bytes 73736 | tf_op jit(solution)/shard_map/ppermute | solution.py:272
  14.8 1.4 %shard_map.98 = (f32[1,128]{1,0:T(1,128)S(1)}, f32[24,1024]{1,0:T(8,128)S(1)}) custom-call(f32[24,2048]{1,0:T(8,128)S(1)} %get-tuple-element.61.spread_ref, s32[4,512]{1,0:T(4,128)S(1)} %get-tuple-element.48.map_ref, f32[24,1024]{1,0:T(8,128)S(1)} %get-tuple-element.49.field_ref, f32[1,1024]{1,0:T(1,128)S(1)} %get-tuple-element.62.diagonal_ref, ...), custom_call_target="tpu_custom_call" | custom-call | tf_op jit(solution)/shard_map/pallas_call | solution.py:249
  16.7 0.8 %collective-permute-done.5.mid_ref = f32[2,24,128]{2,1,0:T(8,128)S(1)} collective-permute-done((f32[2,24,128]{2,1,0:T(8,128)S(1)}, f32[2,24,128]{2,1,0:T(8,128)S(1)}, u32[]{:S(2)}, u32[]{:S(2)}) %collective-permute-start.5) | collective-permute-done | bytes 24608 | tf_op jit(solution)/shard_map/ppermute | solution.py:280
  17.6 0.6 %shard_map.99 = (f32[24,1024]{1,0:T(8,128)S(1)}, f32[2,24,128]{2,1,0:T(8,128)S(1)}, f32[2,24,128]{2,1,0:T(8,128)S(1)}, f32[24,128]{1,0:T(8,128)S(1)}) custom-call(f32[24,1024]{1,0:T(8,128)S(1)} %get-tuple-element.66.own_ref, f32[2,24,128]{2,1,0:T(8,128)S(1)} %collective-permute-done.3.near_ref, f32[2,24,128]{2,1,0:T(8,128)S(1)} %collective-permute-done.4.far_ref, ...), custom_call_target="tpu_custom_call" | custom-call | tf_op jit(solution)/shard_map/pallas_call | solution.py:249
  18.2 2.8 %collective-permute-start.6 = (f32[2,24,128]{2,1,0:T(8,128)S(1)}, f32[2,24,128]{2,1,0:T(8,128)S(1)}, u32[]{:S(2)}, u32[]{:S(2)}) collective-permute-start(f32[2,24,128]{2,1,0:T(8,128)S(1)} %get-tuple-element.71), channel_id=1, source_target_pairs={{0,2},{1,3},{2,0},{3,1},{4,6},{5,7},{6,4},{7,5},{8,10},{9,11},{10,... | collective-permute-start | bytes 73736 | tf_op jit(solution)/shard_map/ppermute | solution.py:272
  21.7 0.9 %shard_map.100 = (f32[24,2048]{1,0:T(8,128)S(1)}, f32[1,128]{1,0:T(1,128)S(1)}) custom-call(f32[24,1024]{1,0:T(8,128)S(1)} %get-tuple-element.73.image_ref.field_ref, s32[4,512]{1,0:T(4,128)S(1)} %get-tuple-element.48.map_ref, f32[1,1024]{1,0:T(1,128)S(1)} %get-tuple-element.62.diagonal_ref), custom_call_target="tpu_custom_call" | custom-call | tf_op jit(solution)/shard_map/pallas_call | solution.py:249
  22.6 1.0 %collective-permute-start.8 = (f32[2,24,128]{2,1,0:T(8,128)S(1)}, f32[2,24,128]{2,1,0:T(8,128)S(1)}, u32[]{:S(2)}, u32[]{:S(2)}) collective-permute-start(f32[2,24,128]{2,1,0:T(8,128)S(1)} %pad_maximum_fusion.2), channel_id=1, source_target_pairs={{0,1},{1,0},{2,3},{3,2},{4,5},{5,4},{6,7},{7,6},{8,9},{9,8},{10,11... | collective-permute-start | bytes 73736 | tf_op jit(solution)/shard_map/ppermute | solution.py:280
  23.6 0.8 %collective-permute-done.8.mid_ref = f32[2,24,128]{2,1,0:T(8,128)S(1)} collective-permute-done((f32[2,24,128]{2,1,0:T(8,128)S(1)}, f32[2,24,128]{2,1,0:T(8,128)S(1)}, u32[]{:S(2)}, u32[]{:S(2)}) %collective-permute-start.8) | collective-permute-done | bytes 24608 | tf_op jit(solution)/shard_map/ppermute | solution.py:280
  24.4 2.0 %shard_map.101 = (f32[128,1,128]{2,1,0:T(1,128)}, f32[2,24,128]{2,1,0:T(8,128)S(1)}, f32[2,24,128]{2,1,0:T(8,128)S(1)}, f32[24,128]{1,0:T(8,128)S(1)}, f32[24,2048]{1,0:T(8,128)S(1)}) custom-call(f32[2,24,128]{2,1,0:T(8,128)S(1)} %collective-permute-done.6.near_ref, f32[2,24,128]{2,1,0:T(8,128)S(1)} %collective-permute-done.7.far_ref, ...), custom_call_target="tpu_custom_call" | custom-call | tf_op jit(solution)/shard_map/pallas_call | solution.py:249
  26.5 4.0 %collective-permute-start.9 = (f32[2,24,128]{2,1,0:T(8,128)S(1)}, f32[2,24,128]{2,1,0:T(8,128)S(1)}, u32[]{:S(2)}, u32[]{:S(2)}) collective-permute-start(f32[2,24,128]{2,1,0:T(8,128)S(1)} %get-tuple-element.82), channel_id=1, source_target_pairs={{0,2},{1,3},{2,0},{3,1},{4,6},{5,7},{6,4},{7,5},{8,10},{9,11},{10,... | collective-permute-start | bytes 73736 | tf_op jit(solution)/shard_map/ppermute | solution.py:272
  30.5 0.6 %collective-permute-start.10 = (f32[2,24,128]{2,1,0:T(8,128)S(1)}, f32[2,24,128]{2,1,0:T(8,128)S(1)}, u32[]{:S(2)}, u32[]{:S(2)}) collective-permute-start(f32[2,24,128]{2,1,0:T(8,128)S(1)} %get-tuple-element.83), channel_id=1, source_target_pairs={{0,1},{1,0},{2,4},{3,5},{4,2},{5,3},{6,8},{7,9},{8,6},{9,7},{10,12... | collective-permute-start | bytes 73736 | tf_op jit(solution)/shard_map/ppermute | solution.py:272
  31.1 17.8 %all-to-all-start = ((f32[128,1,128]{2,1,0:T(1,128)}), f32[128,1,128]{2,1,0:T(1,128)S(1)}, u32[]{:S(2)}, u32[]{:S(2)}) async-start(f32[128,1,128]{2,1,0:T(1,128)} %get-tuple-element.89), calls=%async_computation | async-start | bytes 131072 | tf_op jit(solution)/shard_map/all_to_all | solution.py:333
  48.9 1.4 %shard_map.102.own_ref = f32[24,1024]{1,0:T(8,128)S(1)} custom-call(f32[24,2048]{1,0:T(8,128)S(1)} %get-tuple-element.84.spread_ref, s32[4,512]{1,0:T(4,128)S(1)} %get-tuple-element.48.map_ref, f32[24,1024]{1,0:T(8,128)S(1)} %get-tuple-element.73.image_ref.field_ref, f32[1,1024]{1,0:T(1,128)S(1)} %get-tuple-element.62.diagonal_ref), custom_call_target="tpu_custom_call" | custom-call | tf_op jit(solution)/shard_map/pallas_call | solution.py:249
  50.3 1.1 %collective-permute-start.11 = (f32[2,24,128]{2,1,0:T(8,128)S(1)}, f32[2,24,128]{2,1,0:T(8,128)S(1)}, u32[]{:S(2)}, u32[]{:S(2)}) collective-permute-start(f32[2,24,128]{2,1,0:T(8,128)S(1)} %pad_maximum_fusion.3), channel_id=1, source_target_pairs={{0,1},{1,0},{2,3},{3,2},{4,5},{5,4},{6,7},{7,6},{8,9},{9,8},{10,11... | collective-permute-start | bytes 73736 | tf_op jit(solution)/shard_map/ppermute | solution.py:280
  51.5 0.8 %collective-permute-done.11.mid_ref = f32[2,24,128]{2,1,0:T(8,128)S(1)} collective-permute-done((f32[2,24,128]{2,1,0:T(8,128)S(1)}, f32[2,24,128]{2,1,0:T(8,128)S(1)}, u32[]{:S(2)}, u32[]{:S(2)}) %collective-permute-start.11) | collective-permute-done | bytes 24608 | tf_op jit(solution)/shard_map/ppermute | solution.py:280
  52.3 6.1 %all-to-all-done.sums_ref = f32[128,1,128]{2,1,0:T(1,128)S(1)} async-done(((f32[128,1,128]{2,1,0:T(1,128)}), f32[128,1,128]{2,1,0:T(1,128)S(1)}, u32[]{:S(2)}, u32[]{:S(2)}) %all-to-all-start) | async-done | bytes 65568 | tf_op jit(solution)/shard_map/all_to_all | solution.py:333
  58.5 1.1 %shard_map.103 = (f32[18,1024]{1,0:T(8,128)}, f32[18,1024]{1,0:T(8,128)}) custom-call(f32[24,1024]{1,0:T(8,128)S(1)} %shard_map.102.own_ref, f32[2,24,128]{2,1,0:T(8,128)S(1)} %collective-permute-done.9.near_ref, f32[2,24,128]{2,1,0:T(8,128)S(1)} %collective-permute-done.10.far_ref, f32[2,24,128]{2,1,0:T(8,128)S(1)} %collective-permute-done.11.mid_ref, ...), custom_call_target="tpu_custom_call" | custom-call | tf_op jit(solution)/shard_map/pallas_call | solution.py:249
  (19 shorter events, 1.2 us)
Async XLA Ops:
  2.1 6.7 %collective-permute-start = (f32[2,24,128]{2,1,0:T(8,128)S(1)}, f32[2,24,128]{2,1,0:T(8,128)S(1)}, u32[]{:S(2)}, u32[]{:S(2)}) collective-permute-start(f32[2,24,128]{2,1,0:T(8,128)S(1)} %get-tuple-element.46), channel_id=1, source_target_pairs={{0,2},{1,3},{2,0},{3,1},{4,6},{5,7},{6,4},{7,5},{8,10},{9,11},{10,... | collective-permute-start | bytes 73736 | tf_op jit(solution)/shard_map/ppermute | solution.py:272
  4.2 4.6 %collective-permute-start.1 = (f32[2,24,128]{2,1,0:T(8,128)S(1)}, f32[2,24,128]{2,1,0:T(8,128)S(1)}, u32[]{:S(2)}, u32[]{:S(2)}) collective-permute-start(f32[2,24,128]{2,1,0:T(8,128)S(1)} %get-tuple-element.47), channel_id=1, source_target_pairs={{0,1},{1,0},{2,4},{3,5},{4,2},{5,3},{6,8},{7,9},{8,6},{9,7},{10,12... | collective-permute-start | bytes 73736 | tf_op jit(solution)/shard_map/ppermute | solution.py:272
  8.9 1.3 %collective-permute-start.2 = (f32[2,24,128]{2,1,0:T(8,128)S(1)}, f32[2,24,128]{2,1,0:T(8,128)S(1)}, u32[]{:S(2)}, u32[]{:S(2)}) collective-permute-start(f32[2,24,128]{2,1,0:T(8,128)S(1)} %pad_maximum_fusion), channel_id=1, source_target_pairs={{0,1},{1,0},{2,3},{3,2},{4,5},{5,4},{6,7},{7,6},{8,9},{9,8},{10,11... | collective-permute-start | bytes 73736 | tf_op jit(solution)/shard_map/ppermute | solution.py:280
  12.1 4.2 %collective-permute-start.3 = (f32[2,24,128]{2,1,0:T(8,128)S(1)}, f32[2,24,128]{2,1,0:T(8,128)S(1)}, u32[]{:S(2)}, u32[]{:S(2)}) collective-permute-start(f32[2,24,128]{2,1,0:T(8,128)S(1)} %get-tuple-element.59), channel_id=1, source_target_pairs={{0,2},{1,3},{2,0},{3,1},{4,6},{5,7},{6,4},{7,5},{8,10},{9,11},{10,... | collective-permute-start | bytes 73736 | tf_op jit(solution)/shard_map/ppermute | solution.py:272
  14.2 2.0 %collective-permute-start.4 = (f32[2,24,128]{2,1,0:T(8,128)S(1)}, f32[2,24,128]{2,1,0:T(8,128)S(1)}, u32[]{:S(2)}, u32[]{:S(2)}) collective-permute-start(f32[2,24,128]{2,1,0:T(8,128)S(1)} %get-tuple-element.60), channel_id=1, source_target_pairs={{0,1},{1,0},{2,4},{3,5},{4,2},{5,3},{6,8},{7,9},{8,6},{9,7},{10,12... | collective-permute-start | bytes 73736 | tf_op jit(solution)/shard_map/ppermute | solution.py:272
  16.3 1.3 %collective-permute-start.5 = (f32[2,24,128]{2,1,0:T(8,128)S(1)}, f32[2,24,128]{2,1,0:T(8,128)S(1)}, u32[]{:S(2)}, u32[]{:S(2)}) collective-permute-start(f32[2,24,128]{2,1,0:T(8,128)S(1)} %pad_maximum_fusion.1), channel_id=1, source_target_pairs={{0,1},{1,0},{2,3},{3,2},{4,5},{5,4},{6,7},{7,6},{8,9},{9,8},{10,11... | collective-permute-start | bytes 73736 | tf_op jit(solution)/shard_map/ppermute | solution.py:280
  18.2 4.4 %collective-permute-start.6 = (f32[2,24,128]{2,1,0:T(8,128)S(1)}, f32[2,24,128]{2,1,0:T(8,128)S(1)}, u32[]{:S(2)}, u32[]{:S(2)}) collective-permute-start(f32[2,24,128]{2,1,0:T(8,128)S(1)} %get-tuple-element.71), channel_id=1, source_target_pairs={{0,2},{1,3},{2,0},{3,1},{4,6},{5,7},{6,4},{7,5},{8,10},{9,11},{10,... | collective-permute-start | bytes 73736 | tf_op jit(solution)/shard_map/ppermute | solution.py:272
  21.1 1.5 %collective-permute-start.7 = (f32[2,24,128]{2,1,0:T(8,128)S(1)}, f32[2,24,128]{2,1,0:T(8,128)S(1)}, u32[]{:S(2)}, u32[]{:S(2)}) collective-permute-start(f32[2,24,128]{2,1,0:T(8,128)S(1)} %get-tuple-element.72), channel_id=1, source_target_pairs={{0,1},{1,0},{2,4},{3,5},{4,2},{5,3},{6,8},{7,9},{8,6},{9,7},{10,12... | collective-permute-start | bytes 73736 | tf_op jit(solution)/shard_map/ppermute | solution.py:272
  22.6 1.8 %collective-permute-start.8 = (f32[2,24,128]{2,1,0:T(8,128)S(1)}, f32[2,24,128]{2,1,0:T(8,128)S(1)}, u32[]{:S(2)}, u32[]{:S(2)}) collective-permute-start(f32[2,24,128]{2,1,0:T(8,128)S(1)} %pad_maximum_fusion.2), channel_id=1, source_target_pairs={{0,1},{1,0},{2,3},{3,2},{4,5},{5,4},{6,7},{7,6},{8,9},{9,8},{10,11... | collective-permute-start | bytes 73736 | tf_op jit(solution)/shard_map/ppermute | solution.py:280
  26.5 23.8 %collective-permute-start.9 = (f32[2,24,128]{2,1,0:T(8,128)S(1)}, f32[2,24,128]{2,1,0:T(8,128)S(1)}, u32[]{:S(2)}, u32[]{:S(2)}) collective-permute-start(f32[2,24,128]{2,1,0:T(8,128)S(1)} %get-tuple-element.82), channel_id=1, source_target_pairs={{0,2},{1,3},{2,0},{3,1},{4,6},{5,7},{6,4},{7,5},{8,10},{9,11},{10,... | collective-permute-start | bytes 73736 | tf_op jit(solution)/shard_map/ppermute | solution.py:272
  30.5 19.8 %collective-permute-start.10 = (f32[2,24,128]{2,1,0:T(8,128)S(1)}, f32[2,24,128]{2,1,0:T(8,128)S(1)}, u32[]{:S(2)}, u32[]{:S(2)}) collective-permute-start(f32[2,24,128]{2,1,0:T(8,128)S(1)} %get-tuple-element.83), channel_id=1, source_target_pairs={{0,1},{1,0},{2,4},{3,5},{4,2},{5,3},{6,8},{7,9},{8,6},{9,7},{10,12... | collective-permute-start | bytes 73736 | tf_op jit(solution)/shard_map/ppermute | solution.py:272
  31.1 27.3 %all-to-all-start = ((f32[128,1,128]{2,1,0:T(1,128)}), f32[128,1,128]{2,1,0:T(1,128)S(1)}, u32[]{:S(2)}, u32[]{:S(2)}) async-start(f32[128,1,128]{2,1,0:T(1,128)} %get-tuple-element.89), calls=%async_computation | async-start | bytes 131072 | tf_op jit(solution)/shard_map/all_to_all | solution.py:333
  50.3 2.0 %collective-permute-start.11 = (f32[2,24,128]{2,1,0:T(8,128)S(1)}, f32[2,24,128]{2,1,0:T(8,128)S(1)}, u32[]{:S(2)}, u32[]{:S(2)}) collective-permute-start(f32[2,24,128]{2,1,0:T(8,128)S(1)} %pad_maximum_fusion.3), channel_id=1, source_target_pairs={{0,1},{1,0},{2,3},{3,2},{4,5},{5,4},{6,7},{7,6},{8,9},{9,8},{10,11... | collective-permute-start | bytes 73736 | tf_op jit(solution)/shard_map/ppermute | solution.py:280

commit v8 on v7

--- a/solution.py
+++ b/solution.py
@@ -29,14 +29,12 @@
 
 def pieces(x):
     hi = upper(x)
-    rest = x - hi
-    mid = upper(rest)
-    return jnp.concatenate([hi, mid, rest - mid], axis=0).astype(BF16)
+    return jnp.concatenate([hi, x - hi], axis=0).astype(BF16)
 
 
 def joined(y):
-    rows = y.shape[0] // 3
-    return y[:rows] + y[rows : 2 * rows] + y[2 * rows :]
+    rows = y.shape[0] // 2
+    return y[:rows] + y[rows:]
 
 
 def pick(x, selector):
@@ -220,7 +218,11 @@
         back_ref[:, k * GH : (k + 1) * GH] = block
     second = own_ref[...] + spread_out(back_ref[...], share_ref[...])
     field, image = field_ref[:TR], image_ref[:TR]
-    row = jnp.sum(sums_ref[...], axis=0)
+    row = sums_ref[...]
+    while row.shape[0] > 1:
+        half = row.shape[0] // 2
+        row = row[:half] + row[half:]
+    row = row[0]
     s0, s1, s2, s3 = (row[:, k : k + 1] for k in range(4))
     step0 = quotient(s0, s1)
     ratio = quotient(quotient(determinant(s0, s1, s2), s1), s1)

time: 59.8 us -> 59.5 us (level)
  Pallas kernels: 14.4 us -> 13.7 us
    pallas_call x9, Pallas kernels: 14.4 us -> 13.7 us  [call(): pl.pallas_call(kernel, in_specs=[pl.BlockSpec(memory_space=m) for m in sp...]
  transfers between devices with their start and end apart: 13 -> 13, of which waited for: 5 -> 5; matrix products, arithmetic and copies ran while one was open for 0% -> 0% of each run, Pallas kernels for 12% -> 11%
where the time goes in v8:
time: 59.5 us; the launch traced here: 59.3 us
  starting transfers between devices  34.8 us (58%)
  Pallas kernels  13.7 us (23%)
  waiting for transfers between devices  9.9 us (17%)
  between operations  0.84 us (1%)
    all_to_all x1, starting transfers between devices, shards(): row = lax.all_to_all(row, DOM, 0, 0)  17.7 us
    ppermute x8, starting transfers between devices, swap(): return lax.ppermute(value, DOM, pairs)  14.4 us
    pallas_call x9, Pallas kernels, call(): pl.pallas_call(kernel, in_specs=[pl.BlockSpec(memory_space=m) for m in sp...  13.7 us
    all_to_all x1, waiting for transfers between devices, shards(): row = lax.all_to_all(row, DOM, 0, 0)  6.15 us
    ppermute x4, waiting for transfers between devices, exchange(): got_mid = lax.ppermute(pair, DOM, [(i, i ^ 1) for i in range(count)])  3.73 us
    ppermute x4, starting transfers between devices, exchange(): got_mid = lax.ppermute(pair, DOM, [(i, i ^ 1) for i in range(count)])  2.71 us
  transfers between devices with their start and end apart: 13, of which 5 were waited for; matrix products, arithmetic and copies ran while one was open for 0% of the time, Pallas kernels for 11%

profile of v8, /device:TPU:1, one launch (start us, length us, event | category | flops | bytes accessed | tf_op | source)
XLA Modules:
  0.0 59.3 jit_solution(9248831748911355312)
XLA Ops:
  0.6 1.4 %shard_map.95 = (f32[2,24,128]{2,1,0:T(8,128)S(1)}, f32[2,24,128]{2,1,0:T(8,128)S(1)}, f32[24,128]{1,0:T(8,128)S(1)}, bf16[1024,512]{1,0:T(8,128)(2,1)S(1)}, f32...) custom-call(s32[1,4]{1,0:T(1,128)} %count_ref.1, f32[18,1024]{1,0:T(8,128)} %field_ref.1, ...), custom_call_target="tpu_custom_call" | custom-call | tf_op jit(solution)/shard_map/pallas_call | solution.py:251
  2.1 2.1 %collective-permute-start = (f32[2,24,128]{2,1,0:T(8,128)S(1)}, f32[2,24,128]{2,1,0:T(8,128)S(1)}, u32[]{:S(2)}, u32[]{:S(2)}) collective-permute-start(f32[2,24,128]{2,1,0:T(8,128)S(1)} %get-tuple-element.46), channel_id=1, source_target_pairs={{0,2},{1,3},{2,0},{3,1},{4,6},{5,7},{6,4},{7,5},{8,10},{9,11},{10,... | collective-permute-start | bytes 73736 | tf_op jit(solution)/shard_map/ppermute | solution.py:274
  4.2 1.0 %collective-permute-start.1 = (f32[2,24,128]{2,1,0:T(8,128)S(1)}, f32[2,24,128]{2,1,0:T(8,128)S(1)}, u32[]{:S(2)}, u32[]{:S(2)}) collective-permute-start(f32[2,24,128]{2,1,0:T(8,128)S(1)} %get-tuple-element.47), channel_id=1, source_target_pairs={{0,1},{1,0},{2,4},{3,5},{4,2},{5,3},{6,8},{7,9},{8,6},{9,7},{10,12... | collective-permute-start | bytes 73736 | tf_op jit(solution)/shard_map/ppermute | solution.py:274
  5.1 3.2 %shard_map.96 = (bf16[512,2048]{1,0:T(8,128)(2,1)S(1)}, f32[24,2048]{1,0:T(8,128)S(1)}, f32[4,72,72,128]{3,2,1,0:T(8,128)S(1)}) custom-call(s32[4,512]{1,0:T(4,128)S(1)} %get-tuple-element.48.map_ref, f32[24,1024]{1,0:T(8,128)S(1)} %get-tuple-element.49.field_ref, bf16[72,72,512]{2,1,0:T(8,128)(2,1)} %matrix_ref.1), custom_call_target="tpu_custom_call" | custom-call | tf_op jit(solution)/shard_map/pallas_call | solution.py:251
  8.5 1.2 %collective-permute-done.2.mid_ref = f32[2,24,128]{2,1,0:T(8,128)S(1)} collective-permute-done((f32[2,24,128]{2,1,0:T(8,128)S(1)}, f32[2,24,128]{2,1,0:T(8,128)S(1)}, u32[]{:S(2)}, u32[]{:S(2)}) %collective-permute-start.2) | collective-permute-done | bytes 24608 | tf_op jit(solution)/shard_map/ppermute | solution.py:282
  9.7 1.8 %shard_map.97 = (f32[2,24,128]{2,1,0:T(8,128)S(1)}, f32[2,24,128]{2,1,0:T(8,128)S(1)}, f32[24,128]{1,0:T(8,128)S(1)}, f32[24,2048]{1,0:T(8,128)S(1)}, f32[24,2048]{1,0:T(8,128)S(1)}) custom-call(f32[2,24,128]{2,1,0:T(8,128)S(1)} %collective-permute-done.near_ref, f32[2,24,128]{2,1,0:T(8,128)S(1)} %collective-permute-done.1.far_ref, ...), custom_call_target="tpu_custom_call" | custom-call | tf_op jit(solution)/shard_map/pallas_call | solution.py:251
  11.5 2.1 %collective-permute-start.3 = (f32[2,24,128]{2,1,0:T(8,128)S(1)}, f32[2,24,128]{2,1,0:T(8,128)S(1)}, u32[]{:S(2)}, u32[]{:S(2)}) collective-permute-start(f32[2,24,128]{2,1,0:T(8,128)S(1)} %get-tuple-element.59), channel_id=1, source_target_pairs={{0,2},{1,3},{2,0},{3,1},{4,6},{5,7},{6,4},{7,5},{8,10},{9,11},{10,... | collective-permute-start | bytes 73736 | tf_op jit(solution)/shard_map/ppermute | solution.py:274
  13.7 0.6 %collective-permute-start.4 = (f32[2,24,128]{2,1,0:T(8,128)S(1)}, f32[2,24,128]{2,1,0:T(8,128)S(1)}, u32[]{:S(2)}, u32[]{:S(2)}) collective-permute-start(f32[2,24,128]{2,1,0:T(8,128)S(1)} %get-tuple-element.60), channel_id=1, source_target_pairs={{0,1},{1,0},{2,4},{3,5},{4,2},{5,3},{6,8},{7,9},{8,6},{9,7},{10,12... | collective-permute-start | bytes 73736 | tf_op jit(solution)/shard_map/ppermute | solution.py:274
  14.3 1.4 %shard_map.98 = (f32[1,128]{1,0:T(1,128)S(1)}, f32[24,1024]{1,0:T(8,128)S(1)}) custom-call(f32[24,2048]{1,0:T(8,128)S(1)} %get-tuple-element.61.spread_ref, s32[4,512]{1,0:T(4,128)S(1)} %get-tuple-element.48.map_ref, f32[24,1024]{1,0:T(8,128)S(1)} %get-tuple-element.49.field_ref, f32[1,1024]{1,0:T(1,128)S(1)} %get-tuple-element.62.diagonal_ref, ...), custom_call_target="tpu_custom_call" | custom-call | tf_op jit(solution)/shard_map/pallas_call | solution.py:251
  16.2 0.8 %collective-permute-done.5.mid_ref = f32[2,24,128]{2,1,0:T(8,128)S(1)} collective-permute-done((f32[2,24,128]{2,1,0:T(8,128)S(1)}, f32[2,24,128]{2,1,0:T(8,128)S(1)}, u32[]{:S(2)}, u32[]{:S(2)}) %collective-permute-start.5) | collective-permute-done | bytes 24608 | tf_op jit(solution)/shard_map/ppermute | solution.py:282
  17.7 3.3 %collective-permute-start.6 = (f32[2,24,128]{2,1,0:T(8,128)S(1)}, f32[2,24,128]{2,1,0:T(8,128)S(1)}, u32[]{:S(2)}, u32[]{:S(2)}) collective-permute-start(f32[2,24,128]{2,1,0:T(8,128)S(1)} %get-tuple-element.71), channel_id=1, source_target_pairs={{0,2},{1,3},{2,0},{3,1},{4,6},{5,7},{6,4},{7,5},{8,10},{9,11},{10,... | collective-permute-start | bytes 73736 | tf_op jit(solution)/shard_map/ppermute | solution.py:274
  21.0 0.6 %collective-permute-start.7 = (f32[2,24,128]{2,1,0:T(8,128)S(1)}, f32[2,24,128]{2,1,0:T(8,128)S(1)}, u32[]{:S(2)}, u32[]{:S(2)}) collective-permute-start(f32[2,24,128]{2,1,0:T(8,128)S(1)} %get-tuple-element.72), channel_id=1, source_target_pairs={{0,1},{1,0},{2,4},{3,5},{4,2},{5,3},{6,8},{7,9},{8,6},{9,7},{10,12... | collective-permute-start | bytes 73736 | tf_op jit(solution)/shard_map/ppermute | solution.py:274
  21.6 0.9 %shard_map.100 = (f32[24,2048]{1,0:T(8,128)S(1)}, f32[1,128]{1,0:T(1,128)S(1)}) custom-call(f32[24,1024]{1,0:T(8,128)S(1)} %get-tuple-element.73.image_ref.field_ref, s32[4,512]{1,0:T(4,128)S(1)} %get-tuple-element.48.map_ref, f32[1,1024]{1,0:T(1,128)S(1)} %get-tuple-element.62.diagonal_ref), custom_call_target="tpu_custom_call" | custom-call | tf_op jit(solution)/shard_map/pallas_call | solution.py:251
  22.5 1.0 %collective-permute-start.8 = (f32[2,24,128]{2,1,0:T(8,128)S(1)}, f32[2,24,128]{2,1,0:T(8,128)S(1)}, u32[]{:S(2)}, u32[]{:S(2)}) collective-permute-start(f32[2,24,128]{2,1,0:T(8,128)S(1)} %pad_maximum_fusion.2), channel_id=1, source_target_pairs={{0,1},{1,0},{2,3},{3,2},{4,5},{5,4},{6,7},{7,6},{8,9},{9,8},{10,11... | collective-permute-start | bytes 73736 | tf_op jit(solution)/shard_map/ppermute | solution.py:282
  23.5 0.8 %collective-permute-done.8.mid_ref = f32[2,24,128]{2,1,0:T(8,128)S(1)} collective-permute-done((f32[2,24,128]{2,1,0:T(8,128)S(1)}, f32[2,24,128]{2,1,0:T(8,128)S(1)}, u32[]{:S(2)}, u32[]{:S(2)}) %collective-permute-start.8) | collective-permute-done | bytes 24608 | tf_op jit(solution)/shard_map/ppermute | solution.py:282
  24.3 1.9 %shard_map.101 = (f32[128,1,128]{2,1,0:T(1,128)}, f32[2,24,128]{2,1,0:T(8,128)S(1)}, f32[2,24,128]{2,1,0:T(8,128)S(1)}, f32[24,128]{1,0:T(8,128)S(1)}, f32[24,2048]{1,0:T(8,128)S(1)}) custom-call(f32[2,24,128]{2,1,0:T(8,128)S(1)} %collective-permute-done.6.near_ref, f32[2,24,128]{2,1,0:T(8,128)S(1)} %collective-permute-done.7.far_ref, ...), custom_call_target="tpu_custom_call" | custom-call | tf_op jit(solution)/shard_map/pallas_call | solution.py:251
  26.3 4.0 %collective-permute-start.9 = (f32[2,24,128]{2,1,0:T(8,128)S(1)}, f32[2,24,128]{2,1,0:T(8,128)S(1)}, u32[]{:S(2)}, u32[]{:S(2)}) collective-permute-start(f32[2,24,128]{2,1,0:T(8,128)S(1)} %get-tuple-element.82), channel_id=1, source_target_pairs={{0,2},{1,3},{2,0},{3,1},{4,6},{5,7},{6,4},{7,5},{8,10},{9,11},{10,... | collective-permute-start | bytes 73736 | tf_op jit(solution)/shard_map/ppermute | solution.py:274
  30.3 0.6 %collective-permute-start.10 = (f32[2,24,128]{2,1,0:T(8,128)S(1)}, f32[2,24,128]{2,1,0:T(8,128)S(1)}, u32[]{:S(2)}, u32[]{:S(2)}) collective-permute-start(f32[2,24,128]{2,1,0:T(8,128)S(1)} %get-tuple-element.83), channel_id=1, source_target_pairs={{0,1},{1,0},{2,4},{3,5},{4,2},{5,3},{6,8},{7,9},{8,6},{9,7},{10,12... | collective-permute-start | bytes 73736 | tf_op jit(solution)/shard_map/ppermute | solution.py:274
  30.9 17.7 %all-to-all-start = ((f32[128,1,128]{2,1,0:T(1,128)}), f32[128,1,128]{2,1,0:T(1,128)S(1)}, u32[]{:S(2)}, u32[]{:S(2)}) async-start(f32[128,1,128]{2,1,0:T(1,128)} %get-tuple-element.89), calls=%async_computation | async-start | bytes 131072 | tf_op jit(solution)/shard_map/all_to_all | solution.py:335
  48.6 1.4 %shard_map.102.own_ref = f32[24,1024]{1,0:T(8,128)S(1)} custom-call(f32[24,2048]{1,0:T(8,128)S(1)} %get-tuple-element.84.spread_ref, s32[4,512]{1,0:T(4,128)S(1)} %get-tuple-element.48.map_ref, f32[24,1024]{1,0:T(8,128)S(1)} %get-tuple-element.73.image_ref.field_ref, f32[1,1024]{1,0:T(1,128)S(1)} %get-tuple-element.62.diagonal_ref), custom_call_target="tpu_custom_call" | custom-call | tf_op jit(solution)/shard_map/pallas_call | solution.py:251
  50.1 1.1 %collective-permute-start.11 = (f32[2,24,128]{2,1,0:T(8,128)S(1)}, f32[2,24,128]{2,1,0:T(8,128)S(1)}, u32[]{:S(2)}, u32[]{:S(2)}) collective-permute-start(f32[2,24,128]{2,1,0:T(8,128)S(1)} %pad_maximum_fusion.3), channel_id=1, source_target_pairs={{0,1},{1,0},{2,3},{3,2},{4,5},{5,4},{6,7},{7,6},{8,9},{9,8},{10,11... | collective-permute-start | bytes 73736 | tf_op jit(solution)/shard_map/ppermute | solution.py:282
  51.2 0.8 %collective-permute-done.11.mid_ref = f32[2,24,128]{2,1,0:T(8,128)S(1)} collective-permute-done((f32[2,24,128]{2,1,0:T(8,128)S(1)}, f32[2,24,128]{2,1,0:T(8,128)S(1)}, u32[]{:S(2)}, u32[]{:S(2)}) %collective-permute-start.11) | collective-permute-done | bytes 24608 | tf_op jit(solution)/shard_map/ppermute | solution.py:282
  52.1 6.1 %all-to-all-done.sums_ref = f32[128,1,128]{2,1,0:T(1,128)S(1)} async-done(((f32[128,1,128]{2,1,0:T(1,128)}), f32[128,1,128]{2,1,0:T(1,128)S(1)}, u32[]{:S(2)}, u32[]{:S(2)}) %all-to-all-start) | async-done | bytes 65568 | tf_op jit(solution)/shard_map/all_to_all | solution.py:335
  58.2 1.1 %shard_map.103 = (f32[18,1024]{1,0:T(8,128)}, f32[18,1024]{1,0:T(8,128)}) custom-call(f32[24,1024]{1,0:T(8,128)S(1)} %shard_map.102.own_ref, f32[2,24,128]{2,1,0:T(8,128)S(1)} %collective-permute-done.9.near_ref, f32[2,24,128]{2,1,0:T(8,128)S(1)} %collective-permute-done.10.far_ref, f32[2,24,128]{2,1,0:T(8,128)S(1)} %collective-permute-done.11.mid_ref, ...), custom_call_target="tpu_custom_call" | custom-call | tf_op jit(solution)/shard_map/pallas_call | solution.py:251
  (19 shorter events, 1.3 us)
Async XLA Ops:
  2.1 6.3 %collective-permute-start = (f32[2,24,128]{2,1,0:T(8,128)S(1)}, f32[2,24,128]{2,1,0:T(8,128)S(1)}, u32[]{:S(2)}, u32[]{:S(2)}) collective-permute-start(f32[2,24,128]{2,1,0:T(8,128)S(1)} %get-tuple-element.46), channel_id=1, source_target_pairs={{0,2},{1,3},{2,0},{3,1},{4,6},{5,7},{6,4},{7,5},{8,10},{9,11},{10,... | collective-permute-start | bytes 73736 | tf_op jit(solution)/shard_map/ppermute | solution.py:274
  4.2 4.2 %collective-permute-start.1 = (f32[2,24,128]{2,1,0:T(8,128)S(1)}, f32[2,24,128]{2,1,0:T(8,128)S(1)}, u32[]{:S(2)}, u32[]{:S(2)}) collective-permute-start(f32[2,24,128]{2,1,0:T(8,128)S(1)} %get-tuple-element.47), channel_id=1, source_target_pairs={{0,1},{1,0},{2,4},{3,5},{4,2},{5,3},{6,8},{7,9},{8,6},{9,7},{10,12... | collective-permute-start | bytes 73736 | tf_op jit(solution)/shard_map/ppermute | solution.py:274
  8.4 1.3 %collective-permute-start.2 = (f32[2,24,128]{2,1,0:T(8,128)S(1)}, f32[2,24,128]{2,1,0:T(8,128)S(1)}, u32[]{:S(2)}, u32[]{:S(2)}) collective-permute-start(f32[2,24,128]{2,1,0:T(8,128)S(1)} %pad_maximum_fusion), channel_id=1, source_target_pairs={{0,1},{1,0},{2,3},{3,2},{4,5},{5,4},{6,7},{7,6},{8,9},{9,8},{10,11... | collective-permute-start | bytes 73736 | tf_op jit(solution)/shard_map/ppermute | solution.py:282
  11.5 4.1 %collective-permute-start.3 = (f32[2,24,128]{2,1,0:T(8,128)S(1)}, f32[2,24,128]{2,1,0:T(8,128)S(1)}, u32[]{:S(2)}, u32[]{:S(2)}) collective-permute-start(f32[2,24,128]{2,1,0:T(8,128)S(1)} %get-tuple-element.59), channel_id=1, source_target_pairs={{0,2},{1,3},{2,0},{3,1},{4,6},{5,7},{6,4},{7,5},{8,10},{9,11},{10,... | collective-permute-start | bytes 73736 | tf_op jit(solution)/shard_map/ppermute | solution.py:274
  13.7 2.0 %collective-permute-start.4 = (f32[2,24,128]{2,1,0:T(8,128)S(1)}, f32[2,24,128]{2,1,0:T(8,128)S(1)}, u32[]{:S(2)}, u32[]{:S(2)}) collective-permute-start(f32[2,24,128]{2,1,0:T(8,128)S(1)} %get-tuple-element.60), channel_id=1, source_target_pairs={{0,1},{1,0},{2,4},{3,5},{4,2},{5,3},{6,8},{7,9},{8,6},{9,7},{10,12... | collective-permute-start | bytes 73736 | tf_op jit(solution)/shard_map/ppermute | solution.py:274
  15.7 1.3 %collective-permute-start.5 = (f32[2,24,128]{2,1,0:T(8,128)S(1)}, f32[2,24,128]{2,1,0:T(8,128)S(1)}, u32[]{:S(2)}, u32[]{:S(2)}) collective-permute-start(f32[2,24,128]{2,1,0:T(8,128)S(1)} %pad_maximum_fusion.1), channel_id=1, source_target_pairs={{0,1},{1,0},{2,3},{3,2},{4,5},{5,4},{6,7},{7,6},{8,9},{9,8},{10,11... | collective-permute-start | bytes 73736 | tf_op jit(solution)/shard_map/ppermute | solution.py:282
  17.7 4.8 %collective-permute-start.6 = (f32[2,24,128]{2,1,0:T(8,128)S(1)}, f32[2,24,128]{2,1,0:T(8,128)S(1)}, u32[]{:S(2)}, u32[]{:S(2)}) collective-permute-start(f32[2,24,128]{2,1,0:T(8,128)S(1)} %get-tuple-element.71), channel_id=1, source_target_pairs={{0,2},{1,3},{2,0},{3,1},{4,6},{5,7},{6,4},{7,5},{8,10},{9,11},{10,... | collective-permute-start | bytes 73736 | tf_op jit(solution)/shard_map/ppermute | solution.py:274
  21.0 1.5 %collective-permute-start.7 = (f32[2,24,128]{2,1,0:T(8,128)S(1)}, f32[2,24,128]{2,1,0:T(8,128)S(1)}, u32[]{:S(2)}, u32[]{:S(2)}) collective-permute-start(f32[2,24,128]{2,1,0:T(8,128)S(1)} %get-tuple-element.72), channel_id=1, source_target_pairs={{0,1},{1,0},{2,4},{3,5},{4,2},{5,3},{6,8},{7,9},{8,6},{9,7},{10,12... | collective-permute-start | bytes 73736 | tf_op jit(solution)/shard_map/ppermute | solution.py:274
  22.5 1.8 %collective-permute-start.8 = (f32[2,24,128]{2,1,0:T(8,128)S(1)}, f32[2,24,128]{2,1,0:T(8,128)S(1)}, u32[]{:S(2)}, u32[]{:S(2)}) collective-permute-start(f32[2,24,128]{2,1,0:T(8,128)S(1)} %pad_maximum_fusion.2), channel_id=1, source_target_pairs={{0,1},{1,0},{2,3},{3,2},{4,5},{5,4},{6,7},{7,6},{8,9},{9,8},{10,11... | collective-permute-start | bytes 73736 | tf_op jit(solution)/shard_map/ppermute | solution.py:282
  26.3 23.7 %collective-permute-start.9 = (f32[2,24,128]{2,1,0:T(8,128)S(1)}, f32[2,24,128]{2,1,0:T(8,128)S(1)}, u32[]{:S(2)}, u32[]{:S(2)}) collective-permute-start(f32[2,24,128]{2,1,0:T(8,128)S(1)} %get-tuple-element.82), channel_id=1, source_target_pairs={{0,2},{1,3},{2,0},{3,1},{4,6},{5,7},{6,4},{7,5},{8,10},{9,11},{10,... | collective-permute-start | bytes 73736 | tf_op jit(solution)/shard_map/ppermute | solution.py:274
  30.3 19.7 %collective-permute-start.10 = (f32[2,24,128]{2,1,0:T(8,128)S(1)}, f32[2,24,128]{2,1,0:T(8,128)S(1)}, u32[]{:S(2)}, u32[]{:S(2)}) collective-permute-start(f32[2,24,128]{2,1,0:T(8,128)S(1)} %get-tuple-element.83), channel_id=1, source_target_pairs={{0,1},{1,0},{2,4},{3,5},{4,2},{5,3},{6,8},{7,9},{8,6},{9,7},{10,12... | collective-permute-start | bytes 73736 | tf_op jit(solution)/shard_map/ppermute | solution.py:274
  30.9 27.3 %all-to-all-start = ((f32[128,1,128]{2,1,0:T(1,128)}), f32[128,1,128]{2,1,0:T(1,128)S(1)}, u32[]{:S(2)}, u32[]{:S(2)}) async-start(f32[128,1,128]{2,1,0:T(1,128)} %get-tuple-element.89), calls=%async_computation | async-start | bytes 131072 | tf_op jit(solution)/shard_map/all_to_all | solution.py:335
  50.1 2.0 %collective-permute-start.11 = (f32[2,24,128]{2,1,0:T(8,128)S(1)}, f32[2,24,128]{2,1,0:T(8,128)S(1)}, u32[]{:S(2)}, u32[]{:S(2)}) collective-permute-start(f32[2,24,128]{2,1,0:T(8,128)S(1)} %pad_maximum_fusion.3), channel_id=1, source_target_pairs={{0,1},{1,0},{2,3},{3,2},{4,5},{5,4},{6,7},{7,6},{8,9},{9,8},{10,11... | collective-permute-start | bytes 73736 | tf_op jit(solution)/shard_map/ppermute | solution.py:282

commit v9 on v8

--- a/solution.py
+++ b/solution.py
@@ -59,16 +59,16 @@
 def write_blocks(blocks, near_ref, far_ref, mid_ref):
     core, odd = place()
     ahead, next_up, next_down, behind = (blocks[k] for k in (3, 2, 1, 0))
-    near_ref[0] = jnp.where(odd == 1, behind, ahead)
-    near_ref[1] = jnp.where(odd == 1, next_down, next_up)
-    far_ref[0] = jnp.where(odd == 1, ahead, behind)
-    far_ref[1] = jnp.where(odd == 1, next_up, next_down)
+    near_ref[:TR] = jnp.where(odd == 1, behind, ahead)[:TR]
+    near_ref[TR : 2 * TR] = jnp.where(odd == 1, next_down, next_up)[:TR]
+    far_ref[:TR] = jnp.where(odd == 1, ahead, behind)[:TR]
+    far_ref[TR : 2 * TR] = jnp.where(odd == 1, next_up, next_down)[:TR]
     mid_ref[...] = jnp.where(core == 1, next_down, next_up)
 
 
 def read_blocks(near_ref, far_ref, mid_ref):
     core, odd = place()
-    near, far, first, second = near_ref[0], far_ref[0], mid_ref[0], mid_ref[1]
+    near, far, first, second = near_ref[:TR], far_ref[:TR], mid_ref[0, :TR], mid_ref[1, :TR]
     return [
         jnp.where(odd == 1, far, near),
         jnp.where(core == 1, second, first),
@@ -148,8 +148,9 @@
 def product_kernel(near_ref, far_ref, mid_ref, sel_ref, matrix_ref, local_ref, *refs):
     last = len(refs) > 7
     near_out, far_out, mid_out, spread_ref, pick_ref, ghost_ref, prod_ref = refs[3:10] if last else refs
+    ghost_ref[TR:, :] = jnp.zeros((TP - TR, SHARED), F32)
     for k, block in enumerate(read_blocks(near_ref, far_ref, mid_ref)):
-        ghost_ref[:, k * GH : (k + 1) * GH] = block
+        ghost_ref[:TR, k * GH : (k + 1) * GH] = block
     pick_ref[...] = local_ref[...] + pick(ghost_ref[...], sel_ref[...])
     for t in range(E // 128):
         acc = jnp.zeros((DOFS, 128), F32)
@@ -195,8 +196,9 @@
 
 
 def combine_kernel(own_ref, near_ref, far_ref, mid_ref, share_ref, image_ref, near_out, far_out, mid_out, back_ref):
+    back_ref[TR:, :] = jnp.zeros((TP - TR, SHARED), F32)
     for k, block in enumerate(read_blocks(near_ref, far_ref, mid_ref)[::-1]):
-        back_ref[:, k * GH : (k + 1) * GH] = block
+        back_ref[:TR, k * GH : (k + 1) * GH] = block
     image = own_ref[...] + spread_out(back_ref[...], share_ref[...])
     image_ref[...] = image
     write_blocks(split(pick(image, share_ref[...])), near_out, far_out, mid_out)
@@ -214,8 +216,9 @@
 def final_kernel(
     own_ref, near_ref, far_ref, mid_ref, share_ref, field_ref, image_ref, sums_ref, solution_ref, residual_ref, back_ref
 ):
+    back_ref[TR:, :] = jnp.zeros((TP - TR, SHARED), F32)
     for k, block in enumerate(read_blocks(near_ref, far_ref, mid_ref)[::-1]):
-        back_ref[:, k * GH : (k + 1) * GH] = block
+        back_ref[:TR, k * GH : (k + 1) * GH] = block
     second = own_ref[...] + spread_out(back_ref[...], share_ref[...])
     field, image = field_ref[:TR], image_ref[:TR]
     row = sums_ref[...]
@@ -234,7 +237,7 @@
     residual_ref[...] = field - along * image + (step0 * step1) * second[:TR]
 
 
-MESSAGE = (VMEM((2, TP, GH), F32), VMEM((2, TP, GH), F32), VMEM((TP, GH), F32))
+MESSAGE = (VMEM((2 * TR, GH), F32), VMEM((2 * TR, GH), F32), VMEM((TP, GH), F32))
 WIDE = VMEM((TP, PICKS), F32)
 FACES = VMEM((TP, F), F32)
 GHOSTS = VMEM((TP, SHARED), F32)
@@ -277,7 +280,7 @@
         got_far = swap(far, lambda c: ((c + 1) ^ 1) - 1)
         got_near = swap(near, lambda c: c ^ 1)
         got_near, got_far, beside = lax.optimization_barrier((got_near, got_far, beside()))
-        onward = jnp.where(core == odd, got_near[1], got_far[1])
+        onward = jnp.pad(jnp.where(core == odd, got_near, got_far)[TR:], ((0, TP - TR), (0, 0)))
         pair = jnp.stack([mid, onward])
         got_mid = lax.ppermute(pair, DOM, [(i, i ^ 1) for i in range(count)])
         return (got_near, got_far, got_mid), beside

time: 59.5 us -> 59.4 us (level)
  no operation moved by 1% of the time
where the time goes in v9:
time: 59.4 us; the launch traced here: 59.2 us
  starting transfers between devices  34.7 us (58%)
  Pallas kernels  13.7 us (23%)
  waiting for transfers between devices  9.89 us (17%)
  between operations  0.87 us (1%)
    all_to_all x1, starting transfers between devices, shards(): row = lax.all_to_all(row, DOM, 0, 0)  17.7 us
    ppermute x8, starting transfers between devices, swap(): return lax.ppermute(value, DOM, pairs)  14.4 us
    pallas_call x9, Pallas kernels, call(): pl.pallas_call(kernel, in_specs=[pl.BlockSpec(memory_space=m) for m in sp...  13.7 us
    all_to_all x1, waiting for transfers between devices, shards(): row = lax.all_to_all(row, DOM, 0, 0)  6.14 us
    ppermute x4, waiting for transfers between devices, exchange(): got_mid = lax.ppermute(pair, DOM, [(i, i ^ 1) for i in range(count)])  3.73 us
    ppermute x4, starting transfers between devices, exchange(): got_mid = lax.ppermute(pair, DOM, [(i, i ^ 1) for i in range(count)])  2.64 us
  transfers between devices with their start and end apart: 13, of which 5 were waited for; matrix products, arithmetic and copies ran while one was open for 0% of the time, Pallas kernels for 11%

profile of v9, /device:TPU:1, one launch (start us, length us, event | category | flops | bytes accessed | tf_op | source)
XLA Modules:
  0.0 59.2 jit_solution(13974424358031930657)
XLA Ops:
  0.6 1.4 %shard_map.95 = (f32[36,128]{1,0:T(8,128)S(1)}, f32[36,128]{1,0:T(8,128)S(1)}, f32[24,128]{1,0:T(8,128)S(1)}, bf16[1024,512]{1,0:T(8,128)(2,1)S(1)}, f32[24,1024...) custom-call(s32[1,4]{1,0:T(1,128)} %count_ref.1, f32[18,1024]{1,0:T(8,128)} %field_ref.1, ...), custom_call_target="tpu_custom_call" | custom-call | tf_op jit(solution)/shard_map/pallas_call | solution.py:254
  2.1 2.1 %collective-permute-start = (f32[36,128]{1,0:T(8,128)S(1)}, f32[36,128]{1,0:T(8,128)S(1)}, u32[]{:S(2)}, u32[]{:S(2)}) collective-permute-start(f32[36,128]{1,0:T(8,128)S(1)} %get-tuple-element.46), channel_id=1, source_target_pairs={{0,2},{1,3},{2,0},{3,1},{4,6},{5,7},{6,4},{7,5},{8,10},{9,11},{10,... | collective-permute-start | bytes 55304 | tf_op jit(solution)/shard_map/ppermute | solution.py:277
  4.2 1.0 %collective-permute-start.1 = (f32[36,128]{1,0:T(8,128)S(1)}, f32[36,128]{1,0:T(8,128)S(1)}, u32[]{:S(2)}, u32[]{:S(2)}) collective-permute-start(f32[36,128]{1,0:T(8,128)S(1)} %get-tuple-element.47), channel_id=1, source_target_pairs={{0,1},{1,0},{2,4},{3,5},{4,2},{5,3},{6,8},{7,9},{8,6},{9,7},{10,12... | collective-permute-start | bytes 55304 | tf_op jit(solution)/shard_map/ppermute | solution.py:277
  5.1 3.2 %shard_map.96 = (bf16[512,2048]{1,0:T(8,128)(2,1)S(1)}, f32[24,2048]{1,0:T(8,128)S(1)}, f32[4,72,72,128]{3,2,1,0:T(8,128)S(1)}) custom-call(s32[4,512]{1,0:T(4,128)S(1)} %get-tuple-element.48.map_ref, f32[24,1024]{1,0:T(8,128)S(1)} %get-tuple-element.49.field_ref, bf16[72,72,512]{2,1,0:T(8,128)(2,1)} %matrix_ref.1), custom_call_target="tpu_custom_call" | custom-call | tf_op jit(solution)/shard_map/pallas_call | solution.py:254
  8.5 1.2 %collective-permute-done.2.mid_ref = f32[2,24,128]{2,1,0:T(8,128)S(1)} collective-permute-done((f32[2,24,128]{2,1,0:T(8,128)S(1)}, f32[2,24,128]{2,1,0:T(8,128)S(1)}, u32[]{:S(2)}, u32[]{:S(2)}) %collective-permute-start.2) | collective-permute-done | bytes 24608 | tf_op jit(solution)/shard_map/ppermute | solution.py:285
  9.7 1.9 %shard_map.97 = (f32[36,128]{1,0:T(8,128)S(1)}, f32[36,128]{1,0:T(8,128)S(1)}, f32[24,128]{1,0:T(8,128)S(1)}, f32[24,2048]{1,0:T(8,128)S(1)}, f32[24,2048]{1,0:T(8,128)S(1)}) custom-call(f32[36,128]{1,0:T(8,128)S(1)} %collective-permute-done.near_ref, f32[36,128]{1,0:T(8,128)S(1)} %collective-permute-done.1.far_ref, ...), custom_call_target="tpu_custom_call" | custom-call | tf_op jit(solution)/shard_map/pallas_call | solution.py:254
  11.6 2.1 %collective-permute-start.3 = (f32[36,128]{1,0:T(8,128)S(1)}, f32[36,128]{1,0:T(8,128)S(1)}, u32[]{:S(2)}, u32[]{:S(2)}) collective-permute-start(f32[36,128]{1,0:T(8,128)S(1)} %get-tuple-element.59), channel_id=1, source_target_pairs={{0,2},{1,3},{2,0},{3,1},{4,6},{5,7},{6,4},{7,5},{8,10},{9,11},{10,... | collective-permute-start | bytes 55304 | tf_op jit(solution)/shard_map/ppermute | solution.py:277
  13.7 0.6 %collective-permute-start.4 = (f32[36,128]{1,0:T(8,128)S(1)}, f32[36,128]{1,0:T(8,128)S(1)}, u32[]{:S(2)}, u32[]{:S(2)}) collective-permute-start(f32[36,128]{1,0:T(8,128)S(1)} %get-tuple-element.60), channel_id=1, source_target_pairs={{0,1},{1,0},{2,4},{3,5},{4,2},{5,3},{6,8},{7,9},{8,6},{9,7},{10,12... | collective-permute-start | bytes 55304 | tf_op jit(solution)/shard_map/ppermute | solution.py:277
  14.3 1.4 %shard_map.98 = (f32[1,128]{1,0:T(1,128)S(1)}, f32[24,1024]{1,0:T(8,128)S(1)}) custom-call(f32[24,2048]{1,0:T(8,128)S(1)} %get-tuple-element.61.spread_ref, s32[4,512]{1,0:T(4,128)S(1)} %get-tuple-element.48.map_ref, f32[24,1024]{1,0:T(8,128)S(1)} %get-tuple-element.49.field_ref, f32[1,1024]{1,0:T(1,128)S(1)} %get-tuple-element.62.diagonal_ref, ...), custom_call_target="tpu_custom_call" | custom-call | tf_op jit(solution)/shard_map/pallas_call | solution.py:254
  16.2 0.8 %collective-permute-done.5.mid_ref = f32[2,24,128]{2,1,0:T(8,128)S(1)} collective-permute-done((f32[2,24,128]{2,1,0:T(8,128)S(1)}, f32[2,24,128]{2,1,0:T(8,128)S(1)}, u32[]{:S(2)}, u32[]{:S(2)}) %collective-permute-start.5) | collective-permute-done | bytes 24608 | tf_op jit(solution)/shard_map/ppermute | solution.py:285
  17.7 3.3 %collective-permute-start.6 = (f32[36,128]{1,0:T(8,128)S(1)}, f32[36,128]{1,0:T(8,128)S(1)}, u32[]{:S(2)}, u32[]{:S(2)}) collective-permute-start(f32[36,128]{1,0:T(8,128)S(1)} %get-tuple-element.71), channel_id=1, source_target_pairs={{0,2},{1,3},{2,0},{3,1},{4,6},{5,7},{6,4},{7,5},{8,10},{9,11},{10,... | collective-permute-start | bytes 55304 | tf_op jit(solution)/shard_map/ppermute | solution.py:277
  20.9 0.6 %collective-permute-start.7 = (f32[36,128]{1,0:T(8,128)S(1)}, f32[36,128]{1,0:T(8,128)S(1)}, u32[]{:S(2)}, u32[]{:S(2)}) collective-permute-start(f32[36,128]{1,0:T(8,128)S(1)} %get-tuple-element.72), channel_id=1, source_target_pairs={{0,1},{1,0},{2,4},{3,5},{4,2},{5,3},{6,8},{7,9},{8,6},{9,7},{10,12... | collective-permute-start | bytes 55304 | tf_op jit(solution)/shard_map/ppermute | solution.py:277
  21.6 0.9 %shard_map.100 = (f32[24,2048]{1,0:T(8,128)S(1)}, f32[1,128]{1,0:T(1,128)S(1)}) custom-call(f32[24,1024]{1,0:T(8,128)S(1)} %get-tuple-element.73.image_ref.field_ref, s32[4,512]{1,0:T(4,128)S(1)} %get-tuple-element.48.map_ref, f32[1,1024]{1,0:T(1,128)S(1)} %get-tuple-element.62.diagonal_ref), custom_call_target="tpu_custom_call" | custom-call | tf_op jit(solution)/shard_map/pallas_call | solution.py:254
  22.5 0.9 %collective-permute-start.8 = (f32[2,24,128]{2,1,0:T(8,128)S(1)}, f32[2,24,128]{2,1,0:T(8,128)S(1)}, u32[]{:S(2)}, u32[]{:S(2)}) collective-permute-start(f32[2,24,128]{2,1,0:T(8,128)S(1)} %pad_maximum_fusion.2), channel_id=1, source_target_pairs={{0,1},{1,0},{2,3},{3,2},{4,5},{5,4},{6,7},{7,6},{8,9},{9,8},{10,11... | collective-permute-start | bytes 73736 | tf_op jit(solution)/shard_map/ppermute | solution.py:285
  23.4 0.8 %collective-permute-done.8.mid_ref = f32[2,24,128]{2,1,0:T(8,128)S(1)} collective-permute-done((f32[2,24,128]{2,1,0:T(8,128)S(1)}, f32[2,24,128]{2,1,0:T(8,128)S(1)}, u32[]{:S(2)}, u32[]{:S(2)}) %collective-permute-start.8) | collective-permute-done | bytes 24608 | tf_op jit(solution)/shard_map/ppermute | solution.py:285
  24.3 1.9 %shard_map.101 = (f32[128,1,128]{2,1,0:T(1,128)}, f32[36,128]{1,0:T(8,128)S(1)}, f32[36,128]{1,0:T(8,128)S(1)}, f32[24,128]{1,0:T(8,128)S(1)}, f32[24,2048]{1,0:T(8,128)S(1)}) custom-call(f32[36,128]{1,0:T(8,128)S(1)} %collective-permute-done.6.near_ref, f32[36,128]{1,0:T(8,128)S(1)} %collective-permute-done.7.far_ref, ...), custom_call_target="tpu_custom_call" | custom-call | tf_op jit(solution)/shard_map/pallas_call | solution.py:254
  26.2 4.0 %collective-permute-start.9 = (f32[36,128]{1,0:T(8,128)S(1)}, f32[36,128]{1,0:T(8,128)S(1)}, u32[]{:S(2)}, u32[]{:S(2)}) collective-permute-start(f32[36,128]{1,0:T(8,128)S(1)} %get-tuple-element.82), channel_id=1, source_target_pairs={{0,2},{1,3},{2,0},{3,1},{4,6},{5,7},{6,4},{7,5},{8,10},{9,11},{10,... | collective-permute-start | bytes 55304 | tf_op jit(solution)/shard_map/ppermute | solution.py:277
  30.3 0.6 %collective-permute-start.10 = (f32[36,128]{1,0:T(8,128)S(1)}, f32[36,128]{1,0:T(8,128)S(1)}, u32[]{:S(2)}, u32[]{:S(2)}) collective-permute-start(f32[36,128]{1,0:T(8,128)S(1)} %get-tuple-element.83), channel_id=1, source_target_pairs={{0,1},{1,0},{2,4},{3,5},{4,2},{5,3},{6,8},{7,9},{8,6},{9,7},{10,12... | collective-permute-start | bytes 55304 | tf_op jit(solution)/shard_map/ppermute | solution.py:277
  30.9 17.7 %all-to-all-start = ((f32[128,1,128]{2,1,0:T(1,128)}), f32[128,1,128]{2,1,0:T(1,128)S(1)}, u32[]{:S(2)}, u32[]{:S(2)}) async-start(f32[128,1,128]{2,1,0:T(1,128)} %get-tuple-element.89), calls=%async_computation | async-start | bytes 131072 | tf_op jit(solution)/shard_map/all_to_all | solution.py:338
  48.6 1.4 %shard_map.102.own_ref = f32[24,1024]{1,0:T(8,128)S(1)} custom-call(f32[24,2048]{1,0:T(8,128)S(1)} %get-tuple-element.84.spread_ref, s32[4,512]{1,0:T(4,128)S(1)} %get-tuple-element.48.map_ref, f32[24,1024]{1,0:T(8,128)S(1)} %get-tuple-element.73.image_ref.field_ref, f32[1,1024]{1,0:T(1,128)S(1)} %get-tuple-element.62.diagonal_ref), custom_call_target="tpu_custom_call" | custom-call | tf_op jit(solution)/shard_map/pallas_call | solution.py:254
  50.0 1.1 %collective-permute-start.11 = (f32[2,24,128]{2,1,0:T(8,128)S(1)}, f32[2,24,128]{2,1,0:T(8,128)S(1)}, u32[]{:S(2)}, u32[]{:S(2)}) collective-permute-start(f32[2,24,128]{2,1,0:T(8,128)S(1)} %pad_maximum_fusion.3), channel_id=1, source_target_pairs={{0,1},{1,0},{2,3},{3,2},{4,5},{5,4},{6,7},{7,6},{8,9},{9,8},{10,11... | collective-permute-start | bytes 73736 | tf_op jit(solution)/shard_map/ppermute | solution.py:285
  51.2 0.8 %collective-permute-done.11.mid_ref = f32[2,24,128]{2,1,0:T(8,128)S(1)} collective-permute-done((f32[2,24,128]{2,1,0:T(8,128)S(1)}, f32[2,24,128]{2,1,0:T(8,128)S(1)}, u32[]{:S(2)}, u32[]{:S(2)}) %collective-permute-start.11) | collective-permute-done | bytes 24608 | tf_op jit(solution)/shard_map/ppermute | solution.py:285
  52.0 6.1 %all-to-all-done.sums_ref = f32[128,1,128]{2,1,0:T(1,128)S(1)} async-done(((f32[128,1,128]{2,1,0:T(1,128)}), f32[128,1,128]{2,1,0:T(1,128)S(1)}, u32[]{:S(2)}, u32[]{:S(2)}) %all-to-all-start) | async-done | bytes 65568 | tf_op jit(solution)/shard_map/all_to_all | solution.py:338
  58.2 1.1 %shard_map.103 = (f32[18,1024]{1,0:T(8,128)}, f32[18,1024]{1,0:T(8,128)}) custom-call(f32[24,1024]{1,0:T(8,128)S(1)} %shard_map.102.own_ref, f32[36,128]{1,0:T(8,128)S(1)} %collective-permute-done.9.near_ref, f32[36,128]{1,0:T(8,128)S(1)} %collective-permute-done.10.far_ref, f32[2,24,128]{2,1,0:T(8,128)S(1)} %collective-permute-done.11.mid_ref, ...), custom_call_target="tpu_custom_call" | custom-call | tf_op jit(solution)/shard_map/pallas_call | solution.py:254
  (23 shorter events, 1.2 us)
Async XLA Ops:
  2.1 6.3 %collective-permute-start = (f32[36,128]{1,0:T(8,128)S(1)}, f32[36,128]{1,0:T(8,128)S(1)}, u32[]{:S(2)}, u32[]{:S(2)}) collective-permute-start(f32[36,128]{1,0:T(8,128)S(1)} %get-tuple-element.46), channel_id=1, source_target_pairs={{0,2},{1,3},{2,0},{3,1},{4,6},{5,7},{6,4},{7,5},{8,10},{9,11},{10,... | collective-permute-start | bytes 55304 | tf_op jit(solution)/shard_map/ppermute | solution.py:277
  4.2 4.2 %collective-permute-start.1 = (f32[36,128]{1,0:T(8,128)S(1)}, f32[36,128]{1,0:T(8,128)S(1)}, u32[]{:S(2)}, u32[]{:S(2)}) collective-permute-start(f32[36,128]{1,0:T(8,128)S(1)} %get-tuple-element.47), channel_id=1, source_target_pairs={{0,1},{1,0},{2,4},{3,5},{4,2},{5,3},{6,8},{7,9},{8,6},{9,7},{10,12... | collective-permute-start | bytes 55304 | tf_op jit(solution)/shard_map/ppermute | solution.py:277
  8.4 1.3 %collective-permute-start.2 = (f32[2,24,128]{2,1,0:T(8,128)S(1)}, f32[2,24,128]{2,1,0:T(8,128)S(1)}, u32[]{:S(2)}, u32[]{:S(2)}) collective-permute-start(f32[2,24,128]{2,1,0:T(8,128)S(1)} %pad_maximum_fusion), channel_id=1, source_target_pairs={{0,1},{1,0},{2,3},{3,2},{4,5},{5,4},{6,7},{7,6},{8,9},{9,8},{10,11... | collective-permute-start | bytes 73736 | tf_op jit(solution)/shard_map/ppermute | solution.py:285
  11.6 4.1 %collective-permute-start.3 = (f32[36,128]{1,0:T(8,128)S(1)}, f32[36,128]{1,0:T(8,128)S(1)}, u32[]{:S(2)}, u32[]{:S(2)}) collective-permute-start(f32[36,128]{1,0:T(8,128)S(1)} %get-tuple-element.59), channel_id=1, source_target_pairs={{0,2},{1,3},{2,0},{3,1},{4,6},{5,7},{6,4},{7,5},{8,10},{9,11},{10,... | collective-permute-start | bytes 55304 | tf_op jit(solution)/shard_map/ppermute | solution.py:277
  13.7 2.0 %collective-permute-start.4 = (f32[36,128]{1,0:T(8,128)S(1)}, f32[36,128]{1,0:T(8,128)S(1)}, u32[]{:S(2)}, u32[]{:S(2)}) collective-permute-start(f32[36,128]{1,0:T(8,128)S(1)} %get-tuple-element.60), channel_id=1, source_target_pairs={{0,1},{1,0},{2,4},{3,5},{4,2},{5,3},{6,8},{7,9},{8,6},{9,7},{10,12... | collective-permute-start | bytes 55304 | tf_op jit(solution)/shard_map/ppermute | solution.py:277
  15.7 1.3 %collective-permute-start.5 = (f32[2,24,128]{2,1,0:T(8,128)S(1)}, f32[2,24,128]{2,1,0:T(8,128)S(1)}, u32[]{:S(2)}, u32[]{:S(2)}) collective-permute-start(f32[2,24,128]{2,1,0:T(8,128)S(1)} %pad_maximum_fusion.1), channel_id=1, source_target_pairs={{0,1},{1,0},{2,3},{3,2},{4,5},{5,4},{6,7},{7,6},{8,9},{9,8},{10,11... | collective-permute-start | bytes 73736 | tf_op jit(solution)/shard_map/ppermute | solution.py:285
  17.7 4.8 %collective-permute-start.6 = (f32[36,128]{1,0:T(8,128)S(1)}, f32[36,128]{1,0:T(8,128)S(1)}, u32[]{:S(2)}, u32[]{:S(2)}) collective-permute-start(f32[36,128]{1,0:T(8,128)S(1)} %get-tuple-element.71), channel_id=1, source_target_pairs={{0,2},{1,3},{2,0},{3,1},{4,6},{5,7},{6,4},{7,5},{8,10},{9,11},{10,... | collective-permute-start | bytes 55304 | tf_op jit(solution)/shard_map/ppermute | solution.py:277
  20.9 1.5 %collective-permute-start.7 = (f32[36,128]{1,0:T(8,128)S(1)}, f32[36,128]{1,0:T(8,128)S(1)}, u32[]{:S(2)}, u32[]{:S(2)}) collective-permute-start(f32[36,128]{1,0:T(8,128)S(1)} %get-tuple-element.72), channel_id=1, source_target_pairs={{0,1},{1,0},{2,4},{3,5},{4,2},{5,3},{6,8},{7,9},{8,6},{9,7},{10,12... | collective-permute-start | bytes 55304 | tf_op jit(solution)/shard_map/ppermute | solution.py:277
  22.5 1.8 %collective-permute-start.8 = (f32[2,24,128]{2,1,0:T(8,128)S(1)}, f32[2,24,128]{2,1,0:T(8,128)S(1)}, u32[]{:S(2)}, u32[]{:S(2)}) collective-permute-start(f32[2,24,128]{2,1,0:T(8,128)S(1)} %pad_maximum_fusion.2), channel_id=1, source_target_pairs={{0,1},{1,0},{2,3},{3,2},{4,5},{5,4},{6,7},{7,6},{8,9},{9,8},{10,11... | collective-permute-start | bytes 73736 | tf_op jit(solution)/shard_map/ppermute | solution.py:285
  26.2 23.7 %collective-permute-start.9 = (f32[36,128]{1,0:T(8,128)S(1)}, f32[36,128]{1,0:T(8,128)S(1)}, u32[]{:S(2)}, u32[]{:S(2)}) collective-permute-start(f32[36,128]{1,0:T(8,128)S(1)} %get-tuple-element.82), channel_id=1, source_target_pairs={{0,2},{1,3},{2,0},{3,1},{4,6},{5,7},{6,4},{7,5},{8,10},{9,11},{10,... | collective-permute-start | bytes 55304 | tf_op jit(solution)/shard_map/ppermute | solution.py:277
  30.3 19.7 %collective-permute-start.10 = (f32[36,128]{1,0:T(8,128)S(1)}, f32[36,128]{1,0:T(8,128)S(1)}, u32[]{:S(2)}, u32[]{:S(2)}) collective-permute-start(f32[36,128]{1,0:T(8,128)S(1)} %get-tuple-element.83), channel_id=1, source_target_pairs={{0,1},{1,0},{2,4},{3,5},{4,2},{5,3},{6,8},{7,9},{8,6},{9,7},{10,12... | collective-permute-start | bytes 55304 | tf_op jit(solution)/shard_map/ppermute | solution.py:277
  30.9 27.3 %all-to-all-start = ((f32[128,1,128]{2,1,0:T(1,128)}), f32[128,1,128]{2,1,0:T(1,128)S(1)}, u32[]{:S(2)}, u32[]{:S(2)}) async-start(f32[128,1,128]{2,1,0:T(1,128)} %get-tuple-element.89), calls=%async_computation | async-start | bytes 131072 | tf_op jit(solution)/shard_map/all_to_all | solution.py:338
  50.0 2.0 %collective-permute-start.11 = (f32[2,24,128]{2,1,0:T(8,128)S(1)}, f32[2,24,128]{2,1,0:T(8,128)S(1)}, u32[]{:S(2)}, u32[]{:S(2)}) collective-permute-start(f32[2,24,128]{2,1,0:T(8,128)S(1)} %pad_maximum_fusion.3), channel_id=1, source_target_pairs={{0,1},{1,0},{2,3},{3,2},{4,5},{5,4},{6,7},{7,6},{8,9},{9,8},{10,11... | collective-permute-start | bytes 73736 | tf_op jit(solution)/shard_map/ppermute | solution.py:285
